TPU v7x, 8 devices: a whole 2x2x1 slice. The times are simulated.
8 devices in a mesh: tp: 2 (over z, y), ep: 4 (over x, core).
Axes of the slice: x: 2, y: 2, z: 1, core: 2. Of those that a mesh axis runs over, the one named last changes fastest.
Arguments:
- x: bfloat16 [1536, 1536], P(('ep', 'tp'))
- grad_y: bfloat16 [1536, 1536], P(('ep', 'tp'))
- w_router: bfloat16 [1536, 64], replicated
- w_gate: bfloat16 [64, 1536, 512], P('ep', None, 'tp')
- w_up: bfloat16 [64, 1536, 512], P('ep', None, 'tp')
- w_down: bfloat16 [64, 512, 1536], P('ep', 'tp')
- ws_gate: bfloat16 [1536, 1024], P(None, 'tp')
- ws_up: bfloat16 [1536, 1024], P(None, 'tp')
- ws_down: bfloat16 [1024, 1536], P('tp')
- topk_idx: int32 [1536, 6], P(('ep', 'tp'))
Outputs:
- output 1: bfloat16 [1536, 1536], P(('ep', 'tp'))
- output 2: bfloat16 [1536, 1536], P(('ep', 'tp'))
- output 3: float32 [1536, 64], replicated
- output 4: float32 [64, 1536, 512], P('ep', None, 'tp')
- output 5: float32 [64, 1536, 512], P('ep', None, 'tp')
- output 6: float32 [64, 512, 1536], P('ep', 'tp')
- output 7: float32 [1536, 1024], P(None, 'tp')
- output 8: float32 [1536, 1024], P(None, 'tp')
- output 9: float32 [1024, 1536], P('tp')
All inputs are finite; a program needn't handle non-finite values.
Results may differ from a plain program's by a relative error of at most 0.0131065.
Values are sent between devices in bfloat16 or wider.
A program may use at most 1 GiB of HBM per device.

v0:
```python
import functools

import jax
import jax.numpy as jnp
from jax import lax
from jax.experimental import pallas as pl
from jax.experimental.pallas import tpu as pltpu
from jax.sharding import PartitionSpec as P


GATE_SCALE = 16.0
BF16 = jnp.bfloat16
F32 = jnp.float32
FWD_CHUNKS = (2, 8, 6)
BWD_CHUNKS = 2
MESH = pl.DeviceIdType.MESH

NN = (((1,), (0,)), ((), ()))
NT = (((1,), (1,)), ((), ()))
TN = (((0,), (0,)), ((), ()))


def dot(a, b, dims=NN):
    return lax.dot_general(a, b, dims, preferred_element_type=F32)


def sigmoid(v):
    return 1.0 / (1.0 + jnp.exp(-jnp.maximum(v, -88.0)))


def swiglu_fwd(a, b):
    return (a * sigmoid(a) * b).astype(BF16)


def swiglu_bwd(a, b, dh):
    sig = sigmoid(a)
    silu = a * sig
    h = (silu * b).astype(BF16)
    da = (dh * b * (sig * (1.0 + a * (1.0 - sig)))).astype(BF16)
    db = (dh * silu).astype(BF16)
    return h, da, db


def rounded(v):
    return v.astype(BF16).astype(F32)


def half_rows(cap, ep_size):
    half = cap * ep_size
    return half, half + (-half) % 8


def store_parts(parity, part, send_ref, own_ref, half, padded):
    shift = padded - half

    @pl.when(parity == 0)
    def _():
        send_ref[0:half, :] = part[0:half]
        own_ref[0:half, :] = part[padded:padded + half]

    @pl.when(parity == 1)
    def _():
        send_ref[half:2 * half, :] = part[shift:padded]
        own_ref[half:2 * half, :] = part[padded + shift:2 * padded]


def pick_matrix(row_ref, rows):
    ids = row_ref[0]
    iota = lax.broadcasted_iota(jnp.int32, (rows, ids.shape[1]), 0)
    return iota == ids


def pick_rows(pick_ref, table_ref, out_ref, scale=None, step=512):
    @pl.loop(0, table_ref.shape[1] // step)
    def _(i):
        cols = pl.ds(pl.multiple_of(i * step, step), step)
        rows = dot(pick_ref[...], table_ref[:, cols])
        out_ref[:, cols] = (rows if scale is None else rows * scale).astype(out_ref.dtype)


def fwd_kernel(half, padded, x_ref, row_ref, w1_ref, w3_ref, w2_ref, send_ref, own_ref, pick_ref, rows_ref):
    pick_ref[...] = jnp.where(pick_matrix(row_ref, 2 * padded), 1.0, 0.0).astype(BF16)
    pick_rows(pick_ref, x_ref, rows_ref)
    rows = rows_ref[...]
    a = rounded(dot(rows, w1_ref[0]))
    b = rounded(dot(rows, w3_ref[0]))
    h = swiglu_fwd(a, b)
    part = dot(h, w2_ref[0])
    store_parts(pl.program_id(0) % 2, part, send_ref, own_ref, half, padded)


def windows(cap, ep_size):
    other, own = (ep_size - 1) * cap, cap
    return other, other + 7 + (-other - 7) % 8, own, own + 7 + (-own - 7) % 8


def bwd_kernel(sizes, per_chunk, x_ref, dy_ref, row_ref, gate_ref, w1_ref, w3_ref, w2_ref, *refs):
    other, win_other, own, win_own = sizes
    dw1_ref, dw3_ref, dw2_ref = refs[:3]
    outs, (far_ref, near_ref, sem, pick_ref, rows_ref, d_out_ref) = refs[3:-6], refs[-6:]
    chunks = far_ref.shape[0] // 2
    e = pl.program_id(0)
    total = 2 * (win_other + win_own)

    @pl.when(e == 0)
    def _():
        far_ref[...] = jnp.zeros_like(far_ref)
        near_ref[...] = jnp.zeros_like(near_ref)

    hit = pick_matrix(row_ref, total)
    pick_ref[...] = jnp.where(hit, 1.0, 0.0).astype(BF16)
    gates = jnp.sum(jnp.where(hit, gate_ref[0], 0.0), axis=1, keepdims=True)
    pick_rows(pick_ref, x_ref, rows_ref)
    pick_rows(pick_ref, dy_ref, d_out_ref, gates)
    rows, d_out = rows_ref[...], d_out_ref[...]
    a = rounded(dot(rows, w1_ref[0]))
    b = rounded(dot(rows, w3_ref[0]))
    dh = rounded(dot(d_out, w2_ref[0], NT))
    h, da, db = swiglu_bwd(a, b, dh)

    chunk = e // per_chunk
    far_base = pl.multiple_of((e % per_chunk) * other // 8 * 8, 8)
    near_base = pl.multiple_of(e * own // 8 * 8, 8)
    step = 512

    @pl.loop(0, rows_ref.shape[1] // step)
    def _(i):
        cols = pl.ds(pl.multiple_of(i * step, step), step)
        dw2_ref[0, :, cols] = dot(h, d_out_ref[:, cols], TN)
        dw1_ref[0, cols, :] = dot(rows_ref[:, cols], da, TN)
        dw3_ref[0, cols, :] = dot(rows_ref[:, cols], db, TN)
        part = dot(da, w1_ref[0, cols, :], NT) + dot(db, w3_ref[0, cols, :], NT)
        for side in range(2):
            far_ref[chunk * 2 + side, pl.ds(far_base, win_other), cols] += part[side * win_other:(side + 1) * win_other]
            first = 2 * win_other + side * win_own
            near_ref[side, pl.ds(near_base, win_own), cols] += part[first:first + win_own]

    def copies(c):
        out = []
        for side in range(2):
            k = 2 * c + side
            src = far_ref.at[k] if c < chunks else near_ref.at[side]
            out.append(pltpu.make_async_copy(src.at[pl.ds(0, outs[k].shape[0])], outs[k], sem.at[k]))
        return out

    for c in range(chunks):
        @pl.when(e == (c + 1) * per_chunk - 1)
        def _():
            for copy in copies(c):
                copy.start()

    @pl.when(e == chunks * per_chunk - 1)
    def _():
        for copy in copies(chunks):
            copy.start()
        for c in range(chunks + 1):
            for copy in copies(c):
                copy.wait()


def expert_fwd(start, count, half, padded, x_all, row_ids, w_gate, w_up, w_down):
    tokens, model = x_all.shape
    width = w_gate.shape[2]
    out = jax.ShapeDtypeStruct((count * half, model), F32)
    return pl.pallas_call(
        functools.partial(fwd_kernel, half, padded),
        grid=(count,),
        in_specs=[
            pl.BlockSpec((tokens, model), lambda i: (0, 0), pipeline_mode=pl.Buffered(1)),
            pl.BlockSpec((1, 1, tokens), lambda i: (start + i, 0, 0)),
            pl.BlockSpec((1, model, width), lambda i: (start + i, 0, 0)),
            pl.BlockSpec((1, model, width), lambda i: (start + i, 0, 0)),
            pl.BlockSpec((1, width, model), lambda i: (start + i, 0, 0)),
        ],
        out_specs=[pl.BlockSpec((2 * half, model), lambda i: (i // 2, 0))] * 2,
        out_shape=[out, out],
        scratch_shapes=[pltpu.VMEM((2 * padded, tokens), BF16), pltpu.VMEM((2 * padded, model), BF16)],
        cost_estimate=pl.CostEstimate(
            flops=count * 2 * 2 * padded * model * (tokens + 3 * width),
            bytes_accessed=count * (6 * model * width + 8 * half * model) + 2 * tokens * model,
            transcendentals=count * 2 * padded * width),
        compiler_params=pltpu.CompilerParams(dimension_semantics=('arbitrary',), vmem_limit_bytes=48 << 20),
    )(x_all, row_ids, w_gate, w_up, w_down)


def expert_bwd(chunks, sizes, x_all, dy_all, row_ids, gates, w_gate, w_up, w_down):
    other, win_other, own, win_own = sizes
    tokens, model = x_all.shape
    count, _, width = w_gate.shape
    per_chunk = count // chunks
    far_rows, near_rows = per_chunk * other, count * own
    far_pad = max(j * other // 8 * 8 + win_other for j in range(per_chunk))
    near_pad = max(j * own // 8 * 8 + win_own for j in range(count))
    part_shapes = [jax.ShapeDtypeStruct((far_rows, model), F32)] * (2 * chunks) + [jax.ShapeDtypeStruct((near_rows, model), F32)] * 2
    rows = 2 * (win_other + win_own)
    outs = pl.pallas_call(
        functools.partial(bwd_kernel, sizes, per_chunk),
        grid=(count,),
        in_specs=[
            pl.BlockSpec((tokens, model), lambda i: (0, 0), pipeline_mode=pl.Buffered(1)),
            pl.BlockSpec((tokens, model), lambda i: (0, 0), pipeline_mode=pl.Buffered(1)),
            pl.BlockSpec((1, 1, tokens), lambda i: (i, 0, 0)),
            pl.BlockSpec((1, 1, tokens), lambda i: (i, 0, 0)),
            pl.BlockSpec((1, model, width), lambda i: (i, 0, 0)),
            pl.BlockSpec((1, model, width), lambda i: (i, 0, 0)),
            pl.BlockSpec((1, width, model), lambda i: (i, 0, 0)),
        ],
        out_specs=[
            pl.BlockSpec((1, model, width), lambda i: (i, 0, 0)),
            pl.BlockSpec((1, model, width), lambda i: (i, 0, 0)),
            pl.BlockSpec((1, width, model), lambda i: (i, 0, 0)),
        ] + [pl.BlockSpec(memory_space=pl.ANY)] * len(part_shapes),
        out_shape=[
            jax.ShapeDtypeStruct((count, model, width), F32),
            jax.ShapeDtypeStruct((count, model, width), F32),
            jax.ShapeDtypeStruct((count, width, model), F32),
        ] + part_shapes,
        scratch_shapes=[
            pltpu.VMEM((2 * chunks, far_pad, model), F32),
            pltpu.VMEM((2, near_pad, model), F32),
            pltpu.SemaphoreType.DMA((len(part_shapes),)),
            pltpu.VMEM((rows, tokens), BF16),
            pltpu.VMEM((rows, model), BF16),
            pltpu.VMEM((rows, model), BF16),
        ],
        cost_estimate=pl.CostEstimate(
            flops=count * 2 * rows * model * (2 * tokens + 8 * width),
            bytes_accessed=count * (18 * model * width + 4 * rows * model) + 4 * tokens * model,
            transcendentals=count * rows * width),
        compiler_params=pltpu.CompilerParams(dimension_semantics=('arbitrary',), vmem_limit_bytes=60 << 20),
        name='expert_bwd',
    )(x_all, dy_all, row_ids, gates, w_gate, w_up, w_down)
    parts = outs[3:]
    return outs[:3], [(parts[2 * c], parts[2 * c + 1]) for c in range(chunks + 1)]


def shared_grad_kernel(step, x_ref, dy_ref, wg_ref, wu_ref, wd_ref, dg_ref, du_ref, dd_ref, h_ref, da_ref, db_ref):
    tokens, model = x_ref.shape

    @pl.loop(0, tokens // step)
    def _(i):
        rows = pl.ds(pl.multiple_of(i * step, step), step)
        a = rounded(dot(x_ref[rows, :], wg_ref[...]))
        b = rounded(dot(x_ref[rows, :], wu_ref[...]))
        dh = rounded(dot(dy_ref[rows, :], wd_ref[...], NT))
        h_ref[rows, :], da_ref[rows, :], db_ref[rows, :] = swiglu_bwd(a, b, dh)

    @pl.loop(0, model // step)
    def _(i):
        cols = pl.ds(pl.multiple_of(i * step, step), step)
        dd_ref[:, cols] = dot(h_ref[...], dy_ref[:, cols], TN)
        dg_ref[cols, :] = dot(x_ref[:, cols], da_ref[...], TN)
        du_ref[cols, :] = dot(x_ref[:, cols], db_ref[...], TN)


def shared_grad(x_all, dy_all, ws_gate, ws_up, ws_down):
    tokens, model = x_all.shape
    width = ws_gate.shape[1]
    block = min(width, 256)
    full = pl.BlockSpec((tokens, model), lambda i: (0, 0), pipeline_mode=pl.Buffered(1))
    col = pl.BlockSpec((model, block), lambda i: (0, i))
    row = pl.BlockSpec((block, model), lambda i: (i, 0))
    return pl.pallas_call(
        functools.partial(shared_grad_kernel, 256),
        grid=(width // block,),
        in_specs=[full, full, col, col, row],
        out_specs=[col, col, row],
        out_shape=[jax.ShapeDtypeStruct((model, width), F32)] * 2 + [jax.ShapeDtypeStruct((width, model), F32)],
        scratch_shapes=[pltpu.VMEM((tokens, block), BF16)] * 3,
        cost_estimate=pl.CostEstimate(
            flops=12 * tokens * model * width, bytes_accessed=4 * tokens * model + 18 * model * width,
            transcendentals=tokens * width),
        compiler_params=pltpu.CompilerParams(dimension_semantics=('arbitrary',), vmem_limit_bytes=48 << 20),
        name='shared_grad',
    )(x_all, dy_all, ws_gate, ws_up, ws_down)


def split3(v):
    hi = lax.reduce_precision(v, 8, 7)
    rest = v - hi
    mid = lax.reduce_precision(rest, 8, 7)
    low = rest - mid
    return hi.astype(BF16), mid.astype(BF16), low.astype(BF16)


def sum3(v, axis):
    first, second, third = jnp.split(v, 3, axis=axis)
    return first + second + third


def core_partner(ep):
    return ep + 1 - 2 * (ep % 2)


def gather_kernel(x_ref, idx_ref, dy_ref, wg_ref, wu_ref, wd_ref, x_all, idx_all, dy_pair, wd_part, quarter, send_sem, recv_sem, idx_send, idx_recv, local_sem):
    tp = lax.axis_index('tp')
    ep = lax.axis_index('ep')
    eps = x_all.shape[0] // 2
    half = eps // 2
    tp_o = 1 - tp
    ep_x = (ep + half) % eps
    ep_c = core_partner(ep)

    def slot(e, t):
        return e * 2 + t

    others = [(tp_o, ep)]
    for k in range(1, eps):
        others += [(tp, (ep + k) % eps), (tp_o, (ep + k) % eps)]
    barrier = pltpu.get_barrier_semaphore()
    for t, e in others:
        pl.semaphore_signal(barrier, inc=1, device_id={'tp': t, 'ep': e}, device_id_type=MESH)
    pl.semaphore_wait(barrier, len(others))

    def send(k, src, dst, t, e):
        copy = pltpu.make_async_remote_copy(
            src_ref=src, dst_ref=dst, send_sem=send_sem.at[k], recv_sem=recv_sem.at[k],
            device_id={'tp': t, 'ep': e}, device_id_type=MESH)
        copy.start()
        return copy

    def block(e, t):
        return x_all.at[slot(e, t)]

    mine = block(ep, tp)
    to_y = send(0, x_ref, mine, tp_o, ep)
    to_x = send(1, x_ref, mine, tp, ep_x)
    to_c = send(2, x_ref, mine, tp, ep_c)
    own_idx = idx_all.at[slot(ep, tp)]
    idx_copies = []
    for k, (t, e) in enumerate(others):
        copy = pltpu.make_async_remote_copy(
            src_ref=idx_ref, dst_ref=own_idx, send_sem=idx_send.at[k], recv_sem=idx_recv.at[k],
            device_id={'tp': t, 'ep': e}, device_id_type=MESH)
        copy.start()
        idx_copies.append(copy)
    local = [
        pltpu.make_async_copy(x_ref, mine, local_sem.at[0]),
        pltpu.make_async_copy(idx_ref, own_idx, local_sem.at[1]),
        pltpu.make_async_copy(dy_ref, dy_pair.at[tp], local_sem.at[2]),
    ]
    width = quarter.shape[1] // 2
    cols = pl.ds(pl.multiple_of(ep * width, width), width)
    for k, ref in enumerate((wg_ref, wu_ref)):
        local.append(pltpu.make_async_copy(ref.at[:, cols], quarter.at[:, pl.ds(k * width, width)], local_sem.at[3 + k]))
    for copy in local:
        copy.start()
    dy_y = send(3, dy_ref, dy_pair.at[tp], tp_o, ep)
    rows = wd_part.shape[0]
    wd_y = send(4, wd_ref.at[pl.ds(ep * rows, rows)], wd_part, tp_o, ep)

    to_y.wait_recv()
    y_to_x = send(5, block(ep, tp_o), block(ep, tp_o), tp, ep_x)
    y_to_c = send(6, block(ep, tp_o), block(ep, tp_o), tp, ep_c)
    to_x.wait_recv()
    x_to_c = send(7, block(ep_x, tp), block(ep_x, tp), tp, ep_c)
    y_to_x.wait_recv()
    xy_to_c = send(8, block(ep_x, tp_o), block(ep_x, tp_o), tp, ep_c)
    for copy in (to_c, dy_y, wd_y, y_to_c, x_to_c, xy_to_c):
        copy.wait_recv()
    for copy in idx_copies:
        copy.wait_recv()
    for copy in local:
        copy.wait()
    for copy in (to_y, to_x, to_c, dy_y, wd_y, y_to_x, y_to_c, x_to_c, xy_to_c):
        copy.wait_send()
    for copy in idx_copies:
        copy.wait_send()


def gather_rows(devices, ep_size, x, idx_t, dy, ws_gate, ws_up, ws_down):
    _, model = x.shape
    any_spec = pl.BlockSpec(memory_space=pl.ANY)
    return pl.pallas_call(
        gather_kernel,
        in_specs=[any_spec] * 6,
        out_specs=[any_spec] * 5,
        out_shape=[
            jax.ShapeDtypeStruct((devices,) + x.shape, x.dtype),
            jax.ShapeDtypeStruct((devices,) + idx_t.shape, idx_t.dtype),
            jax.ShapeDtypeStruct((2,) + dy.shape, dy.dtype),
            jax.ShapeDtypeStruct((ws_down.shape[0] // ep_size, model), ws_down.dtype),
            jax.ShapeDtypeStruct((model, 2 * ws_gate.shape[1] // ep_size), ws_gate.dtype),
        ],
        scratch_shapes=[
            pltpu.SemaphoreType.DMA((9,)),
            pltpu.SemaphoreType.DMA((9,)),
            pltpu.SemaphoreType.DMA((devices - 1,)),
            pltpu.SemaphoreType.DMA((devices - 1,)),
            pltpu.SemaphoreType.DMA((5,)),
        ],
        cost_estimate=pl.CostEstimate(flops=60_000_000_000, bytes_accessed=4 * devices * x.size, transcendentals=0),
        compiler_params=pltpu.CompilerParams(collective_id=0, has_side_effects=True),
        name='gather_rows',
    )(x, idx_t, dy, ws_gate, ws_up, ws_down)


def solution(mesh):
    tp_size = mesh.shape['tp']
    ep_size = mesh.shape['ep']
    swap_tp = [(i, tp_size - 1 - i) for i in range(tp_size)]
    swap_x = [(i, (i + ep_size // 2) % ep_size) for i in range(ep_size)]
    swap_c = [(i, core_partner(i)) for i in range(ep_size)]

    def device_step(x, grad_y, w_router, w_gate, w_up, w_down, ws_gate, ws_up, ws_down, topk_idx):
        tok, model = x.shape
        top_k = topk_idx.shape[1]
        experts = w_router.shape[1]
        local_exp = w_gate.shape[0]
        groups = top_k // 2
        most = groups * tok // (2 * ep_size) + min(groups, ep_size // 2) * tok // ep_size
        cap = (2 * most + local_exp - 1) // local_exp
        half, padded = half_rows(cap, ep_size)
        shift = padded - half
        ep_i = lax.axis_index('ep')
        tp_i = lax.axis_index('tp')
        devices = ep_size * tp_size
        ep_order = (ep_i, (ep_i + ep_size // 2) % ep_size, core_partner(ep_i), core_partner((ep_i + ep_size // 2) % ep_size))

        def ep_pieces(piece):
            far = lax.ppermute(piece, 'ep', swap_x)
            return piece, far, lax.ppermute(piece, 'ep', swap_c), lax.ppermute(far, 'ep', swap_c)

        def ep_gather(piece):
            out = jnp.zeros((ep_size,) + piece.shape, piece.dtype)
            for e, part in zip(ep_order, ep_pieces(piece)):
                out = lax.dynamic_update_slice_in_dim(out, part[None], e, 0)
            return out

        x_blocks, idx_all, dy_pair, wd_part, quarter = gather_rows(devices, ep_size, x, topk_idx.T, grad_y, ws_gate, ws_up, ws_down)
        x_all = x_blocks.reshape(devices * tok, model)

        width_q = ws_gate.shape[1] // ep_size
        gu_part = lax.ppermute(quarter, 'tp', swap_tp)

        lower = (lax.broadcasted_iota(jnp.int32, (tok, tok), 0) > lax.broadcasted_iota(jnp.int32, (tok, tok), 1)).astype(BF16)
        local_ids = ep_i * local_exp + jnp.arange(local_exp, dtype=jnp.int32)
        hit = jnp.any(idx_all[None] == local_ids[:, None, None, None], axis=2)
        rank = jnp.einsum('edj,ij->edi', hit.astype(BF16), lower, preferred_element_type=F32).astype(jnp.int32)
        dev = jnp.arange(devices, dtype=jnp.int32)
        is_own = (dev % tp_size) == tp_i
        parity = jnp.arange(local_exp, dtype=jnp.int32) % 2
        base = (jnp.where(is_own, padded, 0) + (dev // tp_size) * cap)[None, :] + (parity * shift)[:, None]
        row_ids = jnp.where(hit, base[:, :, None] + rank, -1).reshape(local_exp, 1, devices * tok)

        fwd_parts = []
        start = 0
        rows_now = row_ids
        for count in FWD_CHUNKS:
            send, own = expert_fwd(start, count, half, padded, x_all, rows_now, w_gate, w_up, w_down)
            start += count
            rows_now, own = lax.optimization_barrier((rows_now, own))
            fwd_parts.append((lax.ppermute(send, 'tp', swap_tp), own))

        own0 = fwd_parts[-1][1]
        x_late, hit, rank, w_router, own0 = lax.optimization_barrier((x_all, hit, rank, w_router, own0))
        fwd_parts[-1] = (fwd_parts[-1][0], own0)

        logits_t = jnp.einsum('de,td->et', w_router, x_late, preferred_element_type=F32)
        probs_t = jax.nn.softmax(logits_t, axis=0)
        gates_local = GATE_SCALE * lax.dynamic_slice_in_dim(probs_t, ep_i * local_exp, local_exp, 0).reshape(local_exp, 1, devices * tok)

        sizes = windows(cap, ep_size)
        other, win_other, near, win_near = sizes
        per_chunk = local_exp // BWD_CHUNKS
        dev_ep = dev // tp_size
        place = jnp.zeros_like(dev)
        for k, e in enumerate(ep_order[1:]):
            place = jnp.where(dev_ep == e, k * cap, place)
        exp = jnp.arange(local_exp, dtype=jnp.int32)
        far_first = (jnp.where(is_own, win_other, 0) + place)[None, :] + ((exp % per_chunk) * other % 8)[:, None]
        near_first = jnp.where(is_own, win_near, 0)[None, :] + (2 * win_other + exp * near % 8)[:, None]
        first = jnp.where((dev_ep == ep_i)[None, :], near_first, far_first)
        bwd_ids = jnp.where(hit, first[:, :, None] + rank, -1).reshape(local_exp, 1, devices * tok)
        dy_all = ep_gather(dy_pair).reshape(devices * tok, model)
        (d_w_gate, d_w_up, d_w_down), bwd_out = expert_bwd(BWD_CHUNKS, sizes, x_all, dy_all, bwd_ids, gates_local, w_gate, w_up, w_down)
        bwd_parts = [(lax.ppermute(bwd_out[0][0], 'tp', swap_tp), bwd_out[0][1])]

        own_last = bwd_out[-1][1]
        x, grad_y, x_all, dy_all, topk_idx, w_router, own_last = lax.optimization_barrier(
            (x, grad_y, x_all, dy_all, topk_idx, w_router, own_last))
        bwd_out[-1] = (bwd_out[-1][0], own_last)

        gu_other = ep_pieces(gu_part)
        wd_other = jnp.concatenate(ep_pieces(wd_part), axis=0)
        wg_other = jnp.concatenate([p[:, :width_q] for p in gu_other], axis=1)
        wu_other = jnp.concatenate([p[:, width_q:] for p in gu_other], axis=1)
        shared = jnp.zeros((tok, model), F32)
        dx_shared = jnp.zeros((tok, model), F32)
        for wg, wu, wd in ((ws_gate, ws_up, ws_down), (wg_other, wu_other, wd_other)):
            a = rounded(dot(x, wg))
            b = rounded(dot(x, wu))
            dh = rounded(dot(grad_y, wd, NT))
            h, da, db = swiglu_bwd(a, b, dh)
            shared = shared + dot(h, wd)
            dx_shared = dx_shared + dot(da, wg, NT) + dot(db, wu, NT)
        ds_gate, ds_up, ds_down = shared_grad(x_all, dy_all, ws_gate, ws_up, ws_down)

        def back_rows(count):
            return count * cap + (-count * cap) % 8

        def slot_index(count):
            new = jnp.arange(ep_size * back_rows(count), dtype=jnp.int32)
            block, rest = new // back_rows(count), new % back_rows(count)
            return block, rest // cap, rest % cap, rest < count * cap

        def give_back(parts, count):
            recv, own = parts
            rows = (recv + own).astype(BF16)
            src, exp, rank, valid = slot_index(count)
            old = jnp.where(valid, exp * half + src * cap + rank, -1)
            perm = (old[:, None] == jnp.arange(count * half, dtype=jnp.int32)[None, :]).astype(BF16)
            out = dot(perm, rows).astype(BF16)
            out = out.reshape(ep_size, back_rows(count), model)
            return lax.all_to_all(out, 'ep', 0, 0).reshape(ep_size * back_rows(count), model)

        hit_own = jnp.any(topk_idx[:, None, :] == jnp.arange(experts, dtype=jnp.int32)[None, :, None], axis=2)
        rank_own = dot(lower, hit_own.astype(BF16))
        want = jnp.where(hit_own, rank_own, -1.0).astype(BF16)
        probs = jax.nn.softmax(dot(x, w_router), axis=-1)
        prob_parts = jnp.concatenate(split3(probs), axis=0)

        def expand(start, count):
            grp, exp, rank, valid = slot_index(count)
            col = jnp.where(valid, grp * local_exp + start + exp, -1)
            table = (jnp.arange(experts, dtype=jnp.int32)[:, None] == col[None, :]).astype(BF16)
            return table, jnp.where(valid, rank, -2).astype(F32)[None, :]

        routed = jnp.zeros((tok, model), F32)
        d_scores = jnp.zeros((tok, experts), F32)
        start = 0
        for parts, count in zip(fwd_parts, FWD_CHUNKS):
            back = give_back(parts, count)
            table, rank = expand(start, count)
            hits = dot(want, table) == rank
            gates = jnp.where(jnp.concatenate([hits] * 3, axis=0), dot(prob_parts, table), 0.0).astype(BF16)
            routed = routed + GATE_SCALE * sum3(dot(gates, back), 0)
            score = jnp.where(hits, dot(grad_y, back, NT), 0.0)
            part = dot(jnp.concatenate(split3(score), axis=0), table, NT)
            d_scores = d_scores + sum3(part, 0)
            start += count
        y_out = (shared + routed).astype(BF16)

        d_scores = GATE_SCALE * d_scores
        mean_score = jnp.sum(probs * d_scores, axis=-1, keepdims=True)
        d_logits = probs * (d_scores - mean_score)
        d_other = lax.ppermute(d_logits, 'tp', swap_tp)
        for send, own in bwd_out[1:]:
            bwd_parts.append((lax.ppermute(send, 'tp', swap_tp), own))
        d_pair = jnp.where(tp_i == 0, jnp.stack([d_logits, d_other]), jnp.stack([d_other, d_logits]))
        d_logits_all = ep_gather(d_pair).reshape(devices * tok, experts)
        d_router = sum3(dot(x_all, jnp.concatenate(split3(d_logits_all), axis=1), TN), 1)
        dx_sum = dx_shared + sum3(dot(jnp.concatenate(split3(d_logits), axis=0), w_router, NT), 0)

        def hits_of(grp, start, count):
            slot = jnp.arange(count * cap, dtype=jnp.int32)
            col = grp * local_exp + start + slot // cap
            table = (jnp.arange(experts, dtype=jnp.int32)[:, None] == col[None, :]).astype(BF16)
            return (dot(want, table) == (slot % cap).astype(F32)[None, :]).astype(BF16)

        swaps = (swap_x, swap_c, [(i, core_partner(d)) for i, d in swap_x])
        for c, (recv, own) in enumerate(bwd_parts[:-1]):
            rows = (recv + own).astype(BF16)
            slot = jnp.arange(per_chunk * cap, dtype=jnp.int32)
            for k, pairs in enumerate(swaps):
                old = slot // cap * other + k * cap + slot % cap
                perm = (old[:, None] == jnp.arange(per_chunk * other, dtype=jnp.int32)[None, :]).astype(BF16)
                back = dot(perm, rows).astype(BF16)
                back = lax.ppermute(back, 'ep', pairs)
                hits = hits_of(ep_order[1 + k], c * per_chunk, per_chunk)
                dx_sum = dx_sum + dot(hits, back)
        recv, own = bwd_parts[-1]
        dx_sum = lax.optimization_barrier(dx_sum)
        dx_sum = dx_sum + dot(hits_of(ep_i, 0, local_exp), (recv + own).astype(BF16))
        return y_out, dx_sum.astype(BF16), d_router, d_w_gate, d_w_up, d_w_down, ds_gate, ds_up, ds_down

    tok_spec = P(('ep', 'tp'), None)
    in_specs = (tok_spec, tok_spec, P(None, None), P('ep', None, 'tp'), P('ep', None, 'tp'), P('ep', 'tp', None), P(None, 'tp'), P(None, 'tp'), P('tp', None), tok_spec)
    out_specs = (tok_spec, tok_spec, P(None, None), P('ep', None, 'tp'), P('ep', None, 'tp'), P('ep', 'tp', None), P(None, 'tp'), P(None, 'tp'), P('tp', None))

    return jax.shard_map(device_step, mesh=mesh, in_specs=in_specs, out_specs=out_specs, check_vma=False)
```

profile of v0, /device:TPU:0, one launch (start us, length us, event | category | flops | bytes accessed | tf_op | source)
XLA Modules:
  0.0 578.1 jit_solution(11970596324997297293)
XLA Ops:
  0.7 65.6 %gather_rows.1 = (bf16[8,192,1536]{2,1,0:T(8,128)(2,1)}, s32[8,6,192]{2,1,0:T(8,128)}, bf16[2,192,1536]{2,1,0:T(8,128)(2,1)}, bf16[128,1536]{1,0:T(8,128)(2,1)}, bf16[1536,256]{1,0:T(8,128)(2,1)}) custom-call(bf16[192,1536]{1,0:T(8,128)(2,1)} %x_ref.1, s32[6,192]{1,0:T(8,128)} %bitcast.100, bf16[192,1536]{1,0:T(8,128)(2,1)} %dy_ref.1, ...), custom_call_target="tpu_custom_call" | custom-call | flops 60000002048 | bytes 9437184 | tf_op jit(solution)/shard_map/gather_rows/pallas_call | solution.py:374
  76.4 1.8 constant_dynamic-update-slice_fusion.3
  80.9 7.8 %shard_map.169 = (f32[168,1536]{1,0:T(8,128)S(1)}, f32[168,1536]{1,0:T(8,128)S(1)}) custom-call(bf16[1536,1536]{1,0:T(8,128)(2,1)} %bitcast.84, s32[16,1,1536]{2,1,0:T(1,128)S(1)} %reshape.612.row_ref, bf16[16,1536,256]{2,1,0:T(8,128)(2,1)} %w1_ref.7, bf16[16,1536,256]{2,1,0:T(8,128)(2,1)} %w3_ref.7, bf16[16,256,1536]{2,1,0:T(8,128)(2,1)} %w2_ref.7), custom_call_target="tpu_custom_call" | custom-call | flops 2491416576 | bytes 11501568 | tf_op jit(solution)/shard_map/pallas_call | solution.py:165
  88.7 22.4 %shard_map.170 = (f32[672,1536]{1,0:T(8,128)S(1)}, f32[672,1536]{1,0:T(8,128)}) custom-call(bf16[1536,1536]{1,0:T(8,128)(2,1)} %bitcast.85, s32[16,1,1536]{2,1,0:T(1,128)S(1)} %reshape.612.row_ref, bf16[16,1536,256]{2,1,0:T(8,128)(2,1)} %w1_ref.7, bf16[16,1536,256]{2,1,0:T(8,128)(2,1)} %w3_ref.7, bf16[16,256,1536]{2,1,0:T(8,128)(2,1)} %w2_ref.7), custom_call_target="tpu_custom_call" | custom-call | flops 9965666304 | bytes 31850496 | tf_op jit(solution)/shard_map/pallas_call | solution.py:165
  111.1 2.0 copy-done.6
  113.0 18.3 %shard_map.171 = (f32[504,1536]{1,0:T(8,128)}, f32[504,1536]{1,0:T(8,128)}) custom-call(bf16[1536,1536]{1,0:T(8,128)(2,1)} %bitcast.86, s32[16,1,1536]{2,1,0:T(1,128)S(1)} %reshape.612.row_ref, bf16[16,1536,256]{2,1,0:T(8,128)(2,1)} %w1_ref.7, bf16[16,1536,256]{2,1,0:T(8,128)(2,1)} %w3_ref.7, bf16[16,256,1536]{2,1,0:T(8,128)(2,1)} %w2_ref.7), custom_call_target="tpu_custom_call" | custom-call | flops 7474249728 | bytes 25067520 | tf_op jit(solution)/shard_map/pallas_call | solution.py:165
  133.5 5.6 fusion.230
  141.8 1.7 reshape.613.row_ref
  146.3 1.8 constant_dynamic-update-slice_fusion.2
  148.6 1.8 constant_dynamic-update-slice_fusion.1
  150.4 2.0 fusion.226
  154.7 15.8 %collective-permute-done.10 = f32[168,1536]{1,0:T(8,128)S(1)} collective-permute-done((f32[168,1536]{1,0:T(8,128)S(1)}, f32[168,1536]{1,0:T(8,128)S(1)}, u32[]{:S(2)}, u32[]{:S(2)}) %collective-permute-start.10) | collective-permute-done | bytes 1032224 | tf_op jit(solution)/shard_map/ppermute | solution.py:453
  171.7 4.3 all-to-all-start
  176.1 1.8 collective-permute-start.4
  179.0 2.5 bitcast_dynamic-update-slice_fusion.1
  181.4 20.9 %collective-permute-done.4 = bf16[1536,256]{1,0:T(8,128)(2,1)} collective-permute-done((bf16[1536,256]{1,0:T(8,128)(2,1)}, bf16[1536,256]{1,0:T(8,128)(2,1)}, u32[]{:S(2)}, u32[]{:S(2)}) %collective-permute-start.4) | collective-permute-done | bytes 786464 | tf_op jit(solution)/shard_map/ppermute | solution.py:421
  202.3 2.0 fusion.227
  206.4 104.4 %expert_bwd.1 = (f32[16,1536,256]{2,1,0:T(8,128)}, f32[16,1536,256]{2,1,0:T(8,128)}, f32[16,256,1536]{2,1,0:T(8,128)}, f32[504,1536]{1,0:T(8,128)}, f32[504,1536...) custom-call(bf16[1536,1536]{1,0:T(8,128)(2,1)} %bitcast.88, ...), custom_call_target="tpu_custom_call" | custom-call | flops 52344913920 | bytes 143130624 | tf_op jit(solution)/shard_map/expert_bwd/pallas_call | solution.py:196
  315.8 1.6 reduce-precision_convert_fusion.7
  327.1 1.7 fusion.78
  328.8 25.6 %shared_grad.1 = (f32[1536,512]{1,0:T(8,128)}, f32[1536,512]{1,0:T(8,128)}, f32[512,1536]{1,0:T(8,128)}) custom-call(bf16[1536,1536]{1,0:T(8,128)(2,1)} %bitcast.89, bf16[1536,1536]{1,0:T(8,128)(2,1)} %bitcast.92, bf16[1536,512]{1,0:T(8,128)(2,1)S(1)} %copy-done.2, bf16[1536,512]{1,0:T(8,128)(2,1)S(1)} %copy-done.4, bf16[512,1536]{1,0:T(8,128)(2,1)S(1)} %copy-done.1), custom_call_target="tpu_custom_call" | custom-call | flops 14495514624 | bytes 23592960 | tf_op jit(solution)/shard_map/shared_grad/pallas_call | solution.py:263
  355.3 1.7 fusion.68
  357.6 4.2 convolution_convert_fusion.1
  361.8 4.7 all-to-all-start.2
  367.4 2.8 convolution_add_fusion.2
  370.3 5.4 convolution_convert_fusion
  375.6 10.9 %all-to-all-done.2 = bf16[4,128,1536]{2,1,0:T(8,128)(2,1)} async-done(((bf16[4,128,1536]{2,1,0:T(8,128)(2,1)}), bf16[4,128,1536]{2,1,0:T(8,128)(2,1)}, u32[]{:S(2)}, u32[]{:S(2)}) %all-to-all-start.2) | async-done | bytes 1572896 | tf_op jit(solution)/shard_map/all_to_all | solution.py:515
  386.6 4.8 all-to-all-start.1
  391.4 2.1 reduce-precision_convert_fusion.5
  394.5 4.1 fusion.28
  398.6 37.5 %collective-permute-done.13 = f32[504,1536]{1,0:T(8,128)} collective-permute-done((f32[504,1536]{1,0:T(8,128)}, f32[504,1536]{1,0:T(8,128)}, u32[]{:S(2)}, u32[]{:S(2)}) %collective-permute-start.13) | collective-permute-done | bytes 3096608 | tf_op jit(solution)/shard_map/ppermute | solution.py:477
  436.0 2.3 add_convert_fusion.2
  442.0 59.3 %collective-permute-done.17 = f32[504,1536]{1,0:T(8,128)} collective-permute-done((f32[504,1536]{1,0:T(8,128)}, f32[504,1536]{1,0:T(8,128)}, u32[]{:S(2)}, u32[]{:S(2)}) %collective-permute-start.17) | collective-permute-done | bytes 3096608 | tf_op jit(solution)/shard_map/ppermute | solution.py:549
  501.3 2.3 add_convert_fusion.1
  508.0 2.4 reduce-precision_convert_fusion.1
  513.1 5.3 fusion.10
  518.4 4.6 fusion.11
  523.0 3.7 fusion.27
  528.7 5.8 %fusion.8 = bf16[192,1536]{1,0:T(8,128)(2,1)} fusion(f32[192,1536]{1,0:T(8,128)S(1)} %copy-done.24, bf16[512,1536]{1,0:T(8,128)(2,1)S(1)} %copy-done.20, f32[576,1536]{1,0:T(8,128)} %fusion.11, f32[576,1536]{1,0:T(8,128)} %fusion.10, f32[576,1536]{1,0:T(8,128)} %fusion.27, f32[192,512]{1,0:T(8,128)S(1)} %copy-done.75, f32[192,512]{1,0:T(8,128)S(1)} %copy-done.74), kind=kOutput, calls=%fused_computation.18 | convolution fusion | flops 306216960 | bytes 14745600 | tf_op jit(solution)/shard_map/dot_general | solution.py:24
  534.6 1.7 fusion.4
  538.1 3.2 collective-permute-done.23
  544.9 3.7 fusion.50
  554.2 9.1 %collective-permute-done.20 = bf16[168,1536]{1,0:T(8,128)(2,1)} collective-permute-done((bf16[168,1536]{1,0:T(8,128)(2,1)}, bf16[168,1536]{1,0:T(8,128)(2,1)}, u32[]{:S(2)}, u32[]{:S(2)}) %collective-permute-start.20) | collective-permute-done | bytes 516128 | tf_op jit(solution)/shard_map/ppermute | solution.py:569
  563.3 2.6 fusion.34
  565.9 2.7 fusion.33
  568.6 2.6 fusion.32
  571.2 4.3 fusion.7
  575.5 2.6 add_convert_fusion.7
  (279 shorter events, 68.9 us)
Async XLA Ops:
  0.6 132.7 %copy-start = (bf16[1536,64]{0,1:T(8,128)(2,1)S(1)}, bf16[1536,64]{0,1:T(8,128)(2,1)}, u32[]{:S(2)}) copy-start(bf16[1536,64]{0,1:T(8,128)(2,1)} %param.12) | copy-start | bytes 589828
  66.2 81.8 %collective-permute-start.8 = (bf16[128,1536]{1,0:T(8,128)(2,1)}, bf16[128,1536]{1,0:T(8,128)(2,1)}, u32[]{:S(2)}, u32[]{:S(2)}) collective-permute-start(bf16[128,1536]{1,0:T(8,128)(2,1)} %get-tuple-element.65), channel_id=1, source_target_pairs={{0,1},{1,0},{2,3},{3,2},{4,5},{5,4},{6,7},{7,6}} | collective-permute-start | bytes 1179656 | tf_op jit(solution)/shard_map/ppermute | solution.py:422
  66.4 78.4 %collective-permute-start.7 = (bf16[128,1536]{1,0:T(8,128)(2,1)}, bf16[128,1536]{1,0:T(8,128)(2,1)}, u32[]{:S(2)}, u32[]{:S(2)}) collective-permute-start(bf16[128,1536]{1,0:T(8,128)(2,1)} %get-tuple-element.65), channel_id=1, source_target_pairs={{0,2},{1,3},{2,0},{3,1},{4,6},{5,7},{6,4},{7,5}} | collective-permute-start | bytes 1179656 | tf_op jit(solution)/shard_map/ppermute | solution.py:421
  66.9 112.0 %collective-permute-start.1 = (bf16[2,192,1536]{2,1,0:T(8,128)(2,1)}, bf16[2,192,1536]{2,1,0:T(8,128)(2,1)}, u32[]{:S(2)}, u32[]{:S(2)}) collective-permute-start(bf16[2,192,1536]{2,1,0:T(8,128)(2,1)} %get-tuple-element.50), channel_id=1, source_target_pairs={{0,1},{1,0},{2,3},{3,2},{4,5},{5,4},{6,7},{7,6}} | collective-permute-start | bytes 3538952 | tf_op jit(solution)/shard_map/ppermute | solution.py:422
  67.0 109.0 %collective-permute-start = (bf16[2,192,1536]{2,1,0:T(8,128)(2,1)}, bf16[2,192,1536]{2,1,0:T(8,128)(2,1)S(1)}, u32[]{:S(2)}, u32[]{:S(2)}) collective-permute-start(bf16[2,192,1536]{2,1,0:T(8,128)(2,1)} %get-tuple-element.50), channel_id=1, source_target_pairs={{0,2},{1,3},{2,0},{3,1},{4,6},{5,7},{6,4},{7,5}} | collective-permute-start | bytes 3538952 | tf_op jit(solution)/shard_map/ppermute | solution.py:421
  68.5 81.9 %collective-permute-start.3 = (bf16[1536,256]{1,0:T(8,128)(2,1)}, bf16[1536,256]{1,0:T(8,128)(2,1)}, u32[]{:S(2)}, u32[]{:S(2)}) collective-permute-start(bf16[1536,256]{1,0:T(8,128)(2,1)} %get-tuple-element.64), channel_id=1, source_target_pairs={{0,4},{4,0},{1,5},{5,1},{2,6},{6,2},{3,7},{7,3}} | collective-permute-start | bytes 2359304 | tf_op jit(solution)/shard_map/ppermute | solution.py:434
  144.8 25.7 %collective-permute-start.10 = (f32[168,1536]{1,0:T(8,128)S(1)}, f32[168,1536]{1,0:T(8,128)S(1)}, u32[]{:S(2)}, u32[]{:S(2)}) collective-permute-start(f32[168,1536]{1,0:T(8,128)S(1)} %get-tuple-element.68), channel_id=1, source_target_pairs={{0,4},{4,0},{1,5},{5,1},{2,6},{6,2},{3,7},{7,3}} | collective-permute-start | bytes 3096584 | tf_op jit(solution)/shard_map/ppermute | solution.py:453
  148.1 22.4 %copy-start.60 = (s32[192]{0:T(256)S(1)}, s32[192]{0:T(256)}, u32[]{:S(2)}) copy-start(s32[192]{0:T(256)} %add_select_fusion.12) | copy-start | bytes 2308
  148.1 222.2 %collective-permute-start.11 = (f32[672,1536]{1,0:T(8,128)}, f32[672,1536]{1,0:T(8,128)}, u32[]{:S(2)}, u32[]{:S(2)}) collective-permute-start(f32[672,1536]{1,0:T(8,128)} %copy-done.6), channel_id=1, source_target_pairs={{0,4},{4,0},{1,5},{5,1},{2,6},{6,2},{3,7},{7,3}} | collective-permute-start | bytes 12386312 | tf_op jit(solution)/shard_map/ppermute | solution.py:453
  150.4 2.0 collective-permute-start.9
  152.5 204.6 %collective-permute-start.12 = (f32[504,1536]{1,0:T(8,128)}, f32[504,1536]{1,0:T(8,128)}, u32[]{:S(2)}, u32[]{:S(2)}) collective-permute-start(f32[504,1536]{1,0:T(8,128)} %get-tuple-element.72), channel_id=1, source_target_pairs={{0,4},{4,0},{1,5},{5,1},{2,6},{6,2},{3,7},{7,3}} | collective-permute-start | bytes 9289736 | tf_op jit(solution)/shard_map/ppermute | solution.py:453
  170.5 33.8 %collective-permute-start.5 = (bf16[1536,256]{1,0:T(8,128)(2,1)}, bf16[1536,256]{1,0:T(8,128)(2,1)S(1)}, u32[]{:S(2)}, u32[]{:S(2)}) collective-permute-start(bf16[1536,256]{1,0:T(8,128)(2,1)} %collective-permute-done.3), channel_id=1, source_target_pairs={{0,1},{1,0},{2,3},{3,2},{4,5},{5,4},{6,7},{7,6}} | collective-permute-start | bytes 2359304 | tf_op jit(solution)/shard_map/ppermute | solution.py:422
  171.7 144.1 %all-to-all-start = ((bf16[4,48,1536]{2,1,0:T(8,128)(2,1)}), bf16[4,48,1536]{2,1,0:T(8,128)(2,1)}, u32[]{:S(2)}, u32[]{:S(2)}) async-start(bf16[4,48,1536]{2,1,0:T(8,128)(2,1)} %bitcast.8), calls=%async_computation | async-start | bytes 1179648 | tf_op jit(solution)/shard_map/all_to_all | solution.py:515
  176.1 26.2 %collective-permute-start.4 = (bf16[1536,256]{1,0:T(8,128)(2,1)}, bf16[1536,256]{1,0:T(8,128)(2,1)}, u32[]{:S(2)}, u32[]{:S(2)}) collective-permute-start(bf16[1536,256]{1,0:T(8,128)(2,1)} %collective-permute-done.3), channel_id=1, source_target_pairs={{0,2},{1,3},{2,0},{3,1},{4,6},{5,7},{6,4},{7,5}} | collective-permute-start | bytes 2359304 | tf_op jit(solution)/shard_map/ppermute | solution.py:421
  178.9 26.3 %collective-permute-start.2 = (bf16[2,192,1536]{2,1,0:T(8,128)(2,1)S(1)}, bf16[2,192,1536]{2,1,0:T(8,128)(2,1)S(1)}, u32[]{:S(2)}, u32[]{:S(2)}) collective-permute-start(bf16[2,192,1536]{2,1,0:T(8,128)(2,1)S(1)} %collective-permute-done), channel_id=1, source_target_pairs={{0,1},{1,0},{2,3},{3,2},{4,5},{5,4},{6,7},{7,6}} | collective-permute-start | bytes 3538952 | tf_op jit(solution)/shard_map/ppermute | solution.py:422
  202.3 117.3 %collective-permute-start.6 = (bf16[1536,256]{1,0:T(8,128)(2,1)}, bf16[1536,256]{1,0:T(8,128)(2,1)}, u32[]{:S(2)}, u32[]{:S(2)}) collective-permute-start(bf16[1536,256]{1,0:T(8,128)(2,1)} %collective-permute-done.4), channel_id=1, source_target_pairs={{0,1},{1,0},{2,3},{3,2},{4,5},{5,4},{6,7},{7,6}} | collective-permute-start | bytes 2359304 | tf_op jit(solution)/shard_map/ppermute | solution.py:422
  206.4 104.4 %copy-start.47 = (s32[192,6]{0,1:T(8,128)S(1)}, s32[192,6]{0,1:T(8,128)}, u32[]{:S(2)}) copy-start(s32[192,6]{0,1:T(8,128)} %param.19) | copy-start | bytes 13828
  206.4 104.7 %copy-start.2 = (bf16[1536,512]{1,0:T(8,128)(2,1)S(1)}, bf16[1536,512]{1,0:T(8,128)(2,1)}, u32[]{:S(2)}) copy-start(bf16[1536,512]{1,0:T(8,128)(2,1)} %wg_ref.3) | copy-start | bytes 4718596
  206.4 104.7 %copy-start.9 = (bf16[192,1536]{1,0:T(8,128)(2,1)S(1)}, bf16[192,1536]{1,0:T(8,128)(2,1)}, u32[]{:S(2)}) copy-start(bf16[192,1536]{1,0:T(8,128)(2,1)} %x_ref.1) | copy-start | bytes 1769476
  312.3 82.2 %collective-permute-start.21 = (f32[336,1536]{1,0:T(8,128)}, f32[336,1536]{1,0:T(8,128)}, u32[]{:S(2)}, u32[]{:S(2)}) collective-permute-start(f32[336,1536]{1,0:T(8,128)} %get-tuple-element.79), channel_id=1, source_target_pairs={{0,4},{4,0},{1,5},{5,1},{2,6},{6,2},{3,7},{7,3}} | collective-permute-start | bytes 6193160 | tf_op jit(solution)/shard_map/ppermute | solution.py:549
  313.8 122.3 %collective-permute-start.13 = (f32[504,1536]{1,0:T(8,128)}, f32[504,1536]{1,0:T(8,128)}, u32[]{:S(2)}, u32[]{:S(2)}) collective-permute-start(f32[504,1536]{1,0:T(8,128)} %get-tuple-element.75), channel_id=1, source_target_pairs={{0,4},{4,0},{1,5},{5,1},{2,6},{6,2},{3,7},{7,3}} | collective-permute-start | bytes 9289736 | tf_op jit(solution)/shard_map/ppermute | solution.py:477
  318.9 8.2 %copy-start.14 = (f32[192,512]{1,0:T(8,128)}, f32[192,512]{1,0:T(8,128)S(1)}, u32[]{:S(2)}) copy-start(f32[192,512]{1,0:T(8,128)S(1)} %fusion.25) | copy-start | bytes 1179652
  319.6 35.7 %copy-start.28 = (f32[192,512]{1,0:T(8,128)}, f32[192,512]{1,0:T(8,128)S(1)}, u32[]{:S(2)}) copy-start(f32[192,512]{1,0:T(8,128)S(1)} %fusion.26) | copy-start | bytes 1179652
  319.6 181.7 %collective-permute-start.17 = (f32[504,1536]{1,0:T(8,128)}, f32[504,1536]{1,0:T(8,128)}, u32[]{:S(2)}, u32[]{:S(2)}) collective-permute-start(f32[504,1536]{1,0:T(8,128)} %get-tuple-element.77), channel_id=1, source_target_pairs={{0,4},{4,0},{1,5},{5,1},{2,6},{6,2},{3,7},{7,3}} | collective-permute-start | bytes 9289736 | tf_op jit(solution)/shard_map/ppermute | solution.py:549
  323.0 32.3 %copy-start.73 = (f32[192,512]{1,0:T(8,128)}, f32[192,512]{1,0:T(8,128)S(1)}, u32[]{:S(2)}) copy-start(f32[192,512]{1,0:T(8,128)S(1)} %fusion.23) | copy-start | bytes 1179652
  357.6 8.8 %copy-start.57 = (s32[512]{0:T(512)S(1)}, s32[512]{0:T(512)}, u32[]{:S(2)}) copy-start(s32[512]{0:T(512)} %fusion.173) | copy-start | bytes 6148
  357.6 8.8 %copy-start.58 = (f32[512]{0:T(512)S(1)}, f32[512]{0:T(512)}, u32[]{:S(2)}) copy-start(f32[512]{0:T(512)} %select_convert_fusion.2) | copy-start | bytes 6148
  361.8 24.8 %all-to-all-start.2 = ((bf16[4,128,1536]{2,1,0:T(8,128)(2,1)}), bf16[4,128,1536]{2,1,0:T(8,128)(2,1)}, u32[]{:S(2)}, u32[]{:S(2)}) async-start(bf16[4,128,1536]{2,1,0:T(8,128)(2,1)} %bitcast.12), calls=%async_computation.2 | async-start | bytes 3145728 | tf_op jit(solution)/shard_map/all_to_all | solution.py:515
  386.6 121.4 %all-to-all-start.1 = ((bf16[4,168,1536]{2,1,0:T(8,128)(2,1)}), bf16[4,168,1536]{2,1,0:T(8,128)(2,1)}, u32[]{:S(2)}, u32[]{:S(2)}) async-start(bf16[4,168,1536]{2,1,0:T(8,128)(2,1)} %bitcast.10), calls=%async_computation.1 | async-start | bytes 4128768 | tf_op jit(solution)/shard_map/all_to_all | solution.py:515
  394.5 41.5 %copy-start.18 = (f32[504,1536]{1,0:T(8,128)S(1)}, f32[504,1536]{1,0:T(8,128)}, u32[]{:S(2)}) copy-start(f32[504,1536]{1,0:T(8,128)} %get-tuple-element.76) | copy-start | bytes 9289732
  438.8 62.4 %copy-start.17 = (f32[504,1536]{1,0:T(8,128)S(1)}, f32[504,1536]{1,0:T(8,128)}, u32[]{:S(2)}) copy-start(f32[504,1536]{1,0:T(8,128)} %get-tuple-element.78) | copy-start | bytes 9289732
  439.8 131.4 %collective-permute-start.14 = (bf16[168,1536]{1,0:T(8,128)(2,1)S(1)}, bf16[168,1536]{1,0:T(8,128)(2,1)}, u32[]{:S(2)}, u32[]{:S(2)}) collective-permute-start(bf16[168,1536]{1,0:T(8,128)(2,1)S(1)} %convolution_convert_fusion.8), channel_id=1, source_target_pairs={{0,2},{1,3},{2,0},{3,1},{4,6},{5,7},{6,4},{7,5}} | collective-permute-start | bytes 1548296 | tf_op jit(solution)/shard_map/ppermute | solution.py:569
  440.4 112.2 %collective-permute-start.15 = (bf16[168,1536]{1,0:T(8,128)(2,1)S(1)}, bf16[168,1536]{1,0:T(8,128)(2,1)}, u32[]{:S(2)}, u32[]{:S(2)}) collective-permute-start(bf16[168,1536]{1,0:T(8,128)(2,1)S(1)} %convolution_convert_fusion.7), channel_id=1, source_target_pairs={{0,1},{1,0},{2,3},{3,2},{4,5},{5,4},{6,7},{7,6}} | collective-permute-start | bytes 1548296 | tf_op jit(solution)/shard_map/ppermute | solution.py:569
  440.4 109.1 %collective-permute-start.16 = (bf16[168,1536]{1,0:T(8,128)(2,1)S(1)}, bf16[168,1536]{1,0:T(8,128)(2,1)}, u32[]{:S(2)}, u32[]{:S(2)}) collective-permute-start(bf16[168,1536]{1,0:T(8,128)(2,1)S(1)} %convolution_convert_fusion.6), channel_id=1, source_target_pairs={{0,3},{1,2},{2,1},{3,0},{4,7},{5,6},{6,5},{7,4}} | collective-permute-start | bytes 1548296 | tf_op jit(solution)/shard_map/ppermute | solution.py:569
  504.9 63.7 %collective-permute-start.18 = (bf16[168,1536]{1,0:T(8,128)(2,1)}, bf16[168,1536]{1,0:T(8,128)(2,1)}, u32[]{:S(2)}, u32[]{:S(2)}) collective-permute-start(bf16[168,1536]{1,0:T(8,128)(2,1)} %convolution_convert_fusion.5), channel_id=1, source_target_pairs={{0,2},{1,3},{2,0},{3,1},{4,6},{5,7},{6,4},{7,5}} | collective-permute-start | bytes 1548296 | tf_op jit(solution)/shard_map/ppermute | solution.py:569
  511.6 24.7 %collective-permute-start.22 = (f32[192,64]{0,1:T(8,128)S(1)}, f32[192,64]{0,1:T(8,128)S(1)}, u32[]{:S(2)}, u32[]{:S(2)}) collective-permute-start(f32[192,64]{0,1:T(8,128)S(1)} %get-tuple-element.90), channel_id=1, source_target_pairs={{0,4},{4,0},{1,5},{5,1},{2,6},{6,2},{3,7},{7,3}} | collective-permute-start | bytes 147464 | tf_op jit(solution)/shard_map/ppermute | solution.py:547
  528.7 5.9 %copy-start.31 = (bf16[1536,128]{1,0:T(8,128)(2,1)S(1)}, bf16[1536,128]{1,0:T(8,128)(2,1)}, u32[]{:S(2)}) copy-start(bf16[1536,128]{1,0:T(8,128)(2,1)} %get-tuple-element.95) | copy-start | bytes 1179652
  528.7 5.9 %copy-start.33 = (bf16[1536,128]{1,0:T(8,128)(2,1)S(1)}, bf16[1536,128]{1,0:T(8,128)(2,1)}, u32[]{:S(2)}) copy-start(bf16[1536,128]{1,0:T(8,128)(2,1)} %get-tuple-element.97) | copy-start | bytes 1179652
  528.7 5.9 %copy-start.35 = (bf16[1536,128]{1,0:T(8,128)(2,1)S(1)}, bf16[1536,128]{1,0:T(8,128)(2,1)}, u32[]{:S(2)}) copy-start(bf16[1536,128]{1,0:T(8,128)(2,1)} %get-tuple-element.99) | copy-start | bytes 1179652
  528.7 5.9 %copy-start.37 = (bf16[1536,128]{1,0:T(8,128)(2,1)S(1)}, bf16[1536,128]{1,0:T(8,128)(2,1)}, u32[]{:S(2)}) copy-start(bf16[1536,128]{1,0:T(8,128)(2,1)} %copy-done.36) | copy-start | bytes 1179652
  528.7 5.9 %copy-start.76 = (f32[192,1536]{1,0:T(8,128)S(1)}, f32[192,1536]{1,0:T(8,128)}, u32[]{:S(2)}) copy-start(f32[192,1536]{1,0:T(8,128)} %fusion.68) | copy-start | bytes 3538948
  536.3 5.0 collective-permute-start.23
  541.3 1.3 collective-permute-start.24
  542.6 1.3 collective-permute-start.25
  544.0 21.9 %collective-permute-start.19 = (bf16[168,1536]{1,0:T(8,128)(2,1)}, bf16[168,1536]{1,0:T(8,128)(2,1)}, u32[]{:S(2)}, u32[]{:S(2)}) collective-permute-start(bf16[168,1536]{1,0:T(8,128)(2,1)} %convolution_convert_fusion.4), channel_id=1, source_target_pairs={{0,1},{1,0},{2,3},{3,2},{4,5},{5,4},{6,7},{7,6}} | collective-permute-start | bytes 1548296 | tf_op jit(solution)/shard_map/ppermute | solution.py:569
  549.4 13.8 %collective-permute-start.20 = (bf16[168,1536]{1,0:T(8,128)(2,1)}, bf16[168,1536]{1,0:T(8,128)(2,1)}, u32[]{:S(2)}, u32[]{:S(2)}) collective-permute-start(bf16[168,1536]{1,0:T(8,128)(2,1)} %convolution_convert_fusion.3), channel_id=1, source_target_pairs={{0,3},{1,2},{2,1},{3,0},{4,7},{5,6},{6,5},{7,4}} | collective-permute-start | bytes 1548296 | tf_op jit(solution)/shard_map/ppermute | solution.py:569
  550.9 12.4 %copy-start.56 = (s32[168]{0:T(256)S(1)}, s32[168]{0:T(256)}, u32[]{:S(2)}) copy-start(s32[168]{0:T(256)} %get-tuple-element.134) | copy-start | bytes 2020
  552.5 13.4 %copy-start.55 = (s32[168]{0:T(256)S(1)}, s32[168]{0:T(256)}, u32[]{:S(2)}) copy-start(s32[168]{0:T(256)} %get-tuple-element.135) | copy-start | bytes 2020
  (58 other events, 187.4 us)
where the time goes:
time: 579 us; the launch traced here: 578 us
  Pallas kernels  244 us (42%)
  waiting for transfers between devices  159 us (27%)
  matrix products  91.7 us (16%)
  starting transfers between devices  32.9 us (6%)
  local copies, waits for them, and re-layouts  28.5 us (5%)
  other arithmetic  20.4 us (4%)
    pallas_call x1, Pallas kernels, expert_bwd(): pl.pallas_call(functools.partial(bwd_kernel, sizes, per_chunk), grid=(cou...  104 us
    dot_general x44, matrix products, dot(): return lax.dot_general(a, b, dims, preferred_element_type=F32)  85.2 us
    pallas_call x1, Pallas kernels, gather_rows(): pl.pallas_call(gather_kernel, in_specs=[any_spec] * 6, out_specs=[any_spe...  65.6 us
    ppermute x2, waiting for transfers between devices, device_step(): bwd_parts.append((lax.ppermute(send, 'tp', swap_tp), own))  59.3 us
    pallas_call x3, Pallas kernels, expert_fwd(): pl.pallas_call(functools.partial(fwd_kernel, half, padded), grid=(count,)...  48.5 us
    ppermute x1, waiting for transfers between devices, device_step(): bwd_parts = [(lax.ppermute(bwd_out[0][0], 'tp', swap_tp), bwd_out[0][1])]  37.5 us
    pallas_call x1, Pallas kernels, shared_grad(): pl.pallas_call(functools.partial(shared_grad_kernel, 256), grid=(width //...  25.6 us
    ppermute x4, waiting for transfers between devices, ep_pieces(): far = lax.ppermute(piece, 'ep', swap_x)  24.1 us
  transfers between devices with their start and end apart: 29, of which 9 were waited for; matrix products, arithmetic and copies ran while one was open for 22% of the time, Pallas kernels for 31%

commit v1 on v0

--- a/solution.py
+++ b/solution.py
@@ -292,7 +292,7 @@
     return ep + 1 - 2 * (ep % 2)
 
 
-def gather_kernel(x_ref, idx_ref, dy_ref, wg_ref, wu_ref, wd_ref, x_all, idx_all, dy_pair, wd_part, quarter, send_sem, recv_sem, idx_send, idx_recv, local_sem):
+def gather_kernel(x_ref, idx_ref, dy_ref, wg_ref, wu_ref, wd_ref, x_all, idx_all, dy_pair, wd_part, quarter, send_sem, recv_sem, idx_send, idx_recv, local_sem, x_buf, dy_buf, q_buf):
     tp = lax.axis_index('tp')
     ep = lax.axis_index('ep')
     eps = x_all.shape[0] // 2
@@ -334,21 +334,30 @@
             device_id={'tp': t, 'ep': e}, device_id_type=MESH)
         copy.start()
         idx_copies.append(copy)
-    local = [
-        pltpu.make_async_copy(x_ref, mine, local_sem.at[0]),
-        pltpu.make_async_copy(idx_ref, own_idx, local_sem.at[1]),
-        pltpu.make_async_copy(dy_ref, dy_pair.at[tp], local_sem.at[2]),
-    ]
     width = quarter.shape[1] // 2
     cols = pl.ds(pl.multiple_of(ep * width, width), width)
-    for k, ref in enumerate((wg_ref, wu_ref)):
-        local.append(pltpu.make_async_copy(ref.at[:, cols], quarter.at[:, pl.ds(k * width, width)], local_sem.at[3 + k]))
-    for copy in local:
+    load = [
+        pltpu.make_async_copy(x_ref, x_buf, local_sem.at[0]),
+        pltpu.make_async_copy(dy_ref, dy_buf, local_sem.at[1]),
+        pltpu.make_async_copy(wg_ref.at[:, cols], q_buf.at[:, pl.ds(0, width)], local_sem.at[2]),
+        pltpu.make_async_copy(wu_ref.at[:, cols], q_buf.at[:, pl.ds(width, width)], local_sem.at[3]),
+    ]
+    store = [
+        pltpu.make_async_copy(x_buf, mine, local_sem.at[4]),
+        pltpu.make_async_copy(dy_buf, dy_pair.at[tp], local_sem.at[5]),
+        pltpu.make_async_copy(q_buf, quarter, local_sem.at[6]),
+        pltpu.make_async_copy(idx_ref, own_idx, local_sem.at[7]),
+    ]
+    for copy in load:
         copy.start()
     dy_y = send(3, dy_ref, dy_pair.at[tp], tp_o, ep)
     rows = wd_part.shape[0]
     wd_y = send(4, wd_ref.at[pl.ds(ep * rows, rows)], wd_part, tp_o, ep)
 
+    for copy in load:
+        copy.wait()
+    for copy in store:
+        copy.start()
     to_y.wait_recv()
     y_to_x = send(5, block(ep, tp_o), block(ep, tp_o), tp, ep_x)
     y_to_c = send(6, block(ep, tp_o), block(ep, tp_o), tp, ep_c)
@@ -360,7 +369,7 @@
         copy.wait_recv()
     for copy in idx_copies:
         copy.wait_recv()
-    for copy in local:
+    for copy in store:
         copy.wait()
     for copy in (to_y, to_x, to_c, dy_y, wd_y, y_to_x, y_to_c, x_to_c, xy_to_c):
         copy.wait_send()
@@ -387,7 +396,10 @@
             pltpu.SemaphoreType.DMA((9,)),
             pltpu.SemaphoreType.DMA((devices - 1,)),
             pltpu.SemaphoreType.DMA((devices - 1,)),
-            pltpu.SemaphoreType.DMA((5,)),
+            pltpu.SemaphoreType.DMA((8,)),
+            pltpu.VMEM(x.shape, x.dtype),
+            pltpu.VMEM(dy.shape, dy.dtype),
+            pltpu.VMEM((model, 2 * ws_gate.shape[1] // ep_size), ws_gate.dtype),
         ],
         cost_estimate=pl.CostEstimate(flops=60_000_000_000, bytes_accessed=4 * devices * x.size, transcendentals=0),
         compiler_params=pltpu.CompilerParams(collective_id=0, has_side_effects=True),

time: 579 us -> 555 us (0.959)
  Pallas kernels: 244 us -> 219 us
    pallas_call x1, Pallas kernels: 65.6 us -> 41 us  [gather_rows(): pl.pallas_call(gather_kernel, in_specs=[any_spec] * 6, out_specs=[any_spe...]
  transfers between devices with their start and end apart: 29 -> 29, of which waited for: 9 -> 9; matrix products, arithmetic and copies ran while one was open for 22% -> 23% of each run, Pallas kernels for 31% -> 32%
where the time goes in v1:
time: 555 us; the launch traced here: 553 us
  Pallas kernels  219 us (39%)
  waiting for transfers between devices  161 us (29%)
  matrix products  91.7 us (17%)
  starting transfers between devices  31.1 us (6%)
  local copies, waits for them, and re-layouts  28.5 us (5%)
  other arithmetic  20.4 us (4%)
    pallas_call x1, Pallas kernels, expert_bwd(): pl.pallas_call(functools.partial(bwd_kernel, sizes, per_chunk), grid=(cou...  104 us
    dot_general x44, matrix products, dot(): return lax.dot_general(a, b, dims, preferred_element_type=F32)  85.2 us
    ppermute x2, waiting for transfers between devices, device_step(): bwd_parts.append((lax.ppermute(send, 'tp', swap_tp), own))  59.2 us
    pallas_call x3, Pallas kernels, expert_fwd(): pl.pallas_call(functools.partial(fwd_kernel, half, padded), grid=(count,)...  48.5 us
    pallas_call x1, Pallas kernels, gather_rows(): pl.pallas_call(gather_kernel, in_specs=[any_spec] * 6, out_specs=[any_spe...  41 us
    ppermute x1, waiting for transfers between devices, device_step(): bwd_parts = [(lax.ppermute(bwd_out[0][0], 'tp', swap_tp), bwd_out[0][1])]  38.4 us
    pallas_call x1, Pallas kernels, shared_grad(): pl.pallas_call(functools.partial(shared_grad_kernel, 256), grid=(width //...  25.6 us
    ppermute x4, waiting for transfers between devices, ep_pieces(): far = lax.ppermute(piece, 'ep', swap_x)  24 us
  transfers between devices with their start and end apart: 29, of which 9 were waited for; matrix products, arithmetic and copies ran while one was open for 23% of the time, Pallas kernels for 32%

profile of v1, /device:TPU:0, one launch (start us, length us, event | category | flops | bytes accessed | tf_op | source)
XLA Modules:
  0.0 553.3 jit_solution(18357634488539766434)
XLA Ops:
  0.7 41.0 %gather_rows.1 = (bf16[8,192,1536]{2,1,0:T(8,128)(2,1)}, s32[8,6,192]{2,1,0:T(8,128)}, bf16[2,192,1536]{2,1,0:T(8,128)(2,1)}, bf16[128,1536]{1,0:T(8,128)(2,1)}, bf16[1536,256]{1,0:T(8,128)(2,1)}) custom-call(bf16[192,1536]{1,0:T(8,128)(2,1)} %x_ref.1, s32[6,192]{1,0:T(8,128)} %bitcast.100, bf16[192,1536]{1,0:T(8,128)(2,1)} %dy_ref.1, ...), custom_call_target="tpu_custom_call" | custom-call | flops 60000002048 | bytes 9437184 | tf_op jit(solution)/shard_map/gather_rows/pallas_call | solution.py:383
  52.7 1.8 constant_dynamic-update-slice_fusion.3
  57.2 7.8 %shard_map.169 = (f32[168,1536]{1,0:T(8,128)S(1)}, f32[168,1536]{1,0:T(8,128)S(1)}) custom-call(bf16[1536,1536]{1,0:T(8,128)(2,1)} %bitcast.84, s32[16,1,1536]{2,1,0:T(1,128)S(1)} %reshape.612.row_ref, bf16[16,1536,256]{2,1,0:T(8,128)(2,1)} %w1_ref.7, bf16[16,1536,256]{2,1,0:T(8,128)(2,1)} %w3_ref.7, bf16[16,256,1536]{2,1,0:T(8,128)(2,1)} %w2_ref.7), custom_call_target="tpu_custom_call" | custom-call | flops 2491416576 | bytes 11501568 | tf_op jit(solution)/shard_map/pallas_call | solution.py:165
  65.0 22.4 %shard_map.170 = (f32[672,1536]{1,0:T(8,128)S(1)}, f32[672,1536]{1,0:T(8,128)}) custom-call(bf16[1536,1536]{1,0:T(8,128)(2,1)} %bitcast.85, s32[16,1,1536]{2,1,0:T(1,128)S(1)} %reshape.612.row_ref, bf16[16,1536,256]{2,1,0:T(8,128)(2,1)} %w1_ref.7, bf16[16,1536,256]{2,1,0:T(8,128)(2,1)} %w3_ref.7, bf16[16,256,1536]{2,1,0:T(8,128)(2,1)} %w2_ref.7), custom_call_target="tpu_custom_call" | custom-call | flops 9965666304 | bytes 31850496 | tf_op jit(solution)/shard_map/pallas_call | solution.py:165
  87.4 2.0 copy-done.6
  89.3 18.3 %shard_map.171 = (f32[504,1536]{1,0:T(8,128)}, f32[504,1536]{1,0:T(8,128)}) custom-call(bf16[1536,1536]{1,0:T(8,128)(2,1)} %bitcast.86, s32[16,1,1536]{2,1,0:T(1,128)S(1)} %reshape.612.row_ref, bf16[16,1536,256]{2,1,0:T(8,128)(2,1)} %w1_ref.7, bf16[16,1536,256]{2,1,0:T(8,128)(2,1)} %w3_ref.7, bf16[16,256,1536]{2,1,0:T(8,128)(2,1)} %w2_ref.7), custom_call_target="tpu_custom_call" | custom-call | flops 7474249728 | bytes 25067520 | tf_op jit(solution)/shard_map/pallas_call | solution.py:165
  109.7 5.6 %fusion.230 = (f32[1536]{0:T(1024)S(1)}, f32[64,1536]{1,0:T(8,128)S(1)}) fusion(bf16[1536,64]{0,1:T(8,128)(2,1)S(1)} %copy-done, bf16[1536,1536]{1,0:T(8,128)(2,1)} %bitcast.87), kind=kOutput, calls=%fused_computation.418 | convolution fusion | flops 302086656 | bytes 5314560 | tf_op jit(solution)/shard_map/de,td->et/dot_general | solution.py:471
  118.1 1.7 reshape.613.row_ref
  121.7 1.8 constant_dynamic-update-slice_fusion.2
  124.9 1.8 constant_dynamic-update-slice_fusion.1
  126.7 2.0 fusion.226
  130.1 16.7 %collective-permute-done.10 = f32[168,1536]{1,0:T(8,128)S(1)} collective-permute-done((f32[168,1536]{1,0:T(8,128)S(1)}, f32[168,1536]{1,0:T(8,128)S(1)}, u32[]{:S(2)}, u32[]{:S(2)}) %collective-permute-start.10) | collective-permute-done | bytes 1032224 | tf_op jit(solution)/shard_map/ppermute | solution.py:465
  148.0 4.3 all-to-all-start
  152.3 1.8 collective-permute-start.4
  155.2 2.5 bitcast_dynamic-update-slice_fusion.1
  157.7 20.9 %collective-permute-done.4 = bf16[1536,256]{1,0:T(8,128)(2,1)} collective-permute-done((bf16[1536,256]{1,0:T(8,128)(2,1)}, bf16[1536,256]{1,0:T(8,128)(2,1)}, u32[]{:S(2)}, u32[]{:S(2)}) %collective-permute-start.4) | collective-permute-done | bytes 786464 | tf_op jit(solution)/shard_map/ppermute | solution.py:433
  178.6 2.0 fusion.227
  182.6 104.4 %expert_bwd.1 = (f32[16,1536,256]{2,1,0:T(8,128)}, f32[16,1536,256]{2,1,0:T(8,128)}, f32[16,256,1536]{2,1,0:T(8,128)}, f32[504,1536]{1,0:T(8,128)}, f32[504,1536...) custom-call(bf16[1536,1536]{1,0:T(8,128)(2,1)} %bitcast.88, ...), custom_call_target="tpu_custom_call" | custom-call | flops 52344913920 | bytes 143130624 | tf_op jit(solution)/shard_map/expert_bwd/pallas_call | solution.py:196
  292.1 1.6 reduce-precision_convert_fusion.7
  302.5 1.7 fusion.78
  304.2 25.6 %shared_grad.1 = (f32[1536,512]{1,0:T(8,128)}, f32[1536,512]{1,0:T(8,128)}, f32[512,1536]{1,0:T(8,128)}) custom-call(bf16[1536,1536]{1,0:T(8,128)(2,1)} %bitcast.89, bf16[1536,1536]{1,0:T(8,128)(2,1)} %bitcast.92, bf16[1536,512]{1,0:T(8,128)(2,1)S(1)} %copy-done.2, bf16[1536,512]{1,0:T(8,128)(2,1)S(1)} %copy-done.4, bf16[512,1536]{1,0:T(8,128)(2,1)S(1)} %copy-done.1), custom_call_target="tpu_custom_call" | custom-call | flops 14495514624 | bytes 23592960 | tf_op jit(solution)/shard_map/shared_grad/pallas_call | solution.py:263
  330.7 1.7 fusion.68
  333.0 4.2 convolution_convert_fusion.1
  337.2 4.7 all-to-all-start.2
  342.8 2.8 convolution_add_fusion.2
  345.7 5.4 convolution_convert_fusion
  351.0 10.9 %all-to-all-done.2 = bf16[4,128,1536]{2,1,0:T(8,128)(2,1)} async-done(((bf16[4,128,1536]{2,1,0:T(8,128)(2,1)}), bf16[4,128,1536]{2,1,0:T(8,128)(2,1)}, u32[]{:S(2)}, u32[]{:S(2)}) %all-to-all-start.2) | async-done | bytes 1572896 | tf_op jit(solution)/shard_map/all_to_all | solution.py:527
  362.0 4.8 all-to-all-start.1
  366.8 2.1 reduce-precision_convert_fusion.5
  369.9 4.1 fusion.28
  373.9 38.4 %collective-permute-done.13 = f32[504,1536]{1,0:T(8,128)} collective-permute-done((f32[504,1536]{1,0:T(8,128)}, f32[504,1536]{1,0:T(8,128)}, u32[]{:S(2)}, u32[]{:S(2)}) %collective-permute-start.13) | collective-permute-done | bytes 3096608 | tf_op jit(solution)/shard_map/ppermute | solution.py:489
  412.3 2.3 add_convert_fusion.2
  418.3 59.2 %collective-permute-done.17 = f32[504,1536]{1,0:T(8,128)} collective-permute-done((f32[504,1536]{1,0:T(8,128)}, f32[504,1536]{1,0:T(8,128)}, u32[]{:S(2)}, u32[]{:S(2)}) %collective-permute-start.17) | collective-permute-done | bytes 3096608 | tf_op jit(solution)/shard_map/ppermute | solution.py:561
  477.5 2.3 add_convert_fusion.1
  484.2 2.4 reduce-precision_convert_fusion.1
  488.4 5.3 fusion.10
  493.7 4.6 fusion.11
  498.3 3.7 fusion.27
  504.0 5.8 %fusion.8 = bf16[192,1536]{1,0:T(8,128)(2,1)} fusion(f32[192,1536]{1,0:T(8,128)S(1)} %copy-done.24, bf16[512,1536]{1,0:T(8,128)(2,1)S(1)} %copy-done.20, f32[576,1536]{1,0:T(8,128)} %fusion.11, f32[576,1536]{1,0:T(8,128)} %fusion.10, f32[576,1536]{1,0:T(8,128)} %fusion.27, f32[192,512]{1,0:T(8,128)S(1)} %copy-done.75, f32[192,512]{1,0:T(8,128)S(1)} %copy-done.74), kind=kOutput, calls=%fused_computation.18 | convolution fusion | flops 306216960 | bytes 14745600 | tf_op jit(solution)/shard_map/dot_general | solution.py:24
  509.9 1.7 fusion.4
  513.4 3.2 collective-permute-done.23
  520.2 3.7 fusion.50
  529.5 9.1 %collective-permute-done.20 = bf16[168,1536]{1,0:T(8,128)(2,1)} collective-permute-done((bf16[168,1536]{1,0:T(8,128)(2,1)}, bf16[168,1536]{1,0:T(8,128)(2,1)}, u32[]{:S(2)}, u32[]{:S(2)}) %collective-permute-start.20) | collective-permute-done | bytes 516128 | tf_op jit(solution)/shard_map/ppermute | solution.py:581
  538.5 2.6 fusion.34
  541.2 2.7 fusion.33
  543.9 2.6 fusion.32
  546.5 4.3 fusion.7
  550.8 2.6 add_convert_fusion.7
  (279 shorter events, 67.1 us)
Async XLA Ops:
  0.6 109.0 %copy-start = (bf16[1536,64]{0,1:T(8,128)(2,1)S(1)}, bf16[1536,64]{0,1:T(8,128)(2,1)}, u32[]{:S(2)}) copy-start(bf16[1536,64]{0,1:T(8,128)(2,1)} %param.12) | copy-start | bytes 589828
  41.6 81.8 %collective-permute-start.8 = (bf16[128,1536]{1,0:T(8,128)(2,1)}, bf16[128,1536]{1,0:T(8,128)(2,1)}, u32[]{:S(2)}, u32[]{:S(2)}) collective-permute-start(bf16[128,1536]{1,0:T(8,128)(2,1)} %get-tuple-element.65), channel_id=1, source_target_pairs={{0,1},{1,0},{2,3},{3,2},{4,5},{5,4},{6,7},{7,6}} | collective-permute-start | bytes 1179656 | tf_op jit(solution)/shard_map/ppermute | solution.py:434
  41.7 79.5 %collective-permute-start.7 = (bf16[128,1536]{1,0:T(8,128)(2,1)}, bf16[128,1536]{1,0:T(8,128)(2,1)}, u32[]{:S(2)}, u32[]{:S(2)}) collective-permute-start(bf16[128,1536]{1,0:T(8,128)(2,1)} %get-tuple-element.65), channel_id=1, source_target_pairs={{0,2},{1,3},{2,0},{3,1},{4,6},{5,7},{6,4},{7,5}} | collective-permute-start | bytes 1179656 | tf_op jit(solution)/shard_map/ppermute | solution.py:433
  42.2 113.0 %collective-permute-start.1 = (bf16[2,192,1536]{2,1,0:T(8,128)(2,1)}, bf16[2,192,1536]{2,1,0:T(8,128)(2,1)}, u32[]{:S(2)}, u32[]{:S(2)}) collective-permute-start(bf16[2,192,1536]{2,1,0:T(8,128)(2,1)} %get-tuple-element.50), channel_id=1, source_target_pairs={{0,1},{1,0},{2,3},{3,2},{4,5},{5,4},{6,7},{7,6}} | collective-permute-start | bytes 3538952 | tf_op jit(solution)/shard_map/ppermute | solution.py:434
  42.4 109.9 %collective-permute-start = (bf16[2,192,1536]{2,1,0:T(8,128)(2,1)}, bf16[2,192,1536]{2,1,0:T(8,128)(2,1)S(1)}, u32[]{:S(2)}, u32[]{:S(2)}) collective-permute-start(bf16[2,192,1536]{2,1,0:T(8,128)(2,1)} %get-tuple-element.50), channel_id=1, source_target_pairs={{0,2},{1,3},{2,0},{3,1},{4,6},{5,7},{6,4},{7,5}} | collective-permute-start | bytes 3538952 | tf_op jit(solution)/shard_map/ppermute | solution.py:433
  43.9 82.8 %collective-permute-start.3 = (bf16[1536,256]{1,0:T(8,128)(2,1)}, bf16[1536,256]{1,0:T(8,128)(2,1)}, u32[]{:S(2)}, u32[]{:S(2)}) collective-permute-start(bf16[1536,256]{1,0:T(8,128)(2,1)} %get-tuple-element.64), channel_id=1, source_target_pairs={{0,4},{4,0},{1,5},{5,1},{2,6},{6,2},{3,7},{7,3}} | collective-permute-start | bytes 2359304 | tf_op jit(solution)/shard_map/ppermute | solution.py:446
  121.1 25.7 %collective-permute-start.10 = (f32[168,1536]{1,0:T(8,128)S(1)}, f32[168,1536]{1,0:T(8,128)S(1)}, u32[]{:S(2)}, u32[]{:S(2)}) collective-permute-start(f32[168,1536]{1,0:T(8,128)S(1)} %get-tuple-element.68), channel_id=1, source_target_pairs={{0,4},{4,0},{1,5},{5,1},{2,6},{6,2},{3,7},{7,3}} | collective-permute-start | bytes 3096584 | tf_op jit(solution)/shard_map/ppermute | solution.py:465
  123.4 23.4 %copy-start.60 = (s32[192]{0:T(256)S(1)}, s32[192]{0:T(256)}, u32[]{:S(2)}) copy-start(s32[192]{0:T(256)} %add_select_fusion.12) | copy-start | bytes 2308
  123.4 222.2 %collective-permute-start.11 = (f32[672,1536]{1,0:T(8,128)}, f32[672,1536]{1,0:T(8,128)}, u32[]{:S(2)}, u32[]{:S(2)}) collective-permute-start(f32[672,1536]{1,0:T(8,128)} %copy-done.6), channel_id=1, source_target_pairs={{0,4},{4,0},{1,5},{5,1},{2,6},{6,2},{3,7},{7,3}} | collective-permute-start | bytes 12386312 | tf_op jit(solution)/shard_map/ppermute | solution.py:465
  126.7 2.0 collective-permute-start.9
  128.7 203.7 %collective-permute-start.12 = (f32[504,1536]{1,0:T(8,128)}, f32[504,1536]{1,0:T(8,128)}, u32[]{:S(2)}, u32[]{:S(2)}) collective-permute-start(f32[504,1536]{1,0:T(8,128)} %get-tuple-element.72), channel_id=1, source_target_pairs={{0,4},{4,0},{1,5},{5,1},{2,6},{6,2},{3,7},{7,3}} | collective-permute-start | bytes 9289736 | tf_op jit(solution)/shard_map/ppermute | solution.py:465
  146.8 33.8 %collective-permute-start.5 = (bf16[1536,256]{1,0:T(8,128)(2,1)}, bf16[1536,256]{1,0:T(8,128)(2,1)S(1)}, u32[]{:S(2)}, u32[]{:S(2)}) collective-permute-start(bf16[1536,256]{1,0:T(8,128)(2,1)} %collective-permute-done.3), channel_id=1, source_target_pairs={{0,1},{1,0},{2,3},{3,2},{4,5},{5,4},{6,7},{7,6}} | collective-permute-start | bytes 2359304 | tf_op jit(solution)/shard_map/ppermute | solution.py:434
  148.0 144.1 %all-to-all-start = ((bf16[4,48,1536]{2,1,0:T(8,128)(2,1)}), bf16[4,48,1536]{2,1,0:T(8,128)(2,1)}, u32[]{:S(2)}, u32[]{:S(2)}) async-start(bf16[4,48,1536]{2,1,0:T(8,128)(2,1)} %bitcast.8), calls=%async_computation | async-start | bytes 1179648 | tf_op jit(solution)/shard_map/all_to_all | solution.py:527
  152.3 26.2 %collective-permute-start.4 = (bf16[1536,256]{1,0:T(8,128)(2,1)}, bf16[1536,256]{1,0:T(8,128)(2,1)}, u32[]{:S(2)}, u32[]{:S(2)}) collective-permute-start(bf16[1536,256]{1,0:T(8,128)(2,1)} %collective-permute-done.3), channel_id=1, source_target_pairs={{0,2},{1,3},{2,0},{3,1},{4,6},{5,7},{6,4},{7,5}} | collective-permute-start | bytes 2359304 | tf_op jit(solution)/shard_map/ppermute | solution.py:433
  155.2 26.3 %collective-permute-start.2 = (bf16[2,192,1536]{2,1,0:T(8,128)(2,1)S(1)}, bf16[2,192,1536]{2,1,0:T(8,128)(2,1)S(1)}, u32[]{:S(2)}, u32[]{:S(2)}) collective-permute-start(bf16[2,192,1536]{2,1,0:T(8,128)(2,1)S(1)} %collective-permute-done), channel_id=1, source_target_pairs={{0,1},{1,0},{2,3},{3,2},{4,5},{5,4},{6,7},{7,6}} | collective-permute-start | bytes 3538952 | tf_op jit(solution)/shard_map/ppermute | solution.py:434
  178.6 117.3 %collective-permute-start.6 = (bf16[1536,256]{1,0:T(8,128)(2,1)}, bf16[1536,256]{1,0:T(8,128)(2,1)}, u32[]{:S(2)}, u32[]{:S(2)}) collective-permute-start(bf16[1536,256]{1,0:T(8,128)(2,1)} %collective-permute-done.4), channel_id=1, source_target_pairs={{0,1},{1,0},{2,3},{3,2},{4,5},{5,4},{6,7},{7,6}} | collective-permute-start | bytes 2359304 | tf_op jit(solution)/shard_map/ppermute | solution.py:434
  182.6 104.4 %copy-start.47 = (s32[192,6]{0,1:T(8,128)S(1)}, s32[192,6]{0,1:T(8,128)}, u32[]{:S(2)}) copy-start(s32[192,6]{0,1:T(8,128)} %param.19) | copy-start | bytes 13828
  182.6 104.7 %copy-start.2 = (bf16[1536,512]{1,0:T(8,128)(2,1)S(1)}, bf16[1536,512]{1,0:T(8,128)(2,1)}, u32[]{:S(2)}) copy-start(bf16[1536,512]{1,0:T(8,128)(2,1)} %wg_ref.3) | copy-start | bytes 4718596
  182.6 104.7 %copy-start.9 = (bf16[192,1536]{1,0:T(8,128)(2,1)S(1)}, bf16[192,1536]{1,0:T(8,128)(2,1)}, u32[]{:S(2)}) copy-start(bf16[192,1536]{1,0:T(8,128)(2,1)} %x_ref.1) | copy-start | bytes 1769476
  288.6 81.3 %collective-permute-start.21 = (f32[336,1536]{1,0:T(8,128)}, f32[336,1536]{1,0:T(8,128)}, u32[]{:S(2)}, u32[]{:S(2)}) collective-permute-start(f32[336,1536]{1,0:T(8,128)} %get-tuple-element.79), channel_id=1, source_target_pairs={{0,4},{4,0},{1,5},{5,1},{2,6},{6,2},{3,7},{7,3}} | collective-permute-start | bytes 6193160 | tf_op jit(solution)/shard_map/ppermute | solution.py:561
  289.1 123.2 %collective-permute-start.13 = (f32[504,1536]{1,0:T(8,128)}, f32[504,1536]{1,0:T(8,128)}, u32[]{:S(2)}, u32[]{:S(2)}) collective-permute-start(f32[504,1536]{1,0:T(8,128)} %get-tuple-element.75), channel_id=1, source_target_pairs={{0,4},{4,0},{1,5},{5,1},{2,6},{6,2},{3,7},{7,3}} | collective-permute-start | bytes 9289736 | tf_op jit(solution)/shard_map/ppermute | solution.py:489
  295.2 7.3 %copy-start.14 = (f32[192,512]{1,0:T(8,128)}, f32[192,512]{1,0:T(8,128)S(1)}, u32[]{:S(2)}) copy-start(f32[192,512]{1,0:T(8,128)S(1)} %fusion.25) | copy-start | bytes 1179652
  295.9 34.8 %copy-start.28 = (f32[192,512]{1,0:T(8,128)}, f32[192,512]{1,0:T(8,128)S(1)}, u32[]{:S(2)}) copy-start(f32[192,512]{1,0:T(8,128)S(1)} %fusion.26) | copy-start | bytes 1179652
  295.9 181.6 %collective-permute-start.17 = (f32[504,1536]{1,0:T(8,128)}, f32[504,1536]{1,0:T(8,128)}, u32[]{:S(2)}, u32[]{:S(2)}) collective-permute-start(f32[504,1536]{1,0:T(8,128)} %get-tuple-element.77), channel_id=1, source_target_pairs={{0,4},{4,0},{1,5},{5,1},{2,6},{6,2},{3,7},{7,3}} | collective-permute-start | bytes 9289736 | tf_op jit(solution)/shard_map/ppermute | solution.py:561
  298.4 32.3 %copy-start.73 = (f32[192,512]{1,0:T(8,128)}, f32[192,512]{1,0:T(8,128)S(1)}, u32[]{:S(2)}) copy-start(f32[192,512]{1,0:T(8,128)S(1)} %fusion.23) | copy-start | bytes 1179652
  333.0 8.8 %copy-start.57 = (s32[512]{0:T(512)S(1)}, s32[512]{0:T(512)}, u32[]{:S(2)}) copy-start(s32[512]{0:T(512)} %fusion.173) | copy-start | bytes 6148
  333.0 8.8 %copy-start.58 = (f32[512]{0:T(512)S(1)}, f32[512]{0:T(512)}, u32[]{:S(2)}) copy-start(f32[512]{0:T(512)} %select_convert_fusion.2) | copy-start | bytes 6148
  337.2 24.8 %all-to-all-start.2 = ((bf16[4,128,1536]{2,1,0:T(8,128)(2,1)}), bf16[4,128,1536]{2,1,0:T(8,128)(2,1)}, u32[]{:S(2)}, u32[]{:S(2)}) async-start(bf16[4,128,1536]{2,1,0:T(8,128)(2,1)} %bitcast.12), calls=%async_computation.2 | async-start | bytes 3145728 | tf_op jit(solution)/shard_map/all_to_all | solution.py:527
  362.0 122.2 %all-to-all-start.1 = ((bf16[4,168,1536]{2,1,0:T(8,128)(2,1)}), bf16[4,168,1536]{2,1,0:T(8,128)(2,1)}, u32[]{:S(2)}, u32[]{:S(2)}) async-start(bf16[4,168,1536]{2,1,0:T(8,128)(2,1)} %bitcast.10), calls=%async_computation.1 | async-start | bytes 4128768 | tf_op jit(solution)/shard_map/all_to_all | solution.py:527
  369.9 42.5 %copy-start.18 = (f32[504,1536]{1,0:T(8,128)S(1)}, f32[504,1536]{1,0:T(8,128)}, u32[]{:S(2)}) copy-start(f32[504,1536]{1,0:T(8,128)} %get-tuple-element.76) | copy-start | bytes 9289732
  415.1 62.4 %copy-start.17 = (f32[504,1536]{1,0:T(8,128)S(1)}, f32[504,1536]{1,0:T(8,128)}, u32[]{:S(2)}) copy-start(f32[504,1536]{1,0:T(8,128)} %get-tuple-element.78) | copy-start | bytes 9289732
  416.1 130.4 %collective-permute-start.14 = (bf16[168,1536]{1,0:T(8,128)(2,1)S(1)}, bf16[168,1536]{1,0:T(8,128)(2,1)}, u32[]{:S(2)}, u32[]{:S(2)}) collective-permute-start(bf16[168,1536]{1,0:T(8,128)(2,1)S(1)} %convolution_convert_fusion.8), channel_id=1, source_target_pairs={{0,2},{1,3},{2,0},{3,1},{4,6},{5,7},{6,4},{7,5}} | collective-permute-start | bytes 1548296 | tf_op jit(solution)/shard_map/ppermute | solution.py:581
  416.7 111.1 %collective-permute-start.15 = (bf16[168,1536]{1,0:T(8,128)(2,1)S(1)}, bf16[168,1536]{1,0:T(8,128)(2,1)}, u32[]{:S(2)}, u32[]{:S(2)}) collective-permute-start(bf16[168,1536]{1,0:T(8,128)(2,1)S(1)} %convolution_convert_fusion.7), channel_id=1, source_target_pairs={{0,1},{1,0},{2,3},{3,2},{4,5},{5,4},{6,7},{7,6}} | collective-permute-start | bytes 1548296 | tf_op jit(solution)/shard_map/ppermute | solution.py:581
  416.7 108.0 %collective-permute-start.16 = (bf16[168,1536]{1,0:T(8,128)(2,1)S(1)}, bf16[168,1536]{1,0:T(8,128)(2,1)}, u32[]{:S(2)}, u32[]{:S(2)}) collective-permute-start(bf16[168,1536]{1,0:T(8,128)(2,1)S(1)} %convolution_convert_fusion.6), channel_id=1, source_target_pairs={{0,3},{1,2},{2,1},{3,0},{4,7},{5,6},{6,5},{7,4}} | collective-permute-start | bytes 1548296 | tf_op jit(solution)/shard_map/ppermute | solution.py:581
  481.1 62.8 %collective-permute-start.18 = (bf16[168,1536]{1,0:T(8,128)(2,1)}, bf16[168,1536]{1,0:T(8,128)(2,1)}, u32[]{:S(2)}, u32[]{:S(2)}) collective-permute-start(bf16[168,1536]{1,0:T(8,128)(2,1)} %convolution_convert_fusion.5), channel_id=1, source_target_pairs={{0,2},{1,3},{2,0},{3,1},{4,6},{5,7},{6,4},{7,5}} | collective-permute-start | bytes 1548296 | tf_op jit(solution)/shard_map/ppermute | solution.py:581
  487.8 23.8 %collective-permute-start.22 = (f32[192,64]{0,1:T(8,128)S(1)}, f32[192,64]{0,1:T(8,128)S(1)}, u32[]{:S(2)}, u32[]{:S(2)}) collective-permute-start(f32[192,64]{0,1:T(8,128)S(1)} %get-tuple-element.90), channel_id=1, source_target_pairs={{0,4},{4,0},{1,5},{5,1},{2,6},{6,2},{3,7},{7,3}} | collective-permute-start | bytes 147464 | tf_op jit(solution)/shard_map/ppermute | solution.py:559
  503.9 5.9 %copy-start.31 = (bf16[1536,128]{1,0:T(8,128)(2,1)S(1)}, bf16[1536,128]{1,0:T(8,128)(2,1)}, u32[]{:S(2)}) copy-start(bf16[1536,128]{1,0:T(8,128)(2,1)} %get-tuple-element.95) | copy-start | bytes 1179652
  503.9 5.9 %copy-start.33 = (bf16[1536,128]{1,0:T(8,128)(2,1)S(1)}, bf16[1536,128]{1,0:T(8,128)(2,1)}, u32[]{:S(2)}) copy-start(bf16[1536,128]{1,0:T(8,128)(2,1)} %get-tuple-element.97) | copy-start | bytes 1179652
  504.0 5.9 %copy-start.35 = (bf16[1536,128]{1,0:T(8,128)(2,1)S(1)}, bf16[1536,128]{1,0:T(8,128)(2,1)}, u32[]{:S(2)}) copy-start(bf16[1536,128]{1,0:T(8,128)(2,1)} %get-tuple-element.99) | copy-start | bytes 1179652
  504.0 5.9 %copy-start.37 = (bf16[1536,128]{1,0:T(8,128)(2,1)S(1)}, bf16[1536,128]{1,0:T(8,128)(2,1)}, u32[]{:S(2)}) copy-start(bf16[1536,128]{1,0:T(8,128)(2,1)} %copy-done.36) | copy-start | bytes 1179652
  504.0 5.9 %copy-start.76 = (f32[192,1536]{1,0:T(8,128)S(1)}, f32[192,1536]{1,0:T(8,128)}, u32[]{:S(2)}) copy-start(f32[192,1536]{1,0:T(8,128)} %fusion.68) | copy-start | bytes 3538948
  511.6 5.0 collective-permute-start.23
  516.6 1.3 collective-permute-start.24
  517.9 1.3 collective-permute-start.25
  519.3 21.9 %collective-permute-start.19 = (bf16[168,1536]{1,0:T(8,128)(2,1)}, bf16[168,1536]{1,0:T(8,128)(2,1)}, u32[]{:S(2)}, u32[]{:S(2)}) collective-permute-start(bf16[168,1536]{1,0:T(8,128)(2,1)} %convolution_convert_fusion.4), channel_id=1, source_target_pairs={{0,1},{1,0},{2,3},{3,2},{4,5},{5,4},{6,7},{7,6}} | collective-permute-start | bytes 1548296 | tf_op jit(solution)/shard_map/ppermute | solution.py:581
  524.7 13.8 %collective-permute-start.20 = (bf16[168,1536]{1,0:T(8,128)(2,1)}, bf16[168,1536]{1,0:T(8,128)(2,1)}, u32[]{:S(2)}, u32[]{:S(2)}) collective-permute-start(bf16[168,1536]{1,0:T(8,128)(2,1)} %convolution_convert_fusion.3), channel_id=1, source_target_pairs={{0,3},{1,2},{2,1},{3,0},{4,7},{5,6},{6,5},{7,4}} | collective-permute-start | bytes 1548296 | tf_op jit(solution)/shard_map/ppermute | solution.py:581
  526.2 12.3 %copy-start.56 = (s32[168]{0:T(256)S(1)}, s32[168]{0:T(256)}, u32[]{:S(2)}) copy-start(s32[168]{0:T(256)} %get-tuple-element.134) | copy-start | bytes 2020
  527.8 13.4 %copy-start.55 = (s32[168]{0:T(256)S(1)}, s32[168]{0:T(256)}, u32[]{:S(2)}) copy-start(s32[168]{0:T(256)} %get-tuple-element.135) | copy-start | bytes 2020
  (58 other events, 182.9 us)

commit v2 on v1

--- a/solution.py
+++ b/solution.py
@@ -489,8 +489,10 @@
         bwd_parts = [(lax.ppermute(bwd_out[0][0], 'tp', swap_tp), bwd_out[0][1])]
 
         own_last = bwd_out[-1][1]
-        x, grad_y, x_all, dy_all, topk_idx, w_router, own_last = lax.optimization_barrier(
-            (x, grad_y, x_all, dy_all, topk_idx, w_router, own_last))
+        own_first = fwd_parts[0][1]
+        x, grad_y, x_all, dy_all, topk_idx, w_router, gu_part, wd_part, own_first, own_last = lax.optimization_barrier(
+            (x, grad_y, x_all, dy_all, topk_idx, w_router, gu_part, wd_part, own_first, own_last))
+        fwd_parts[0] = (fwd_parts[0][0], own_first)
         bwd_out[-1] = (bwd_out[-1][0], own_last)
 
         gu_other = ep_pieces(gu_part)
@@ -561,7 +563,8 @@
             bwd_parts.append((lax.ppermute(send, 'tp', swap_tp), own))
         d_pair = jnp.where(tp_i == 0, jnp.stack([d_logits, d_other]), jnp.stack([d_other, d_logits]))
         d_logits_all = ep_gather(d_pair).reshape(devices * tok, experts)
-        d_router = sum3(dot(x_all, jnp.concatenate(split3(d_logits_all), axis=1), TN), 1)
+        d_router = dot(x_all, jnp.concatenate(split3(d_logits_all), axis=1), TN)
+        d_router = sum3(d_router, 1)
         dx_sum = dx_shared + sum3(dot(jnp.concatenate(split3(d_logits), axis=0), w_router, NT), 0)
 
         def hits_of(grp, start, count):
@@ -581,8 +584,8 @@
                 back = lax.ppermute(back, 'ep', pairs)
                 hits = hits_of(ep_order[1 + k], c * per_chunk, per_chunk)
                 dx_sum = dx_sum + dot(hits, back)
+            dx_sum = lax.optimization_barrier(dx_sum)
         recv, own = bwd_parts[-1]
-        dx_sum = lax.optimization_barrier(dx_sum)
         dx_sum = dx_sum + dot(hits_of(ep_i, 0, local_exp), (recv + own).astype(BF16))
         return y_out, dx_sum.astype(BF16), d_router, d_w_gate, d_w_up, d_w_down, ds_gate, ds_up, ds_down
 

time: 555 us -> 521 us (0.939)
  waiting for transfers between devices: 161 us -> 139 us
  other arithmetic: 20.4 us -> 9.18 us
    ppermute x1, waiting for transfers between devices: 38.4 us -> 62.3 us  [device_step(): bwd_parts = [(lax.ppermute(bwd_out[0][0], 'tp', swap_tp), bwd_out[0][1])]]
    ppermute x4, waiting for transfers between devices: 24 us -> 5.84 us  [ep_pieces(): far = lax.ppermute(piece, 'ep', swap_x)]
    ppermute x3, waiting for transfers between devices: 16.7 us -> 0.01 us  [device_step(): fwd_parts.append((lax.ppermute(send, 'tp', swap_tp), own))]
    all_to_all x3, waiting for transfers between devices: 10.9 us -> 0.01 us  [give_back(): lax.all_to_all(out, 'ep', 0, 0).reshape(ep_size * back_rows(count), model)]
    ppermute x6, waiting for transfers between devices: 9.07 us -> 2.85 us  [device_step(): back = lax.ppermute(back, 'ep', pairs)]
    ppermute x2, waiting for transfers between devices: 59.2 us -> 64.8 us  [device_step(): bwd_parts.append((lax.ppermute(send, 'tp', swap_tp), own))]
    unnamed x157 -> x89, local copies, waits for them, and re-layouts: 11.8 us -> 9.66 us
  transfers between devices with their start and end apart: 29 -> 29, of which waited for: 9 -> 9; matrix products, arithmetic and copies ran while one was open for 23% -> 22% of each run, Pallas kernels for 32% -> 35%
where the time goes in v2:
time: 521 us; the launch traced here: 519 us
  Pallas kernels  221 us (42%)
  waiting for transfers between devices  139 us (27%)
  matrix products  89 us (17%)
  starting transfers between devices  32.8 us (6%)
  local copies, waits for them, and re-layouts  26.8 us (5%)
  other arithmetic  9.18 us (2%)
    pallas_call x1, Pallas kernels, expert_bwd(): pl.pallas_call(functools.partial(bwd_kernel, sizes, per_chunk), grid=(cou...  104 us
    dot_general x44, matrix products, dot(): return lax.dot_general(a, b, dims, preferred_element_type=F32)  84.9 us
    ppermute x2, waiting for transfers between devices, device_step(): bwd_parts.append((lax.ppermute(send, 'tp', swap_tp), own))  64.8 us
    ppermute x1, waiting for transfers between devices, device_step(): bwd_parts = [(lax.ppermute(bwd_out[0][0], 'tp', swap_tp), bwd_out[0][1])]  62.3 us
    pallas_call x3, Pallas kernels, expert_fwd(): pl.pallas_call(functools.partial(fwd_kernel, half, padded), grid=(count,)...  50 us
    pallas_call x1, Pallas kernels, gather_rows(): pl.pallas_call(gather_kernel, in_specs=[any_spec] * 6, out_specs=[any_spe...  41 us
    pallas_call x1, Pallas kernels, shared_grad(): pl.pallas_call(functools.partial(shared_grad_kernel, 256), grid=(width //...  25.6 us
    all_to_all x3, starting transfers between devices, give_back(): lax.all_to_all(out, 'ep', 0, 0).reshape(ep_size * back_rows(count), model)  12.8 us
  transfers between devices with their start and end apart: 29, of which 9 were waited for; matrix products, arithmetic and copies ran while one was open for 22% of the time, Pallas kernels for 35%

profile of v2, /device:TPU:0, one launch (start us, length us, event | category | flops | bytes accessed | tf_op | source)
XLA Modules:
  0.0 519.1 jit_solution(1800526592916032618)
XLA Ops:
  0.7 41.0 %gather_rows.1 = (bf16[8,192,1536]{2,1,0:T(8,128)(2,1)}, s32[8,6,192]{2,1,0:T(8,128)}, bf16[2,192,1536]{2,1,0:T(8,128)(2,1)}, bf16[128,1536]{1,0:T(8,128)(2,1)}, bf16[1536,256]{1,0:T(8,128)(2,1)}) custom-call(bf16[192,1536]{1,0:T(8,128)(2,1)} %x_ref.1, s32[6,192]{1,0:T(8,128)} %bitcast.101, bf16[192,1536]{1,0:T(8,128)(2,1)} %dy_ref.1, ...), custom_call_target="tpu_custom_call" | custom-call | flops 60000002048 | bytes 9437184 | tf_op jit(solution)/shard_map/gather_rows/pallas_call | solution.py:383
  45.2 8.8 %shard_map.169 = (f32[168,1536]{1,0:T(8,128)}, f32[168,1536]{1,0:T(8,128)S(1)}) custom-call(bf16[1536,1536]{1,0:T(8,128)(2,1)} %bitcast.84, s32[16,1,1536]{2,1,0:T(1,128)S(1)} %reshape.612.row_ref, bf16[16,1536,256]{2,1,0:T(8,128)(2,1)} %w1_ref.7, bf16[16,1536,256]{2,1,0:T(8,128)(2,1)} %w3_ref.7, bf16[16,256,1536]{2,1,0:T(8,128)(2,1)} %w2_ref.7), custom_call_target="tpu_custom_call" | custom-call | flops 2491416576 | bytes 11501568 | tf_op jit(solution)/shard_map/pallas_call | solution.py:165
  55.5 22.9 %shard_map.170 = (f32[672,1536]{1,0:T(8,128)}, f32[672,1536]{1,0:T(8,128)}) custom-call(bf16[1536,1536]{1,0:T(8,128)(2,1)} %bitcast.85, s32[16,1,1536]{2,1,0:T(1,128)S(1)} %reshape.612.row_ref, bf16[16,1536,256]{2,1,0:T(8,128)(2,1)} %w1_ref.7, bf16[16,1536,256]{2,1,0:T(8,128)(2,1)} %w3_ref.7, bf16[16,256,1536]{2,1,0:T(8,128)(2,1)} %w2_ref.7), custom_call_target="tpu_custom_call" | custom-call | flops 9965666304 | bytes 31850496 | tf_op jit(solution)/shard_map/pallas_call | solution.py:165
  80.2 18.4 %shard_map.171 = (f32[504,1536]{1,0:T(8,128)}, f32[504,1536]{1,0:T(8,128)}) custom-call(bf16[1536,1536]{1,0:T(8,128)(2,1)} %bitcast.86, s32[16,1,1536]{2,1,0:T(1,128)S(1)} %reshape.612.row_ref, bf16[16,1536,256]{2,1,0:T(8,128)(2,1)} %w1_ref.7, bf16[16,1536,256]{2,1,0:T(8,128)(2,1)} %w3_ref.7, bf16[16,256,1536]{2,1,0:T(8,128)(2,1)} %w2_ref.7), custom_call_target="tpu_custom_call" | custom-call | flops 7474249728 | bytes 25067520 | tf_op jit(solution)/shard_map/pallas_call | solution.py:165
  98.6 3.9 fusion.227
  102.7 2.5 broadcast_in_dim.97
  108.0 2.4 bitcast_dynamic-update-slice_fusion.2
  113.1 104.3 %expert_bwd.1 = (f32[16,1536,256]{2,1,0:T(8,128)}, f32[16,1536,256]{2,1,0:T(8,128)}, f32[16,256,1536]{2,1,0:T(8,128)}, f32[504,1536]{1,0:T(8,128)}, f32[504,1536...) custom-call(bf16[1536,1536]{1,0:T(8,128)(2,1)} %bitcast.88, ...), custom_call_target="tpu_custom_call" | custom-call | flops 52344913920 | bytes 143130624 | tf_op jit(solution)/shard_map/expert_bwd/pallas_call | solution.py:196
  219.3 2.3 fusion.18
  221.6 1.8 constant_dynamic-update-slice_fusion.3
  224.6 2.1 fusion.223
  226.7 2.4 convolution_convert_fusion.2
  229.1 4.5 all-to-all-start
  235.3 1.7 fusion.22
  239.2 1.8 convolution_add_fusion.2
  241.9 25.6 %shared_grad.1 = (f32[1536,512]{1,0:T(8,128)}, f32[1536,512]{1,0:T(8,128)}, f32[512,1536]{1,0:T(8,128)}) custom-call(bf16[1536,1536]{1,0:T(8,128)(2,1)} %bitcast.89, bf16[1536,1536]{1,0:T(8,128)(2,1)} %bitcast.6.dy_ref, bf16[1536,512]{1,0:T(8,128)(2,1)S(1)} %copy-done.4, bf16[1536,512]{1,0:T(8,128)(2,1)S(1)} %copy-done.2, bf16[512,1536]{1,0:T(8,128)(2,1)S(1)} %copy-done.1), custom_call_target="tpu_custom_call" | custom-call | flops 14495514624 | bytes 23592960 | tf_op jit(solution)/shard_map/shared_grad/pallas_call | solution.py:263
  268.6 1.8 collective-permute-start.4
  270.4 1.9 constant_dynamic-update-slice_fusion.2
  272.4 2.0 collective-permute-start.21
  274.4 1.8 constant_dynamic-update-slice_fusion.1
  278.7 4.1 convolution_convert_fusion.1
  282.8 3.6 all-to-all-start.2
  286.4 2.6 collective-permute-done.4
  291.8 2.0 collective-permute-start.17
  295.0 2.2 fusion.23
  298.5 1.8 fusion.65
  302.6 5.3 %convolution_convert_fusion = bf16[672,1536]{1,0:T(8,128)(2,1)} fusion(f32[672,1536]{1,0:T(8,128)} %collective-permute-done.11, f32[672,1536]{1,0:T(8,128)S(1)} %copy-done.35, s32[672]{0:T(1024)S(1)} %add_select_fusion.6), kind=kOutput, calls=%fused_computation.1 | convolution fusion | flops 1390814208 | bytes 10324608 | tf_op jit(solution)/shard_map/dot_general | solution.py:24
  307.9 4.8 all-to-all-start.1
  314.4 6.1 %collective-permute-done.21 = f32[336,1536]{1,0:T(8,128)} collective-permute-done((f32[336,1536]{1,0:T(8,128)}, f32[336,1536]{1,0:T(8,128)}, u32[]{:S(2)}, u32[]{:S(2)}) %collective-permute-start.21) | collective-permute-done | bytes 2064416 | tf_op jit(solution)/shard_map/ppermute | solution.py:563
  320.5 4.0 fusion.25
  324.5 62.3 %collective-permute-done.13 = f32[504,1536]{1,0:T(8,128)} collective-permute-done((f32[504,1536]{1,0:T(8,128)}, f32[504,1536]{1,0:T(8,128)}, u32[]{:S(2)}, u32[]{:S(2)}) %collective-permute-start.13) | collective-permute-done | bytes 3096608 | tf_op jit(solution)/shard_map/ppermute | solution.py:489
  386.9 2.3 add_convert_fusion.2
  391.7 1.9 collective-permute-start.16
  393.6 58.8 %collective-permute-done.17 = f32[504,1536]{1,0:T(8,128)} collective-permute-done((f32[504,1536]{1,0:T(8,128)}, f32[504,1536]{1,0:T(8,128)}, u32[]{:S(2)}, u32[]{:S(2)}) %collective-permute-start.17) | collective-permute-done | bytes 3096608 | tf_op jit(solution)/shard_map/ppermute | solution.py:563
  452.3 2.3 add_convert_fusion.1
  459.1 2.4 reduce-precision_convert_fusion.1
  462.7 1.8 collective-permute-start.22
  464.5 5.5 %fusion.7 = f32[576,1536]{1,0:T(8,128)} fusion(bf16[672,1536]{1,0:T(8,128)(2,1)} %bitcast.11, pred[192,672]{1,0:T(32,128)(4,1)} %convolution_compare_fusion, s32[672]{0:T(1024)S(1)} %add_select_fusion.7, bf16[192,64]{0,1:T(8,128)(2,1)S(1)} %get-tuple-element.122, bf16[192,64]{0,1:T(8,128)(2,1)S(1)} %get-tuple-element.121, ...), kind=kOutput, calls=%fused_computation.30 | convolution fusion | flops 1240442880 | bytes 5808768 | tf_op jit(solution)/shard_map/dot_general | solution.py:24
  470.0 3.1 fusion.8
  473.2 3.8 fusion.24
  478.4 6.3 %fusion.5 = bf16[192,1536]{1,0:T(8,128)(2,1)} fusion(f32[192,1536]{1,0:T(8,128)S(1)} %copy-done.18, bf16[512,1536]{1,0:T(8,128)(2,1)} %constant_dynamic-update-slice_fusion, f32[576,1536]{1,0:T(8,128)} %fusion.8, f32[576,1536]{1,0:T(8,128)} %fusion.7, f32[576,1536]{1,0:T(8,128)} %fusion.24, f32[192,512]{1,0:T(8,128)S(1)} %copy-done.41, ...), kind=kOutput, calls=%fused_computation.15 | convolution fusion | flops 306216960 | bytes 14745600 | tf_op jit(solution)/shard_map/dot_general | solution.py:24
  484.8 1.7 fusion.4
  488.3 3.3 collective-permute-done.23
  495.1 3.7 fusion.47
  504.3 3.1 fusion.1
  510.6 2.8 collective-permute-done.20
  513.5 3.1 add_add_fusion
  516.5 2.6 add_convert_fusion.7
  (212 shorter events, 56.8 us)
Async XLA Ops:
  0.6 97.9 %copy-start = (bf16[1536,64]{0,1:T(8,128)(2,1)S(1)}, bf16[1536,64]{0,1:T(8,128)(2,1)}, u32[]{:S(2)}) copy-start(bf16[1536,64]{0,1:T(8,128)(2,1)} %param.12) | copy-start | bytes 589828
  41.6 68.7 %collective-permute-start.1 = (bf16[2,192,1536]{2,1,0:T(8,128)(2,1)}, bf16[2,192,1536]{2,1,0:T(8,128)(2,1)S(1)}, u32[]{:S(2)}, u32[]{:S(2)}) collective-permute-start(bf16[2,192,1536]{2,1,0:T(8,128)(2,1)} %get-tuple-element.53), channel_id=1, source_target_pairs={{0,1},{1,0},{2,3},{3,2},{4,5},{5,4},{6,7},{7,6}} | collective-permute-start | bytes 3538952 | tf_op jit(solution)/shard_map/ppermute | solution.py:434
  41.7 64.7 %collective-permute-start = (bf16[2,192,1536]{2,1,0:T(8,128)(2,1)}, bf16[2,192,1536]{2,1,0:T(8,128)(2,1)}, u32[]{:S(2)}, u32[]{:S(2)}) collective-permute-start(bf16[2,192,1536]{2,1,0:T(8,128)(2,1)} %get-tuple-element.53), channel_id=1, source_target_pairs={{0,2},{1,3},{2,0},{3,1},{4,6},{5,7},{6,4},{7,5}} | collective-permute-start | bytes 3538952 | tf_op jit(solution)/shard_map/ppermute | solution.py:433
  42.2 175.3 %collective-permute-start.3 = (bf16[1536,256]{1,0:T(8,128)(2,1)}, bf16[1536,256]{1,0:T(8,128)(2,1)}, u32[]{:S(2)}, u32[]{:S(2)}) collective-permute-start(bf16[1536,256]{1,0:T(8,128)(2,1)} %get-tuple-element.62), channel_id=1, source_target_pairs={{0,4},{4,0},{1,5},{5,1},{2,6},{6,2},{3,7},{7,3}} | collective-permute-start | bytes 2359304 | tf_op jit(solution)/shard_map/ppermute | solution.py:446
  54.9 171.7 %collective-permute-start.10 = (f32[168,1536]{1,0:T(8,128)}, f32[168,1536]{1,0:T(8,128)}, u32[]{:S(2)}, u32[]{:S(2)}) collective-permute-start(f32[168,1536]{1,0:T(8,128)} %get-tuple-element.74), channel_id=1, source_target_pairs={{0,4},{4,0},{1,5},{5,1},{2,6},{6,2},{3,7},{7,3}} | collective-permute-start | bytes 3096584 | tf_op jit(solution)/shard_map/ppermute | solution.py:465
  78.4 223.2 %collective-permute-start.11 = (f32[672,1536]{1,0:T(8,128)}, f32[672,1536]{1,0:T(8,128)}, u32[]{:S(2)}, u32[]{:S(2)}) collective-permute-start(f32[672,1536]{1,0:T(8,128)} %get-tuple-element.76), channel_id=1, source_target_pairs={{0,4},{4,0},{1,5},{5,1},{2,6},{6,2},{3,7},{7,3}} | collective-permute-start | bytes 12386312 | tf_op jit(solution)/shard_map/ppermute | solution.py:465
  106.4 5.7 %collective-permute-start.2 = (bf16[2,192,1536]{2,1,0:T(8,128)(2,1)}, bf16[2,192,1536]{2,1,0:T(8,128)(2,1)S(1)}, u32[]{:S(2)}, u32[]{:S(2)}) collective-permute-start(bf16[2,192,1536]{2,1,0:T(8,128)(2,1)} %collective-permute-done), channel_id=1, source_target_pairs={{0,1},{1,0},{2,3},{3,2},{4,5},{5,4},{6,7},{7,6}} | collective-permute-start | bytes 3538952 | tf_op jit(solution)/shard_map/ppermute | solution.py:434
  110.3 168.3 %collective-permute-start.12 = (f32[504,1536]{1,0:T(8,128)}, f32[504,1536]{1,0:T(8,128)}, u32[]{:S(2)}, u32[]{:S(2)}) collective-permute-start(f32[504,1536]{1,0:T(8,128)} %get-tuple-element.78), channel_id=1, source_target_pairs={{0,4},{4,0},{1,5},{5,1},{2,6},{6,2},{3,7},{7,3}} | collective-permute-start | bytes 9289736 | tf_op jit(solution)/shard_map/ppermute | solution.py:465
  113.1 106.1 %copy-start.3 = (bf16[1536,512]{1,0:T(8,128)(2,1)S(1)}, bf16[1536,512]{1,0:T(8,128)(2,1)}, u32[]{:S(2)}) copy-start(bf16[1536,512]{1,0:T(8,128)(2,1)} %wg_ref.3) | copy-start | bytes 4718596
  217.5 5.8 %copy-start.2 = (bf16[1536,512]{1,0:T(8,128)(2,1)S(1)}, bf16[1536,512]{1,0:T(8,128)(2,1)}, u32[]{:S(2)}) copy-start(bf16[1536,512]{1,0:T(8,128)(2,1)} %wu_ref.3) | copy-start | bytes 4718596
  217.5 5.8 %copy-start.8 = (bf16[192,1536]{1,0:T(8,128)(2,1)S(1)}, bf16[192,1536]{1,0:T(8,128)(2,1)}, u32[]{:S(2)}) copy-start(bf16[192,1536]{1,0:T(8,128)(2,1)} %x_ref.1) | copy-start | bytes 1769476
  217.5 54.8 %collective-permute-start.8 = (bf16[128,1536]{1,0:T(8,128)(2,1)}, bf16[128,1536]{1,0:T(8,128)(2,1)}, u32[]{:S(2)}, u32[]{:S(2)}) collective-permute-start(bf16[128,1536]{1,0:T(8,128)(2,1)} %get-tuple-element.71), channel_id=1, source_target_pairs={{0,1},{1,0},{2,3},{3,2},{4,5},{5,4},{6,7},{7,6}} | collective-permute-start | bytes 1179656 | tf_op jit(solution)/shard_map/ppermute | solution.py:434
  217.7 50.9 %collective-permute-start.7 = (bf16[128,1536]{1,0:T(8,128)(2,1)}, bf16[128,1536]{1,0:T(8,128)(2,1)}, u32[]{:S(2)}, u32[]{:S(2)}) collective-permute-start(bf16[128,1536]{1,0:T(8,128)(2,1)} %get-tuple-element.71), channel_id=1, source_target_pairs={{0,2},{1,3},{2,0},{3,1},{4,6},{5,7},{6,4},{7,5}} | collective-permute-start | bytes 1179656 | tf_op jit(solution)/shard_map/ppermute | solution.py:433
  226.6 6.9 %copy-start.34 = (s32[192,6]{0,1:T(8,128)S(1)}, s32[192,6]{0,1:T(8,128)}, u32[]{:S(2)}) copy-start(s32[192,6]{0,1:T(8,128)} %param.19) | copy-start | bytes 13828
  226.6 65.1 %collective-permute-start.5 = (bf16[1536,256]{1,0:T(8,128)(2,1)}, bf16[1536,256]{1,0:T(8,128)(2,1)}, u32[]{:S(2)}, u32[]{:S(2)}) collective-permute-start(bf16[1536,256]{1,0:T(8,128)(2,1)} %collective-permute-done.3), channel_id=1, source_target_pairs={{0,1},{1,0},{2,3},{3,2},{4,5},{5,4},{6,7},{7,6}} | collective-permute-start | bytes 2359304 | tf_op jit(solution)/shard_map/ppermute | solution.py:434
  229.1 6.2 %copy-start.1 = (bf16[512,1536]{1,0:T(8,128)(2,1)S(1)}, bf16[512,1536]{1,0:T(8,128)(2,1)}, u32[]{:S(2)}) copy-start(bf16[512,1536]{1,0:T(8,128)(2,1)} %wd_ref.3) | copy-start | bytes 4718596
  229.1 47.1 %all-to-all-start = ((bf16[4,48,1536]{2,1,0:T(8,128)(2,1)}), bf16[4,48,1536]{2,1,0:T(8,128)(2,1)}, u32[]{:S(2)}, u32[]{:S(2)}) async-start(bf16[4,48,1536]{2,1,0:T(8,128)(2,1)} %bitcast.91), calls=%async_computation | async-start | bytes 1179648 | tf_op jit(solution)/shard_map/all_to_all | solution.py:529
  268.6 20.3 %collective-permute-start.4 = (bf16[1536,256]{1,0:T(8,128)(2,1)}, bf16[1536,256]{1,0:T(8,128)(2,1)}, u32[]{:S(2)}, u32[]{:S(2)}) collective-permute-start(bf16[1536,256]{1,0:T(8,128)(2,1)} %collective-permute-done.3), channel_id=1, source_target_pairs={{0,2},{1,3},{2,0},{3,1},{4,6},{5,7},{6,4},{7,5}} | collective-permute-start | bytes 2359304 | tf_op jit(solution)/shard_map/ppermute | solution.py:433
  270.4 8.3 %copy-start.13 = (f32[504,1536]{1,0:T(8,128)S(1)}, f32[504,1536]{1,0:T(8,128)}, u32[]{:S(2)}) copy-start(f32[504,1536]{1,0:T(8,128)} %get-tuple-element.79) | copy-start | bytes 9289732
  272.4 48.1 %collective-permute-start.21 = (f32[336,1536]{1,0:T(8,128)}, f32[336,1536]{1,0:T(8,128)}, u32[]{:S(2)}, u32[]{:S(2)}) collective-permute-start(f32[336,1536]{1,0:T(8,128)} %get-tuple-element.85), channel_id=1, source_target_pairs={{0,4},{4,0},{1,5},{5,1},{2,6},{6,2},{3,7},{7,3}} | collective-permute-start | bytes 6193160 | tf_op jit(solution)/shard_map/ppermute | solution.py:563
  278.7 108.2 %collective-permute-start.13 = (f32[504,1536]{1,0:T(8,128)}, f32[504,1536]{1,0:T(8,128)}, u32[]{:S(2)}, u32[]{:S(2)}) collective-permute-start(f32[504,1536]{1,0:T(8,128)} %get-tuple-element.81), channel_id=1, source_target_pairs={{0,4},{4,0},{1,5},{5,1},{2,6},{6,2},{3,7},{7,3}} | collective-permute-start | bytes 9289736 | tf_op jit(solution)/shard_map/ppermute | solution.py:489
  282.8 25.1 %all-to-all-start.2 = ((bf16[4,128,1536]{2,1,0:T(8,128)(2,1)}), bf16[4,128,1536]{2,1,0:T(8,128)(2,1)S(1)}, u32[]{:S(2)}, u32[]{:S(2)}) async-start(bf16[4,128,1536]{2,1,0:T(8,128)(2,1)} %bitcast.12), calls=%async_computation.2 | async-start | bytes 3145728 | tf_op jit(solution)/shard_map/all_to_all | solution.py:529
  288.9 1.9 collective-permute-start.9
  290.1 7.2 %copy-start.25 = (bf16[1536,128]{1,0:T(8,128)(2,1)}, bf16[1536,128]{1,0:T(8,128)(2,1)S(1)}, u32[]{:S(2)}) copy-start(bf16[1536,128]{1,0:T(8,128)(2,1)S(1)} %get-tuple-element.103) | copy-start | bytes 1179652
  290.9 6.4 %collective-permute-start.6 = (bf16[1536,256]{1,0:T(8,128)(2,1)}, bf16[1536,256]{1,0:T(8,128)(2,1)S(1)}, u32[]{:S(2)}, u32[]{:S(2)}) collective-permute-start(bf16[1536,256]{1,0:T(8,128)(2,1)} %collective-permute-done.4), channel_id=1, source_target_pairs={{0,1},{1,0},{2,3},{3,2},{4,5},{5,4},{6,7},{7,6}} | collective-permute-start | bytes 2359304 | tf_op jit(solution)/shard_map/ppermute | solution.py:434
  291.8 160.6 %collective-permute-start.17 = (f32[504,1536]{1,0:T(8,128)}, f32[504,1536]{1,0:T(8,128)}, u32[]{:S(2)}, u32[]{:S(2)}) collective-permute-start(f32[504,1536]{1,0:T(8,128)} %get-tuple-element.83), channel_id=1, source_target_pairs={{0,4},{4,0},{1,5},{5,1},{2,6},{6,2},{3,7},{7,3}} | collective-permute-start | bytes 9289736 | tf_op jit(solution)/shard_map/ppermute | solution.py:563
  307.9 151.2 %all-to-all-start.1 = ((bf16[4,168,1536]{2,1,0:T(8,128)(2,1)}), bf16[4,168,1536]{2,1,0:T(8,128)(2,1)}, u32[]{:S(2)}, u32[]{:S(2)}) async-start(bf16[4,168,1536]{2,1,0:T(8,128)(2,1)} %bitcast.10), calls=%async_computation.1 | async-start | bytes 4128768 | tf_op jit(solution)/shard_map/all_to_all | solution.py:529
  320.5 66.4 %copy-start.12 = (f32[504,1536]{1,0:T(8,128)S(1)}, f32[504,1536]{1,0:T(8,128)}, u32[]{:S(2)}) copy-start(f32[504,1536]{1,0:T(8,128)} %get-tuple-element.82) | copy-start | bytes 9289732
  390.5 61.9 %copy-start.11 = (f32[504,1536]{1,0:T(8,128)S(1)}, f32[504,1536]{1,0:T(8,128)}, u32[]{:S(2)}) copy-start(f32[504,1536]{1,0:T(8,128)} %get-tuple-element.84) | copy-start | bytes 9289732
  391.4 112.9 %collective-permute-start.14 = (bf16[168,1536]{1,0:T(8,128)(2,1)S(1)}, bf16[168,1536]{1,0:T(8,128)(2,1)}, u32[]{:S(2)}, u32[]{:S(2)}) collective-permute-start(bf16[168,1536]{1,0:T(8,128)(2,1)S(1)} %convolution_convert_fusion.8), channel_id=1, source_target_pairs={{0,2},{1,3},{2,0},{3,1},{4,6},{5,7},{6,4},{7,5}} | collective-permute-start | bytes 1548296 | tf_op jit(solution)/shard_map/ppermute | solution.py:584
  391.7 111.0 %collective-permute-start.15 = (bf16[168,1536]{1,0:T(8,128)(2,1)S(1)}, bf16[168,1536]{1,0:T(8,128)(2,1)}, u32[]{:S(2)}, u32[]{:S(2)}) collective-permute-start(bf16[168,1536]{1,0:T(8,128)(2,1)S(1)} %convolution_convert_fusion.7), channel_id=1, source_target_pairs={{0,1},{1,0},{2,3},{3,2},{4,5},{5,4},{6,7},{7,6}} | collective-permute-start | bytes 1548296 | tf_op jit(solution)/shard_map/ppermute | solution.py:584
  391.7 108.0 %collective-permute-start.16 = (bf16[168,1536]{1,0:T(8,128)(2,1)}, bf16[168,1536]{1,0:T(8,128)(2,1)}, u32[]{:S(2)}, u32[]{:S(2)}) collective-permute-start(bf16[168,1536]{1,0:T(8,128)(2,1)} %convolution_convert_fusion.6), channel_id=1, source_target_pairs={{0,3},{1,2},{2,1},{3,0},{4,7},{5,6},{6,5},{7,4}} | collective-permute-start | bytes 1548296 | tf_op jit(solution)/shard_map/ppermute | solution.py:584
  455.9 53.1 %collective-permute-start.18 = (bf16[168,1536]{1,0:T(8,128)(2,1)}, bf16[168,1536]{1,0:T(8,128)(2,1)}, u32[]{:S(2)}, u32[]{:S(2)}) collective-permute-start(bf16[168,1536]{1,0:T(8,128)(2,1)} %convolution_convert_fusion.5), channel_id=1, source_target_pairs={{0,2},{1,3},{2,0},{3,1},{4,6},{5,7},{6,4},{7,5}} | collective-permute-start | bytes 1548296 | tf_op jit(solution)/shard_map/ppermute | solution.py:584
  462.7 23.8 %collective-permute-start.22 = (f32[192,64]{0,1:T(8,128)S(1)}, f32[192,64]{0,1:T(8,128)S(1)}, u32[]{:S(2)}, u32[]{:S(2)}) collective-permute-start(f32[192,64]{0,1:T(8,128)S(1)} %get-tuple-element.96), channel_id=1, source_target_pairs={{0,4},{4,0},{1,5},{5,1},{2,6},{6,2},{3,7},{7,3}} | collective-permute-start | bytes 147464 | tf_op jit(solution)/shard_map/ppermute | solution.py:561
  464.5 5.6 %copy-start.17 = (bf16[4,128,1536]{2,1,0:T(8,128)(2,1)S(1)}, bf16[4,128,1536]{2,1,0:T(8,128)(2,1)}, u32[]{:S(2)}) copy-start(bf16[4,128,1536]{2,1,0:T(8,128)(2,1)} %copy-done.16) | copy-start | bytes 4718596
  464.5 5.6 %copy-start.37 = (pred[192,512]{1,0:T(32,128)(4,1)S(1)}, pred[192,512]{1,0:T(32,128)(4,1)}, u32[]{:S(2)}) copy-start(pred[192,512]{1,0:T(32,128)(4,1)} %convolution_compare_fusion.1) | copy-start | bytes 294916
  478.4 6.3 %copy-start.20 = (f32[192,1536]{1,0:T(8,128)S(1)}, f32[192,1536]{1,0:T(8,128)}, u32[]{:S(2)}) copy-start(f32[192,1536]{1,0:T(8,128)} %convolution_add_fusion.2) | copy-start | bytes 3538948
  478.4 6.3 %copy-start.22 = (f32[192,512]{1,0:T(8,128)S(1)}, f32[192,512]{1,0:T(8,128)}, u32[]{:S(2)}) copy-start(f32[192,512]{1,0:T(8,128)} %copy-done.21) | copy-start | bytes 1179652
  478.4 6.3 %copy-start.24 = (bf16[1536,128]{1,0:T(8,128)(2,1)S(1)}, bf16[1536,128]{1,0:T(8,128)(2,1)}, u32[]{:S(2)}) copy-start(bf16[1536,128]{1,0:T(8,128)(2,1)} %get-tuple-element.101) | copy-start | bytes 1179652
  478.4 6.3 %copy-start.26 = (bf16[1536,128]{1,0:T(8,128)(2,1)S(1)}, bf16[1536,128]{1,0:T(8,128)(2,1)}, u32[]{:S(2)}) copy-start(bf16[1536,128]{1,0:T(8,128)(2,1)} %copy-done.25) | copy-start | bytes 1179652
  478.4 6.3 %copy-start.28 = (bf16[1536,128]{1,0:T(8,128)(2,1)S(1)}, bf16[1536,128]{1,0:T(8,128)(2,1)}, u32[]{:S(2)}) copy-start(bf16[1536,128]{1,0:T(8,128)(2,1)} %copy-done.27) | copy-start | bytes 1179652
  478.4 6.3 %copy-start.30 = (bf16[1536,128]{1,0:T(8,128)(2,1)S(1)}, bf16[1536,128]{1,0:T(8,128)(2,1)}, u32[]{:S(2)}) copy-start(bf16[1536,128]{1,0:T(8,128)(2,1)} %copy-done.29) | copy-start | bytes 1179652
  478.4 6.3 %copy-start.42 = (f32[192,1536]{1,0:T(8,128)S(1)}, f32[192,1536]{1,0:T(8,128)}, u32[]{:S(2)}) copy-start(f32[192,1536]{1,0:T(8,128)} %fusion.65) | copy-start | bytes 3538948
  486.5 5.0 collective-permute-start.23
  491.5 1.3 collective-permute-start.24
  492.9 1.3 collective-permute-start.25
  494.2 13.1 %collective-permute-start.19 = (bf16[168,1536]{1,0:T(8,128)(2,1)}, bf16[168,1536]{1,0:T(8,128)(2,1)}, u32[]{:S(2)}, u32[]{:S(2)}) collective-permute-start(bf16[168,1536]{1,0:T(8,128)(2,1)} %convolution_convert_fusion.4), channel_id=1, source_target_pairs={{0,1},{1,0},{2,3},{3,2},{4,5},{5,4},{6,7},{7,6}} | collective-permute-start | bytes 1548296 | tf_op jit(solution)/shard_map/ppermute | solution.py:584
  499.6 13.8 %collective-permute-start.20 = (bf16[168,1536]{1,0:T(8,128)(2,1)}, bf16[168,1536]{1,0:T(8,128)(2,1)}, u32[]{:S(2)}, u32[]{:S(2)}) collective-permute-start(bf16[168,1536]{1,0:T(8,128)(2,1)} %convolution_convert_fusion.3), channel_id=1, source_target_pairs={{0,3},{1,2},{2,1},{3,0},{4,7},{5,6},{6,5},{7,4}} | collective-permute-start | bytes 1548296 | tf_op jit(solution)/shard_map/ppermute | solution.py:584
  (24 other events, 56.1 us)

commit v3 on v2

--- a/solution.py
+++ b/solution.py
@@ -526,7 +526,8 @@
             perm = (old[:, None] == jnp.arange(count * half, dtype=jnp.int32)[None, :]).astype(BF16)
             out = dot(perm, rows).astype(BF16)
             out = out.reshape(ep_size, back_rows(count), model)
-            return lax.all_to_all(out, 'ep', 0, 0).reshape(ep_size * back_rows(count), model)
+            out = lax.all_to_all(out, 'ep', 0, 0)
+            return out.reshape(ep_size * back_rows(count), model)
 
         hit_own = jnp.any(topk_idx[:, None, :] == jnp.arange(experts, dtype=jnp.int32)[None, :, None], axis=2)
         rank_own = dot(lower, hit_own.astype(BF16))
@@ -548,7 +549,8 @@
             table, rank = expand(start, count)
             hits = dot(want, table) == rank
             gates = jnp.where(jnp.concatenate([hits] * 3, axis=0), dot(prob_parts, table), 0.0).astype(BF16)
-            routed = routed + GATE_SCALE * sum3(dot(gates, back), 0)
+            mixed = dot(gates, back)
+            routed = routed + GATE_SCALE * sum3(mixed, 0)
             score = jnp.where(hits, dot(grad_y, back, NT), 0.0)
             part = dot(jnp.concatenate(split3(score), axis=0), table, NT)
             d_scores = d_scores + sum3(part, 0)

time: 521 us -> 521 us (level)
  no operation moved by 1% of the time
where the time goes in v3:
time: 521 us; the launch traced here: 519 us
  Pallas kernels  221 us (42%)
  waiting for transfers between devices  139 us (27%)
  matrix products  89 us (17%)
  starting transfers between devices  32.8 us (6%)
  local copies, waits for them, and re-layouts  26.8 us (5%)
  other arithmetic  9.18 us (2%)
    pallas_call x1, Pallas kernels, expert_bwd(): pl.pallas_call(functools.partial(bwd_kernel, sizes, per_chunk), grid=(cou...  104 us
    dot_general x44, matrix products, dot(): return lax.dot_general(a, b, dims, preferred_element_type=F32)  84.9 us
    ppermute x2, waiting for transfers between devices, device_step(): bwd_parts.append((lax.ppermute(send, 'tp', swap_tp), own))  64.8 us
    ppermute x1, waiting for transfers between devices, device_step(): bwd_parts = [(lax.ppermute(bwd_out[0][0], 'tp', swap_tp), bwd_out[0][1])]  62.3 us
    pallas_call x3, Pallas kernels, expert_fwd(): pl.pallas_call(functools.partial(fwd_kernel, half, padded), grid=(count,)...  50 us
    pallas_call x1, Pallas kernels, gather_rows(): pl.pallas_call(gather_kernel, in_specs=[any_spec] * 6, out_specs=[any_spe...  41 us
    pallas_call x1, Pallas kernels, shared_grad(): pl.pallas_call(functools.partial(shared_grad_kernel, 256), grid=(width //...  25.6 us
    all_to_all x3, starting transfers between devices, give_back(): out = lax.all_to_all(out, 'ep', 0, 0)  12.8 us
  transfers between devices with their start and end apart: 29, of which 9 were waited for; matrix products, arithmetic and copies ran while one was open for 22% of the time, Pallas kernels for 35%

profile of v3, /device:TPU:0, one launch (start us, length us, event | category | flops | bytes accessed | tf_op | source)
XLA Modules:
  0.0 519.1 jit_solution(1800526592916032618)
XLA Ops:
  0.7 41.0 %gather_rows.1 = (bf16[8,192,1536]{2,1,0:T(8,128)(2,1)}, s32[8,6,192]{2,1,0:T(8,128)}, bf16[2,192,1536]{2,1,0:T(8,128)(2,1)}, bf16[128,1536]{1,0:T(8,128)(2,1)}, bf16[1536,256]{1,0:T(8,128)(2,1)}) custom-call(bf16[192,1536]{1,0:T(8,128)(2,1)} %x_ref.1, s32[6,192]{1,0:T(8,128)} %bitcast.101, bf16[192,1536]{1,0:T(8,128)(2,1)} %dy_ref.1, ...), custom_call_target="tpu_custom_call" | custom-call | flops 60000002048 | bytes 9437184 | tf_op jit(solution)/shard_map/gather_rows/pallas_call | solution.py:383
  45.2 8.8 %shard_map.169 = (f32[168,1536]{1,0:T(8,128)}, f32[168,1536]{1,0:T(8,128)S(1)}) custom-call(bf16[1536,1536]{1,0:T(8,128)(2,1)} %bitcast.84, s32[16,1,1536]{2,1,0:T(1,128)S(1)} %reshape.612.row_ref, bf16[16,1536,256]{2,1,0:T(8,128)(2,1)} %w1_ref.7, bf16[16,1536,256]{2,1,0:T(8,128)(2,1)} %w3_ref.7, bf16[16,256,1536]{2,1,0:T(8,128)(2,1)} %w2_ref.7), custom_call_target="tpu_custom_call" | custom-call | flops 2491416576 | bytes 11501568 | tf_op jit(solution)/shard_map/pallas_call | solution.py:165
  55.5 22.9 %shard_map.170 = (f32[672,1536]{1,0:T(8,128)}, f32[672,1536]{1,0:T(8,128)}) custom-call(bf16[1536,1536]{1,0:T(8,128)(2,1)} %bitcast.85, s32[16,1,1536]{2,1,0:T(1,128)S(1)} %reshape.612.row_ref, bf16[16,1536,256]{2,1,0:T(8,128)(2,1)} %w1_ref.7, bf16[16,1536,256]{2,1,0:T(8,128)(2,1)} %w3_ref.7, bf16[16,256,1536]{2,1,0:T(8,128)(2,1)} %w2_ref.7), custom_call_target="tpu_custom_call" | custom-call | flops 9965666304 | bytes 31850496 | tf_op jit(solution)/shard_map/pallas_call | solution.py:165
  80.2 18.4 %shard_map.171 = (f32[504,1536]{1,0:T(8,128)}, f32[504,1536]{1,0:T(8,128)}) custom-call(bf16[1536,1536]{1,0:T(8,128)(2,1)} %bitcast.86, s32[16,1,1536]{2,1,0:T(1,128)S(1)} %reshape.612.row_ref, bf16[16,1536,256]{2,1,0:T(8,128)(2,1)} %w1_ref.7, bf16[16,1536,256]{2,1,0:T(8,128)(2,1)} %w3_ref.7, bf16[16,256,1536]{2,1,0:T(8,128)(2,1)} %w2_ref.7), custom_call_target="tpu_custom_call" | custom-call | flops 7474249728 | bytes 25067520 | tf_op jit(solution)/shard_map/pallas_call | solution.py:165
  98.6 3.9 fusion.227
  102.7 2.5 broadcast_in_dim.97
  108.0 2.4 bitcast_dynamic-update-slice_fusion.2
  113.1 104.3 %expert_bwd.1 = (f32[16,1536,256]{2,1,0:T(8,128)}, f32[16,1536,256]{2,1,0:T(8,128)}, f32[16,256,1536]{2,1,0:T(8,128)}, f32[504,1536]{1,0:T(8,128)}, f32[504,1536...) custom-call(bf16[1536,1536]{1,0:T(8,128)(2,1)} %bitcast.88, ...), custom_call_target="tpu_custom_call" | custom-call | flops 52344913920 | bytes 143130624 | tf_op jit(solution)/shard_map/expert_bwd/pallas_call | solution.py:196
  219.3 2.3 fusion.18
  221.6 1.8 constant_dynamic-update-slice_fusion.3
  224.6 2.1 fusion.223
  226.7 2.4 convolution_convert_fusion.2
  229.1 4.5 all-to-all-start
  235.3 1.7 fusion.22
  239.2 1.8 convolution_add_fusion.2
  241.9 25.6 %shared_grad.1 = (f32[1536,512]{1,0:T(8,128)}, f32[1536,512]{1,0:T(8,128)}, f32[512,1536]{1,0:T(8,128)}) custom-call(bf16[1536,1536]{1,0:T(8,128)(2,1)} %bitcast.89, bf16[1536,1536]{1,0:T(8,128)(2,1)} %bitcast.6.dy_ref, bf16[1536,512]{1,0:T(8,128)(2,1)S(1)} %copy-done.4, bf16[1536,512]{1,0:T(8,128)(2,1)S(1)} %copy-done.2, bf16[512,1536]{1,0:T(8,128)(2,1)S(1)} %copy-done.1), custom_call_target="tpu_custom_call" | custom-call | flops 14495514624 | bytes 23592960 | tf_op jit(solution)/shard_map/shared_grad/pallas_call | solution.py:263
  268.6 1.8 collective-permute-start.4
  270.4 1.9 constant_dynamic-update-slice_fusion.2
  272.4 2.0 collective-permute-start.21
  274.4 1.8 constant_dynamic-update-slice_fusion.1
  278.7 4.1 convolution_convert_fusion.1
  282.8 3.6 all-to-all-start.2
  286.4 2.6 collective-permute-done.4
  291.8 2.0 collective-permute-start.17
  295.0 2.2 fusion.23
  298.5 1.8 fusion.65
  302.6 5.3 %convolution_convert_fusion = bf16[672,1536]{1,0:T(8,128)(2,1)} fusion(f32[672,1536]{1,0:T(8,128)} %collective-permute-done.11, f32[672,1536]{1,0:T(8,128)S(1)} %copy-done.35, s32[672]{0:T(1024)S(1)} %add_select_fusion.6), kind=kOutput, calls=%fused_computation.1 | convolution fusion | flops 1390814208 | bytes 10324608 | tf_op jit(solution)/shard_map/dot_general | solution.py:24
  307.9 4.8 all-to-all-start.1
  314.4 6.1 %collective-permute-done.21 = f32[336,1536]{1,0:T(8,128)} collective-permute-done((f32[336,1536]{1,0:T(8,128)}, f32[336,1536]{1,0:T(8,128)}, u32[]{:S(2)}, u32[]{:S(2)}) %collective-permute-start.21) | collective-permute-done | bytes 2064416 | tf_op jit(solution)/shard_map/ppermute | solution.py:565
  320.5 4.0 fusion.25
  324.5 62.3 %collective-permute-done.13 = f32[504,1536]{1,0:T(8,128)} collective-permute-done((f32[504,1536]{1,0:T(8,128)}, f32[504,1536]{1,0:T(8,128)}, u32[]{:S(2)}, u32[]{:S(2)}) %collective-permute-start.13) | collective-permute-done | bytes 3096608 | tf_op jit(solution)/shard_map/ppermute | solution.py:489
  386.9 2.3 add_convert_fusion.2
  391.7 1.9 collective-permute-start.16
  393.6 58.8 %collective-permute-done.17 = f32[504,1536]{1,0:T(8,128)} collective-permute-done((f32[504,1536]{1,0:T(8,128)}, f32[504,1536]{1,0:T(8,128)}, u32[]{:S(2)}, u32[]{:S(2)}) %collective-permute-start.17) | collective-permute-done | bytes 3096608 | tf_op jit(solution)/shard_map/ppermute | solution.py:565
  452.3 2.3 add_convert_fusion.1
  459.1 2.4 reduce-precision_convert_fusion.1
  462.7 1.8 collective-permute-start.22
  464.5 5.5 %fusion.7 = f32[576,1536]{1,0:T(8,128)} fusion(bf16[672,1536]{1,0:T(8,128)(2,1)} %bitcast.11, pred[192,672]{1,0:T(32,128)(4,1)} %convolution_compare_fusion, s32[672]{0:T(1024)S(1)} %add_select_fusion.7, bf16[192,64]{0,1:T(8,128)(2,1)S(1)} %get-tuple-element.122, bf16[192,64]{0,1:T(8,128)(2,1)S(1)} %get-tuple-element.121, ...), kind=kOutput, calls=%fused_computation.30 | convolution fusion | flops 1240442880 | bytes 5808768 | tf_op jit(solution)/shard_map/dot_general | solution.py:24
  470.0 3.1 fusion.8
  473.2 3.8 fusion.24
  478.4 6.3 %fusion.5 = bf16[192,1536]{1,0:T(8,128)(2,1)} fusion(f32[192,1536]{1,0:T(8,128)S(1)} %copy-done.18, bf16[512,1536]{1,0:T(8,128)(2,1)} %constant_dynamic-update-slice_fusion, f32[576,1536]{1,0:T(8,128)} %fusion.8, f32[576,1536]{1,0:T(8,128)} %fusion.7, f32[576,1536]{1,0:T(8,128)} %fusion.24, f32[192,512]{1,0:T(8,128)S(1)} %copy-done.41, ...), kind=kOutput, calls=%fused_computation.15 | convolution fusion | flops 306216960 | bytes 14745600 | tf_op jit(solution)/shard_map/dot_general | solution.py:24
  484.8 1.7 fusion.4
  488.3 3.3 collective-permute-done.23
  495.1 3.7 fusion.47
  504.3 3.1 fusion.1
  510.6 2.8 collective-permute-done.20
  513.5 3.1 add_add_fusion
  516.5 2.6 add_convert_fusion.7
  (212 shorter events, 56.8 us)
Async XLA Ops:
  0.6 97.9 %copy-start = (bf16[1536,64]{0,1:T(8,128)(2,1)S(1)}, bf16[1536,64]{0,1:T(8,128)(2,1)}, u32[]{:S(2)}) copy-start(bf16[1536,64]{0,1:T(8,128)(2,1)} %param.12) | copy-start | bytes 589828
  41.6 68.7 %collective-permute-start.1 = (bf16[2,192,1536]{2,1,0:T(8,128)(2,1)}, bf16[2,192,1536]{2,1,0:T(8,128)(2,1)S(1)}, u32[]{:S(2)}, u32[]{:S(2)}) collective-permute-start(bf16[2,192,1536]{2,1,0:T(8,128)(2,1)} %get-tuple-element.53), channel_id=1, source_target_pairs={{0,1},{1,0},{2,3},{3,2},{4,5},{5,4},{6,7},{7,6}} | collective-permute-start | bytes 3538952 | tf_op jit(solution)/shard_map/ppermute | solution.py:434
  41.7 64.7 %collective-permute-start = (bf16[2,192,1536]{2,1,0:T(8,128)(2,1)}, bf16[2,192,1536]{2,1,0:T(8,128)(2,1)}, u32[]{:S(2)}, u32[]{:S(2)}) collective-permute-start(bf16[2,192,1536]{2,1,0:T(8,128)(2,1)} %get-tuple-element.53), channel_id=1, source_target_pairs={{0,2},{1,3},{2,0},{3,1},{4,6},{5,7},{6,4},{7,5}} | collective-permute-start | bytes 3538952 | tf_op jit(solution)/shard_map/ppermute | solution.py:433
  42.2 175.3 %collective-permute-start.3 = (bf16[1536,256]{1,0:T(8,128)(2,1)}, bf16[1536,256]{1,0:T(8,128)(2,1)}, u32[]{:S(2)}, u32[]{:S(2)}) collective-permute-start(bf16[1536,256]{1,0:T(8,128)(2,1)} %get-tuple-element.62), channel_id=1, source_target_pairs={{0,4},{4,0},{1,5},{5,1},{2,6},{6,2},{3,7},{7,3}} | collective-permute-start | bytes 2359304 | tf_op jit(solution)/shard_map/ppermute | solution.py:446
  54.9 171.7 %collective-permute-start.10 = (f32[168,1536]{1,0:T(8,128)}, f32[168,1536]{1,0:T(8,128)}, u32[]{:S(2)}, u32[]{:S(2)}) collective-permute-start(f32[168,1536]{1,0:T(8,128)} %get-tuple-element.74), channel_id=1, source_target_pairs={{0,4},{4,0},{1,5},{5,1},{2,6},{6,2},{3,7},{7,3}} | collective-permute-start | bytes 3096584 | tf_op jit(solution)/shard_map/ppermute | solution.py:465
  78.4 223.2 %collective-permute-start.11 = (f32[672,1536]{1,0:T(8,128)}, f32[672,1536]{1,0:T(8,128)}, u32[]{:S(2)}, u32[]{:S(2)}) collective-permute-start(f32[672,1536]{1,0:T(8,128)} %get-tuple-element.76), channel_id=1, source_target_pairs={{0,4},{4,0},{1,5},{5,1},{2,6},{6,2},{3,7},{7,3}} | collective-permute-start | bytes 12386312 | tf_op jit(solution)/shard_map/ppermute | solution.py:465
  106.4 5.7 %collective-permute-start.2 = (bf16[2,192,1536]{2,1,0:T(8,128)(2,1)}, bf16[2,192,1536]{2,1,0:T(8,128)(2,1)S(1)}, u32[]{:S(2)}, u32[]{:S(2)}) collective-permute-start(bf16[2,192,1536]{2,1,0:T(8,128)(2,1)} %collective-permute-done), channel_id=1, source_target_pairs={{0,1},{1,0},{2,3},{3,2},{4,5},{5,4},{6,7},{7,6}} | collective-permute-start | bytes 3538952 | tf_op jit(solution)/shard_map/ppermute | solution.py:434
  110.3 168.3 %collective-permute-start.12 = (f32[504,1536]{1,0:T(8,128)}, f32[504,1536]{1,0:T(8,128)}, u32[]{:S(2)}, u32[]{:S(2)}) collective-permute-start(f32[504,1536]{1,0:T(8,128)} %get-tuple-element.78), channel_id=1, source_target_pairs={{0,4},{4,0},{1,5},{5,1},{2,6},{6,2},{3,7},{7,3}} | collective-permute-start | bytes 9289736 | tf_op jit(solution)/shard_map/ppermute | solution.py:465
  113.1 106.1 %copy-start.3 = (bf16[1536,512]{1,0:T(8,128)(2,1)S(1)}, bf16[1536,512]{1,0:T(8,128)(2,1)}, u32[]{:S(2)}) copy-start(bf16[1536,512]{1,0:T(8,128)(2,1)} %wg_ref.3) | copy-start | bytes 4718596
  217.5 5.8 %copy-start.2 = (bf16[1536,512]{1,0:T(8,128)(2,1)S(1)}, bf16[1536,512]{1,0:T(8,128)(2,1)}, u32[]{:S(2)}) copy-start(bf16[1536,512]{1,0:T(8,128)(2,1)} %wu_ref.3) | copy-start | bytes 4718596
  217.5 5.8 %copy-start.8 = (bf16[192,1536]{1,0:T(8,128)(2,1)S(1)}, bf16[192,1536]{1,0:T(8,128)(2,1)}, u32[]{:S(2)}) copy-start(bf16[192,1536]{1,0:T(8,128)(2,1)} %x_ref.1) | copy-start | bytes 1769476
  217.5 54.8 %collective-permute-start.8 = (bf16[128,1536]{1,0:T(8,128)(2,1)}, bf16[128,1536]{1,0:T(8,128)(2,1)}, u32[]{:S(2)}, u32[]{:S(2)}) collective-permute-start(bf16[128,1536]{1,0:T(8,128)(2,1)} %get-tuple-element.71), channel_id=1, source_target_pairs={{0,1},{1,0},{2,3},{3,2},{4,5},{5,4},{6,7},{7,6}} | collective-permute-start | bytes 1179656 | tf_op jit(solution)/shard_map/ppermute | solution.py:434
  217.7 50.9 %collective-permute-start.7 = (bf16[128,1536]{1,0:T(8,128)(2,1)}, bf16[128,1536]{1,0:T(8,128)(2,1)}, u32[]{:S(2)}, u32[]{:S(2)}) collective-permute-start(bf16[128,1536]{1,0:T(8,128)(2,1)} %get-tuple-element.71), channel_id=1, source_target_pairs={{0,2},{1,3},{2,0},{3,1},{4,6},{5,7},{6,4},{7,5}} | collective-permute-start | bytes 1179656 | tf_op jit(solution)/shard_map/ppermute | solution.py:433
  226.6 6.9 %copy-start.34 = (s32[192,6]{0,1:T(8,128)S(1)}, s32[192,6]{0,1:T(8,128)}, u32[]{:S(2)}) copy-start(s32[192,6]{0,1:T(8,128)} %param.19) | copy-start | bytes 13828
  226.6 65.1 %collective-permute-start.5 = (bf16[1536,256]{1,0:T(8,128)(2,1)}, bf16[1536,256]{1,0:T(8,128)(2,1)}, u32[]{:S(2)}, u32[]{:S(2)}) collective-permute-start(bf16[1536,256]{1,0:T(8,128)(2,1)} %collective-permute-done.3), channel_id=1, source_target_pairs={{0,1},{1,0},{2,3},{3,2},{4,5},{5,4},{6,7},{7,6}} | collective-permute-start | bytes 2359304 | tf_op jit(solution)/shard_map/ppermute | solution.py:434
  229.1 6.2 %copy-start.1 = (bf16[512,1536]{1,0:T(8,128)(2,1)S(1)}, bf16[512,1536]{1,0:T(8,128)(2,1)}, u32[]{:S(2)}) copy-start(bf16[512,1536]{1,0:T(8,128)(2,1)} %wd_ref.3) | copy-start | bytes 4718596
  229.1 47.1 %all-to-all-start = ((bf16[4,48,1536]{2,1,0:T(8,128)(2,1)}), bf16[4,48,1536]{2,1,0:T(8,128)(2,1)}, u32[]{:S(2)}, u32[]{:S(2)}) async-start(bf16[4,48,1536]{2,1,0:T(8,128)(2,1)} %bitcast.91), calls=%async_computation | async-start | bytes 1179648 | tf_op jit(solution)/shard_map/all_to_all | solution.py:529
  268.6 20.3 %collective-permute-start.4 = (bf16[1536,256]{1,0:T(8,128)(2,1)}, bf16[1536,256]{1,0:T(8,128)(2,1)}, u32[]{:S(2)}, u32[]{:S(2)}) collective-permute-start(bf16[1536,256]{1,0:T(8,128)(2,1)} %collective-permute-done.3), channel_id=1, source_target_pairs={{0,2},{1,3},{2,0},{3,1},{4,6},{5,7},{6,4},{7,5}} | collective-permute-start | bytes 2359304 | tf_op jit(solution)/shard_map/ppermute | solution.py:433
  270.4 8.3 %copy-start.13 = (f32[504,1536]{1,0:T(8,128)S(1)}, f32[504,1536]{1,0:T(8,128)}, u32[]{:S(2)}) copy-start(f32[504,1536]{1,0:T(8,128)} %get-tuple-element.79) | copy-start | bytes 9289732
  272.4 48.1 %collective-permute-start.21 = (f32[336,1536]{1,0:T(8,128)}, f32[336,1536]{1,0:T(8,128)}, u32[]{:S(2)}, u32[]{:S(2)}) collective-permute-start(f32[336,1536]{1,0:T(8,128)} %get-tuple-element.85), channel_id=1, source_target_pairs={{0,4},{4,0},{1,5},{5,1},{2,6},{6,2},{3,7},{7,3}} | collective-permute-start | bytes 6193160 | tf_op jit(solution)/shard_map/ppermute | solution.py:565
  278.7 108.2 %collective-permute-start.13 = (f32[504,1536]{1,0:T(8,128)}, f32[504,1536]{1,0:T(8,128)}, u32[]{:S(2)}, u32[]{:S(2)}) collective-permute-start(f32[504,1536]{1,0:T(8,128)} %get-tuple-element.81), channel_id=1, source_target_pairs={{0,4},{4,0},{1,5},{5,1},{2,6},{6,2},{3,7},{7,3}} | collective-permute-start | bytes 9289736 | tf_op jit(solution)/shard_map/ppermute | solution.py:489
  282.8 25.1 %all-to-all-start.2 = ((bf16[4,128,1536]{2,1,0:T(8,128)(2,1)}), bf16[4,128,1536]{2,1,0:T(8,128)(2,1)S(1)}, u32[]{:S(2)}, u32[]{:S(2)}) async-start(bf16[4,128,1536]{2,1,0:T(8,128)(2,1)} %bitcast.12), calls=%async_computation.2 | async-start | bytes 3145728 | tf_op jit(solution)/shard_map/all_to_all | solution.py:529
  288.9 1.9 collective-permute-start.9
  290.1 7.2 %copy-start.25 = (bf16[1536,128]{1,0:T(8,128)(2,1)}, bf16[1536,128]{1,0:T(8,128)(2,1)S(1)}, u32[]{:S(2)}) copy-start(bf16[1536,128]{1,0:T(8,128)(2,1)S(1)} %get-tuple-element.103) | copy-start | bytes 1179652
  290.9 6.4 %collective-permute-start.6 = (bf16[1536,256]{1,0:T(8,128)(2,1)}, bf16[1536,256]{1,0:T(8,128)(2,1)S(1)}, u32[]{:S(2)}, u32[]{:S(2)}) collective-permute-start(bf16[1536,256]{1,0:T(8,128)(2,1)} %collective-permute-done.4), channel_id=1, source_target_pairs={{0,1},{1,0},{2,3},{3,2},{4,5},{5,4},{6,7},{7,6}} | collective-permute-start | bytes 2359304 | tf_op jit(solution)/shard_map/ppermute | solution.py:434
  291.8 160.6 %collective-permute-start.17 = (f32[504,1536]{1,0:T(8,128)}, f32[504,1536]{1,0:T(8,128)}, u32[]{:S(2)}, u32[]{:S(2)}) collective-permute-start(f32[504,1536]{1,0:T(8,128)} %get-tuple-element.83), channel_id=1, source_target_pairs={{0,4},{4,0},{1,5},{5,1},{2,6},{6,2},{3,7},{7,3}} | collective-permute-start | bytes 9289736 | tf_op jit(solution)/shard_map/ppermute | solution.py:565
  307.9 151.2 %all-to-all-start.1 = ((bf16[4,168,1536]{2,1,0:T(8,128)(2,1)}), bf16[4,168,1536]{2,1,0:T(8,128)(2,1)}, u32[]{:S(2)}, u32[]{:S(2)}) async-start(bf16[4,168,1536]{2,1,0:T(8,128)(2,1)} %bitcast.10), calls=%async_computation.1 | async-start | bytes 4128768 | tf_op jit(solution)/shard_map/all_to_all | solution.py:529
  320.5 66.4 %copy-start.12 = (f32[504,1536]{1,0:T(8,128)S(1)}, f32[504,1536]{1,0:T(8,128)}, u32[]{:S(2)}) copy-start(f32[504,1536]{1,0:T(8,128)} %get-tuple-element.82) | copy-start | bytes 9289732
  390.5 61.9 %copy-start.11 = (f32[504,1536]{1,0:T(8,128)S(1)}, f32[504,1536]{1,0:T(8,128)}, u32[]{:S(2)}) copy-start(f32[504,1536]{1,0:T(8,128)} %get-tuple-element.84) | copy-start | bytes 9289732
  391.4 112.9 %collective-permute-start.14 = (bf16[168,1536]{1,0:T(8,128)(2,1)S(1)}, bf16[168,1536]{1,0:T(8,128)(2,1)}, u32[]{:S(2)}, u32[]{:S(2)}) collective-permute-start(bf16[168,1536]{1,0:T(8,128)(2,1)S(1)} %convolution_convert_fusion.8), channel_id=1, source_target_pairs={{0,2},{1,3},{2,0},{3,1},{4,6},{5,7},{6,4},{7,5}} | collective-permute-start | bytes 1548296 | tf_op jit(solution)/shard_map/ppermute | solution.py:586
  391.7 111.0 %collective-permute-start.15 = (bf16[168,1536]{1,0:T(8,128)(2,1)S(1)}, bf16[168,1536]{1,0:T(8,128)(2,1)}, u32[]{:S(2)}, u32[]{:S(2)}) collective-permute-start(bf16[168,1536]{1,0:T(8,128)(2,1)S(1)} %convolution_convert_fusion.7), channel_id=1, source_target_pairs={{0,1},{1,0},{2,3},{3,2},{4,5},{5,4},{6,7},{7,6}} | collective-permute-start | bytes 1548296 | tf_op jit(solution)/shard_map/ppermute | solution.py:586
  391.7 108.0 %collective-permute-start.16 = (bf16[168,1536]{1,0:T(8,128)(2,1)}, bf16[168,1536]{1,0:T(8,128)(2,1)}, u32[]{:S(2)}, u32[]{:S(2)}) collective-permute-start(bf16[168,1536]{1,0:T(8,128)(2,1)} %convolution_convert_fusion.6), channel_id=1, source_target_pairs={{0,3},{1,2},{2,1},{3,0},{4,7},{5,6},{6,5},{7,4}} | collective-permute-start | bytes 1548296 | tf_op jit(solution)/shard_map/ppermute | solution.py:586
  455.9 53.1 %collective-permute-start.18 = (bf16[168,1536]{1,0:T(8,128)(2,1)}, bf16[168,1536]{1,0:T(8,128)(2,1)}, u32[]{:S(2)}, u32[]{:S(2)}) collective-permute-start(bf16[168,1536]{1,0:T(8,128)(2,1)} %convolution_convert_fusion.5), channel_id=1, source_target_pairs={{0,2},{1,3},{2,0},{3,1},{4,6},{5,7},{6,4},{7,5}} | collective-permute-start | bytes 1548296 | tf_op jit(solution)/shard_map/ppermute | solution.py:586
  462.7 23.8 %collective-permute-start.22 = (f32[192,64]{0,1:T(8,128)S(1)}, f32[192,64]{0,1:T(8,128)S(1)}, u32[]{:S(2)}, u32[]{:S(2)}) collective-permute-start(f32[192,64]{0,1:T(8,128)S(1)} %get-tuple-element.96), channel_id=1, source_target_pairs={{0,4},{4,0},{1,5},{5,1},{2,6},{6,2},{3,7},{7,3}} | collective-permute-start | bytes 147464 | tf_op jit(solution)/shard_map/ppermute | solution.py:563
  464.5 5.6 %copy-start.17 = (bf16[4,128,1536]{2,1,0:T(8,128)(2,1)S(1)}, bf16[4,128,1536]{2,1,0:T(8,128)(2,1)}, u32[]{:S(2)}) copy-start(bf16[4,128,1536]{2,1,0:T(8,128)(2,1)} %copy-done.16) | copy-start | bytes 4718596
  464.5 5.6 %copy-start.37 = (pred[192,512]{1,0:T(32,128)(4,1)S(1)}, pred[192,512]{1,0:T(32,128)(4,1)}, u32[]{:S(2)}) copy-start(pred[192,512]{1,0:T(32,128)(4,1)} %convolution_compare_fusion.1) | copy-start | bytes 294916
  478.4 6.3 %copy-start.20 = (f32[192,1536]{1,0:T(8,128)S(1)}, f32[192,1536]{1,0:T(8,128)}, u32[]{:S(2)}) copy-start(f32[192,1536]{1,0:T(8,128)} %convolution_add_fusion.2) | copy-start | bytes 3538948
  478.4 6.3 %copy-start.22 = (f32[192,512]{1,0:T(8,128)S(1)}, f32[192,512]{1,0:T(8,128)}, u32[]{:S(2)}) copy-start(f32[192,512]{1,0:T(8,128)} %copy-done.21) | copy-start | bytes 1179652
  478.4 6.3 %copy-start.24 = (bf16[1536,128]{1,0:T(8,128)(2,1)S(1)}, bf16[1536,128]{1,0:T(8,128)(2,1)}, u32[]{:S(2)}) copy-start(bf16[1536,128]{1,0:T(8,128)(2,1)} %get-tuple-element.101) | copy-start | bytes 1179652
  478.4 6.3 %copy-start.26 = (bf16[1536,128]{1,0:T(8,128)(2,1)S(1)}, bf16[1536,128]{1,0:T(8,128)(2,1)}, u32[]{:S(2)}) copy-start(bf16[1536,128]{1,0:T(8,128)(2,1)} %copy-done.25) | copy-start | bytes 1179652
  478.4 6.3 %copy-start.28 = (bf16[1536,128]{1,0:T(8,128)(2,1)S(1)}, bf16[1536,128]{1,0:T(8,128)(2,1)}, u32[]{:S(2)}) copy-start(bf16[1536,128]{1,0:T(8,128)(2,1)} %copy-done.27) | copy-start | bytes 1179652
  478.4 6.3 %copy-start.30 = (bf16[1536,128]{1,0:T(8,128)(2,1)S(1)}, bf16[1536,128]{1,0:T(8,128)(2,1)}, u32[]{:S(2)}) copy-start(bf16[1536,128]{1,0:T(8,128)(2,1)} %copy-done.29) | copy-start | bytes 1179652
  478.4 6.3 %copy-start.42 = (f32[192,1536]{1,0:T(8,128)S(1)}, f32[192,1536]{1,0:T(8,128)}, u32[]{:S(2)}) copy-start(f32[192,1536]{1,0:T(8,128)} %fusion.65) | copy-start | bytes 3538948
  486.5 5.0 collective-permute-start.23
  491.5 1.3 collective-permute-start.24
  492.9 1.3 collective-permute-start.25
  494.2 13.1 %collective-permute-start.19 = (bf16[168,1536]{1,0:T(8,128)(2,1)}, bf16[168,1536]{1,0:T(8,128)(2,1)}, u32[]{:S(2)}, u32[]{:S(2)}) collective-permute-start(bf16[168,1536]{1,0:T(8,128)(2,1)} %convolution_convert_fusion.4), channel_id=1, source_target_pairs={{0,1},{1,0},{2,3},{3,2},{4,5},{5,4},{6,7},{7,6}} | collective-permute-start | bytes 1548296 | tf_op jit(solution)/shard_map/ppermute | solution.py:586
  499.6 13.8 %collective-permute-start.20 = (bf16[168,1536]{1,0:T(8,128)(2,1)}, bf16[168,1536]{1,0:T(8,128)(2,1)}, u32[]{:S(2)}, u32[]{:S(2)}) collective-permute-start(bf16[168,1536]{1,0:T(8,128)(2,1)} %convolution_convert_fusion.3), channel_id=1, source_target_pairs={{0,3},{1,2},{2,1},{3,0},{4,7},{5,6},{6,5},{7,4}} | collective-permute-start | bytes 1548296 | tf_op jit(solution)/shard_map/ppermute | solution.py:586
  (24 other events, 56.1 us)

commit v4 on v3

--- a/solution.py
+++ b/solution.py
@@ -13,6 +13,7 @@
 F32 = jnp.float32
 FWD_CHUNKS = (2, 8, 6)
 BWD_CHUNKS = 2
+RETURN_ORDER = (1, 0, 2)
 MESH = pl.DeviceIdType.MESH
 
 NN = (((1,), (0,)), ((), ()))
@@ -490,13 +491,42 @@
 
         own_last = bwd_out[-1][1]
         own_first = fwd_parts[0][1]
-        x, grad_y, x_all, dy_all, topk_idx, w_router, gu_part, wd_part, own_first, own_last = lax.optimization_barrier(
-            (x, grad_y, x_all, dy_all, topk_idx, w_router, gu_part, wd_part, own_first, own_last))
+        gu_far = lax.ppermute(gu_part, 'ep', swap_x)
+        wd_far = lax.ppermute(wd_part, 'ep', swap_x)
+        x, grad_y, x_all, dy_all, topk_idx, w_router, gu_part, wd_part, gu_far, wd_far, own_first, own_last = lax.optimization_barrier(
+            (x, grad_y, x_all, dy_all, topk_idx, w_router, gu_part, wd_part, gu_far, wd_far, own_first, own_last))
         fwd_parts[0] = (fwd_parts[0][0], own_first)
         bwd_out[-1] = (bwd_out[-1][0], own_last)
 
-        gu_other = ep_pieces(gu_part)
-        wd_other = jnp.concatenate(ep_pieces(wd_part), axis=0)
+        def back_rows(count):
+            return count * cap + (-count * cap) % 8
+
+        def slot_index(count):
+            new = jnp.arange(ep_size * back_rows(count), dtype=jnp.int32)
+            block, rest = new // back_rows(count), new % back_rows(count)
+            return block, rest // cap, rest % cap, rest < count * cap
+
+        def turn(parts, count):
+            recv, own = parts
+            rows = (recv + own).astype(BF16)
+            src, exp, rank, valid = slot_index(count)
+            old = jnp.where(valid, exp * half + src * cap + rank, -1)
+            perm = (old[:, None] == jnp.arange(count * half, dtype=jnp.int32)[None, :]).astype(BF16)
+            return dot(perm, rows).astype(BF16)
+
+        def send_home(out, count):
+            out = out.reshape(ep_size, back_rows(count), model)
+            out = lax.all_to_all(out, 'ep', 0, 0)
+            return out.reshape(ep_size * back_rows(count), model)
+
+        early = RETURN_ORDER[0]
+        early_rows = turn(fwd_parts[early], FWD_CHUNKS[early])
+        x, grad_y, topk_idx, gu_part, wd_part, gu_far, wd_far, early_rows = lax.optimization_barrier(
+            (x, grad_y, topk_idx, gu_part, wd_part, gu_far, wd_far, early_rows))
+        early_back = send_home(early_rows, FWD_CHUNKS[early])
+
+        gu_other = (gu_part, gu_far, lax.ppermute(gu_part, 'ep', swap_c), lax.ppermute(gu_far, 'ep', swap_c))
+        wd_other = jnp.concatenate((wd_part, wd_far, lax.ppermute(wd_part, 'ep', swap_c), lax.ppermute(wd_far, 'ep', swap_c)), axis=0)
         wg_other = jnp.concatenate([p[:, :width_q] for p in gu_other], axis=1)
         wu_other = jnp.concatenate([p[:, width_q:] for p in gu_other], axis=1)
         shared = jnp.zeros((tok, model), F32)
@@ -510,25 +540,6 @@
             dx_shared = dx_shared + dot(da, wg, NT) + dot(db, wu, NT)
         ds_gate, ds_up, ds_down = shared_grad(x_all, dy_all, ws_gate, ws_up, ws_down)
 
-        def back_rows(count):
-            return count * cap + (-count * cap) % 8
-
-        def slot_index(count):
-            new = jnp.arange(ep_size * back_rows(count), dtype=jnp.int32)
-            block, rest = new // back_rows(count), new % back_rows(count)
-            return block, rest // cap, rest % cap, rest < count * cap
-
-        def give_back(parts, count):
-            recv, own = parts
-            rows = (recv + own).astype(BF16)
-            src, exp, rank, valid = slot_index(count)
-            old = jnp.where(valid, exp * half + src * cap + rank, -1)
-            perm = (old[:, None] == jnp.arange(count * half, dtype=jnp.int32)[None, :]).astype(BF16)
-            out = dot(perm, rows).astype(BF16)
-            out = out.reshape(ep_size, back_rows(count), model)
-            out = lax.all_to_all(out, 'ep', 0, 0)
-            return out.reshape(ep_size * back_rows(count), model)
-
         hit_own = jnp.any(topk_idx[:, None, :] == jnp.arange(experts, dtype=jnp.int32)[None, :, None], axis=2)
         rank_own = dot(lower, hit_own.astype(BF16))
         want = jnp.where(hit_own, rank_own, -1.0).astype(BF16)
@@ -543,9 +554,13 @@
 
         routed = jnp.zeros((tok, model), F32)
         d_scores = jnp.zeros((tok, experts), F32)
-        start = 0
-        for parts, count in zip(fwd_parts, FWD_CHUNKS):
-            back = give_back(parts, count)
+        back = early_back
+        for j in RETURN_ORDER:
+            count, start = FWD_CHUNKS[j], sum(FWD_CHUNKS[:j])
+            if j != early:
+                recv, own = fwd_parts[j]
+                back, own = lax.optimization_barrier((back, own))
+                back = send_home(turn((recv, own), count), count)
             table, rank = expand(start, count)
             hits = dot(want, table) == rank
             gates = jnp.where(jnp.concatenate([hits] * 3, axis=0), dot(prob_parts, table), 0.0).astype(BF16)
@@ -554,7 +569,6 @@
             score = jnp.where(hits, dot(grad_y, back, NT), 0.0)
             part = dot(jnp.concatenate(split3(score), axis=0), table, NT)
             d_scores = d_scores + sum3(part, 0)
-            start += count
         y_out = (shared + routed).astype(BF16)
 
         d_scores = GATE_SCALE * d_scores

time: 521 us -> 584 us (1.12)
  waiting for transfers between devices: 139 us -> 197 us
    ppermute x2, waiting for transfers between devices: 64.8 us -> 125 us  [device_step(): bwd_parts.append((lax.ppermute(send, 'tp', swap_tp), own))]
    all_to_all x3, waiting for transfers between devices: 0.01 us -> 25.1 us  [send_home(): out = lax.all_to_all(out, 'ep', 0, 0)]
    ppermute x1, waiting for transfers between devices: 62.3 us -> 40.6 us  [device_step(): bwd_parts = [(lax.ppermute(bwd_out[0][0], 'tp', swap_tp), bwd_out[0][1])]]
    unnamed x89 -> x119, local copies, waits for them, and re-layouts: 9.66 us -> 12.6 us
  transfers between devices with their start and end apart: 29 -> 29, of which waited for: 9 -> 6; matrix products, arithmetic and copies ran while one was open for 22% -> 21% of each run, Pallas kernels for 35% -> 31%
where the time goes in v4:
time: 584 us; the launch traced here: 582 us
  Pallas kernels  221 us (38%)
  waiting for transfers between devices  197 us (34%)
  matrix products  93.5 us (16%)
  local copies, waits for them, and re-layouts  30 us (5%)
  starting transfers between devices  27.9 us (5%)
  other arithmetic  11.2 us (2%)
    ppermute x2, waiting for transfers between devices, device_step(): bwd_parts.append((lax.ppermute(send, 'tp', swap_tp), own))  125 us
    pallas_call x1, Pallas kernels, expert_bwd(): pl.pallas_call(functools.partial(bwd_kernel, sizes, per_chunk), grid=(cou...  105 us
    dot_general x44, matrix products, dot(): return lax.dot_general(a, b, dims, preferred_element_type=F32)  89.4 us
    pallas_call x3, Pallas kernels, expert_fwd(): pl.pallas_call(functools.partial(fwd_kernel, half, padded), grid=(count,)...  49.5 us
    pallas_call x1, Pallas kernels, gather_rows(): pl.pallas_call(gather_kernel, in_specs=[any_spec] * 6, out_specs=[any_spe...  41 us
    ppermute x1, waiting for transfers between devices, device_step(): bwd_parts = [(lax.ppermute(bwd_out[0][0], 'tp', swap_tp), bwd_out[0][1])]  40.6 us
    pallas_call x1, Pallas kernels, shared_grad(): pl.pallas_call(functools.partial(shared_grad_kernel, 256), grid=(width //...  25.7 us
    all_to_all x3, waiting for transfers between devices, send_home(): out = lax.all_to_all(out, 'ep', 0, 0)  25.1 us
  transfers between devices with their start and end apart: 29, of which 6 were waited for; matrix products, arithmetic and copies ran while one was open for 21% of the time, Pallas kernels for 31%

profile of v4, /device:TPU:0, one launch (start us, length us, event | category | flops | bytes accessed | tf_op | source)
XLA Modules:
  0.0 582.1 jit_solution(17703990039370889365)
XLA Ops:
  0.7 41.0 %gather_rows.1 = (bf16[8,192,1536]{2,1,0:T(8,128)(2,1)}, s32[8,6,192]{2,1,0:T(8,128)}, bf16[2,192,1536]{2,1,0:T(8,128)(2,1)}, bf16[128,1536]{1,0:T(8,128)(2,1)}, bf16[1536,256]{1,0:T(8,128)(2,1)}) custom-call(bf16[192,1536]{1,0:T(8,128)(2,1)} %x_ref.1, s32[6,192]{1,0:T(8,128)} %bitcast.102, bf16[192,1536]{1,0:T(8,128)(2,1)} %dy_ref.1, ...), custom_call_target="tpu_custom_call" | custom-call | flops 60000002048 | bytes 9437184 | tf_op jit(solution)/shard_map/gather_rows/pallas_call | solution.py:384
  46.6 8.8 %shard_map.169 = (f32[168,1536]{1,0:T(8,128)}, f32[168,1536]{1,0:T(8,128)S(1)}) custom-call(bf16[1536,1536]{1,0:T(8,128)(2,1)} %bitcast.84, s32[16,1,1536]{2,1,0:T(1,128)S(1)} %reshape.612.row_ref, bf16[16,1536,256]{2,1,0:T(8,128)(2,1)} %w1_ref.7, bf16[16,1536,256]{2,1,0:T(8,128)(2,1)} %w3_ref.7, bf16[16,256,1536]{2,1,0:T(8,128)(2,1)} %w2_ref.7), custom_call_target="tpu_custom_call" | custom-call | flops 2491416576 | bytes 11501568 | tf_op jit(solution)/shard_map/pallas_call | solution.py:166
  58.3 22.4 %shard_map.170 = (f32[672,1536]{1,0:T(8,128)S(1)}, f32[672,1536]{1,0:T(8,128)}) custom-call(bf16[1536,1536]{1,0:T(8,128)(2,1)} %bitcast.85, s32[16,1,1536]{2,1,0:T(1,128)S(1)} %reshape.612.row_ref, bf16[16,1536,256]{2,1,0:T(8,128)(2,1)} %w1_ref.7, bf16[16,1536,256]{2,1,0:T(8,128)(2,1)} %w3_ref.7, bf16[16,256,1536]{2,1,0:T(8,128)(2,1)} %w2_ref.7), custom_call_target="tpu_custom_call" | custom-call | flops 9965666304 | bytes 31850496 | tf_op jit(solution)/shard_map/pallas_call | solution.py:166
  80.7 1.9 copy-done.7
  82.6 18.3 %shard_map.171 = (f32[504,1536]{1,0:T(8,128)}, f32[504,1536]{1,0:T(8,128)}) custom-call(bf16[1536,1536]{1,0:T(8,128)(2,1)} %bitcast.86, s32[16,1,1536]{2,1,0:T(1,128)S(1)} %reshape.612.row_ref, bf16[16,1536,256]{2,1,0:T(8,128)(2,1)} %w1_ref.7, bf16[16,1536,256]{2,1,0:T(8,128)(2,1)} %w3_ref.7, bf16[16,256,1536]{2,1,0:T(8,128)(2,1)} %w2_ref.7), custom_call_target="tpu_custom_call" | custom-call | flops 7474249728 | bytes 25067520 | tf_op jit(solution)/shard_map/pallas_call | solution.py:166
  101.0 3.9 fusion.227
  105.0 2.6 broadcast_in_dim.97
  116.5 2.4 bitcast_dynamic-update-slice_fusion
  118.9 104.6 %expert_bwd.1 = (f32[16,1536,256]{2,1,0:T(8,128)}, f32[16,1536,256]{2,1,0:T(8,128)}, f32[16,256,1536]{2,1,0:T(8,128)}, f32[504,1536]{1,0:T(8,128)}, f32[504,1536...) custom-call(bf16[1536,1536]{1,0:T(8,128)(2,1)} %bitcast.88, ...), custom_call_target="tpu_custom_call" | custom-call | flops 52344913920 | bytes 143130624 | tf_op jit(solution)/shard_map/expert_bwd/pallas_call | solution.py:197
  223.9 1.6 collective-permute-start.13
  226.9 25.7 %shared_grad.1 = (f32[1536,512]{1,0:T(8,128)}, f32[1536,512]{1,0:T(8,128)}, f32[512,1536]{1,0:T(8,128)}) custom-call(bf16[1536,1536]{1,0:T(8,128)(2,1)} %bitcast.89, bf16[1536,1536]{1,0:T(8,128)(2,1)} %bitcast.6.dy_ref, bf16[1536,512]{1,0:T(8,128)(2,1)S(1)} %copy-done.2, bf16[1536,512]{1,0:T(8,128)(2,1)S(1)} %copy-done.3, bf16[512,1536]{1,0:T(8,128)(2,1)S(1)} %copy-done.1), custom_call_target="tpu_custom_call" | custom-call | flops 14495514624 | bytes 23592960 | tf_op jit(solution)/shard_map/shared_grad/pallas_call | solution.py:264
  252.6 5.3 convolution_convert_fusion
  260.4 1.8 constant_dynamic-update-slice_fusion.3
  262.2 4.8 all-to-all-start
  268.6 1.7 fusion.22
  270.9 1.8 constant_dynamic-update-slice_fusion.2
  274.7 1.6 fusion.74
  277.7 1.7 convolution_add_fusion.2
  279.4 2.0 fusion.223
  281.4 2.0 fusion.224
  283.7 4.0 fusion.25
  291.2 1.6 collective-permute-start.17
  295.6 1.8 fusion.65
  297.4 40.6 %collective-permute-done.13 = f32[504,1536]{1,0:T(8,128)} collective-permute-done((f32[504,1536]{1,0:T(8,128)}, f32[504,1536]{1,0:T(8,128)}, u32[]{:S(2)}, u32[]{:S(2)}) %collective-permute-start.13) | collective-permute-done | bytes 3096608 | tf_op jit(solution)/shard_map/ppermute | solution.py:490
  337.9 2.3 add_convert_fusion.2
  344.6 124.8 %collective-permute-done.17 = f32[504,1536]{1,0:T(8,128)S(1)} collective-permute-done((f32[504,1536]{1,0:T(8,128)S(1)}, f32[504,1536]{1,0:T(8,128)S(1)}, u32[]{:S(2)}, u32[]{:S(2)}) %collective-permute-start.17) | collective-permute-done | bytes 3096608 | tf_op jit(solution)/shard_map/ppermute | solution.py:579
  475.5 2.4 convolution_convert_fusion.2
  477.9 3.5 all-to-all-start.1
  481.4 2.4 reduce-precision_convert_fusion.1
  485.3 1.6 fusion.28
  487.0 13.8 %all-to-all-done.1 = bf16[4,48,1536]{2,1,0:T(8,128)(2,1)S(1)} async-done(((bf16[4,48,1536]{2,1,0:T(8,128)(2,1)}), bf16[4,48,1536]{2,1,0:T(8,128)(2,1)S(1)}, u32[]{:S(2)}, u32[]{:S(2)}) %all-to-all-start.1) | async-done | bytes 589856 | tf_op jit(solution)/shard_map/all_to_all | solution.py:519
  500.9 5.0 convolution_convert_fusion.1
  505.9 4.6 all-to-all-start.2
  510.5 2.8 fusion.27
  514.0 1.6 fusion.30
  515.7 2.6 fusion.29
  520.7 11.3 %all-to-all-done.2 = bf16[4,128,1536]{2,1,0:T(8,128)(2,1)} async-done(((bf16[4,128,1536]{2,1,0:T(8,128)(2,1)}), bf16[4,128,1536]{2,1,0:T(8,128)(2,1)}, u32[]{:S(2)}, u32[]{:S(2)}) %all-to-all-start.2) | async-done | bytes 1572896 | tf_op jit(solution)/shard_map/all_to_all | solution.py:519
  532.0 2.3 reduce-precision_convert_fusion.5
  536.2 4.7 fusion.8
  542.8 3.3 fusion.4
  546.1 3.5 fusion.1
  549.6 2.8 fusion.24
  552.4 5.5 fusion.7
  557.9 3.2 add_add_fusion
  561.1 2.7 add_convert_fusion.7
  563.8 5.8 fusion.5
  570.0 5.6 collective-permute-done.23
  577.8 3.4 fusion.47
  (242 shorter events, 55.3 us)
Async XLA Ops:
  0.6 100.3 %copy-start = (bf16[1536,64]{0,1:T(8,128)(2,1)S(1)}, bf16[1536,64]{0,1:T(8,128)(2,1)}, u32[]{:S(2)}) copy-start(bf16[1536,64]{0,1:T(8,128)(2,1)} %param.12) | copy-start | bytes 589828
  41.6 73.1 %collective-permute-start.1 = (bf16[2,192,1536]{2,1,0:T(8,128)(2,1)}, bf16[2,192,1536]{2,1,0:T(8,128)(2,1)S(1)}, u32[]{:S(2)}, u32[]{:S(2)}) collective-permute-start(bf16[2,192,1536]{2,1,0:T(8,128)(2,1)} %get-tuple-element.65), channel_id=1, source_target_pairs={{0,1},{1,0},{2,3},{3,2},{4,5},{5,4},{6,7},{7,6}} | collective-permute-start | bytes 3538952 | tf_op jit(solution)/shard_map/ppermute | solution.py:435
  41.7 68.4 %collective-permute-start = (bf16[2,192,1536]{2,1,0:T(8,128)(2,1)}, bf16[2,192,1536]{2,1,0:T(8,128)(2,1)S(1)}, u32[]{:S(2)}, u32[]{:S(2)}) collective-permute-start(bf16[2,192,1536]{2,1,0:T(8,128)(2,1)} %get-tuple-element.65), channel_id=1, source_target_pairs={{0,2},{1,3},{2,0},{3,1},{4,6},{5,7},{6,4},{7,5}} | collective-permute-start | bytes 3538952 | tf_op jit(solution)/shard_map/ppermute | solution.py:434
  42.2 181.2 %collective-permute-start.5 = (bf16[128,1536]{1,0:T(8,128)(2,1)}, bf16[128,1536]{1,0:T(8,128)(2,1)}, u32[]{:S(2)}, u32[]{:S(2)}) collective-permute-start(bf16[128,1536]{1,0:T(8,128)(2,1)} %get-tuple-element.93), channel_id=1, source_target_pairs={{0,2},{1,3},{2,0},{3,1},{4,6},{5,7},{6,4},{7,5}} | collective-permute-start | bytes 1179656 | tf_op jit(solution)/shard_map/ppermute | solution.py:495
  43.7 69.6 %collective-permute-start.3 = (bf16[1536,256]{1,0:T(8,128)(2,1)}, bf16[1536,256]{1,0:T(8,128)(2,1)}, u32[]{:S(2)}, u32[]{:S(2)}) collective-permute-start(bf16[1536,256]{1,0:T(8,128)(2,1)} %get-tuple-element.74), channel_id=1, source_target_pairs={{0,4},{4,0},{1,5},{5,1},{2,6},{6,2},{3,7},{7,3}} | collective-permute-start | bytes 2359304 | tf_op jit(solution)/shard_map/ppermute | solution.py:447
  56.4 417.7 %collective-permute-start.11 = (f32[168,1536]{1,0:T(8,128)}, f32[168,1536]{1,0:T(8,128)}, u32[]{:S(2)}, u32[]{:S(2)}) collective-permute-start(f32[168,1536]{1,0:T(8,128)} %get-tuple-element.98), channel_id=1, source_target_pairs={{0,4},{4,0},{1,5},{5,1},{2,6},{6,2},{3,7},{7,3}} | collective-permute-start | bytes 3096584 | tf_op jit(solution)/shard_map/ppermute | solution.py:466
  57.0 458.7 %copy-start.37 = (f32[168]{0:T(256)}, f32[168]{0:T(256)S(1)}, u32[]{:S(2)}) copy-start(f32[168]{0:T(256)S(1)} %fusion.192) | copy-start | bytes 2020
  57.6 476.7 %copy-start.44 = (s32[512]{0:T(512)}, s32[512]{0:T(512)S(1)}, u32[]{:S(2)}) copy-start(s32[512]{0:T(512)S(1)} %fusion.170) | copy-start | bytes 6148
  57.7 426.1 %copy-start.42 = (s32[672]{0:T(1024)}, s32[672]{0:T(1024)S(1)}, u32[]{:S(2)}) copy-start(s32[672]{0:T(1024)S(1)} %add_select_fusion.6) | copy-start | bytes 8068
  110.0 6.4 %collective-permute-start.2 = (bf16[2,192,1536]{2,1,0:T(8,128)(2,1)S(1)}, bf16[2,192,1536]{2,1,0:T(8,128)(2,1)}, u32[]{:S(2)}, u32[]{:S(2)}) collective-permute-start(bf16[2,192,1536]{2,1,0:T(8,128)(2,1)S(1)} %collective-permute-done), channel_id=1, source_target_pairs={{0,1},{1,0},{2,3},{3,2},{4,5},{5,4},{6,7},{7,6}} | collective-permute-start | bytes 3538952 | tf_op jit(solution)/shard_map/ppermute | solution.py:435
  113.3 139.3 %collective-permute-start.6 = (f32[672,1536]{1,0:T(8,128)}, f32[672,1536]{1,0:T(8,128)}, u32[]{:S(2)}, u32[]{:S(2)}) collective-permute-start(f32[672,1536]{1,0:T(8,128)} %copy-done.7), channel_id=1, source_target_pairs={{0,4},{4,0},{1,5},{5,1},{2,6},{6,2},{3,7},{7,3}} | collective-permute-start | bytes 12386312 | tf_op jit(solution)/shard_map/ppermute | solution.py:466
  114.8 108.7 %collective-permute-start.4 = (bf16[1536,256]{1,0:T(8,128)(2,1)}, bf16[1536,256]{1,0:T(8,128)(2,1)}, u32[]{:S(2)}, u32[]{:S(2)}) collective-permute-start(bf16[1536,256]{1,0:T(8,128)(2,1)} %collective-permute-done.3), channel_id=1, source_target_pairs={{0,2},{1,3},{2,0},{3,1},{4,6},{5,7},{6,4},{7,5}} | collective-permute-start | bytes 2359304 | tf_op jit(solution)/shard_map/ppermute | solution.py:494
  118.9 106.6 %copy-start.1 = (bf16[512,1536]{1,0:T(8,128)(2,1)S(1)}, bf16[512,1536]{1,0:T(8,128)(2,1)}, u32[]{:S(2)}) copy-start(bf16[512,1536]{1,0:T(8,128)(2,1)} %wd_ref.3) | copy-start | bytes 4718596
  118.9 106.6 %copy-start.2 = (bf16[1536,512]{1,0:T(8,128)(2,1)S(1)}, bf16[1536,512]{1,0:T(8,128)(2,1)}, u32[]{:S(2)}) copy-start(bf16[1536,512]{1,0:T(8,128)(2,1)} %wg_ref.3) | copy-start | bytes 4718596
  223.4 60.1 %collective-permute-start.21 = (f32[336,1536]{1,0:T(8,128)}, f32[336,1536]{1,0:T(8,128)}, u32[]{:S(2)}, u32[]{:S(2)}) collective-permute-start(f32[336,1536]{1,0:T(8,128)} %get-tuple-element.109), channel_id=1, source_target_pairs={{0,4},{4,0},{1,5},{5,1},{2,6},{6,2},{3,7},{7,3}} | collective-permute-start | bytes 6193160 | tf_op jit(solution)/shard_map/ppermute | solution.py:579
  223.9 114.1 %collective-permute-start.13 = (f32[504,1536]{1,0:T(8,128)}, f32[504,1536]{1,0:T(8,128)}, u32[]{:S(2)}, u32[]{:S(2)}) collective-permute-start(f32[504,1536]{1,0:T(8,128)} %get-tuple-element.105), channel_id=1, source_target_pairs={{0,4},{4,0},{1,5},{5,1},{2,6},{6,2},{3,7},{7,3}} | collective-permute-start | bytes 9289736 | tf_op jit(solution)/shard_map/ppermute | solution.py:490
  226.9 25.7 %copy-start.51 = (f32[672,1536]{1,0:T(8,128)S(1)}, f32[672,1536]{1,0:T(8,128)}, u32[]{:S(2)}) copy-start(f32[672,1536]{1,0:T(8,128)} %get-tuple-element.89) | copy-start | bytes 12386308
  252.6 5.4 copy-start.9
  260.4 27.2 %collective-permute-start.9 = (bf16[128,1536]{1,0:T(8,128)(2,1)}, bf16[128,1536]{1,0:T(8,128)(2,1)}, u32[]{:S(2)}, u32[]{:S(2)}) collective-permute-start(bf16[128,1536]{1,0:T(8,128)(2,1)} %get-tuple-element.93), channel_id=1, source_target_pairs={{0,1},{1,0},{2,3},{3,2},{4,5},{5,4},{6,7},{7,6}} | collective-permute-start | bytes 1179656 | tf_op jit(solution)/shard_map/ppermute | solution.py:529
  262.2 4.8 copy-start.41
  262.2 211.9 %all-to-all-start = ((bf16[4,168,1536]{2,1,0:T(8,128)(2,1)}), bf16[4,168,1536]{2,1,0:T(8,128)(2,1)}, u32[]{:S(2)}, u32[]{:S(2)}) async-start(bf16[4,168,1536]{2,1,0:T(8,128)(2,1)} %bitcast.94), calls=%async_computation | async-start | bytes 4128768 | tf_op jit(solution)/shard_map/all_to_all | solution.py:519
  268.6 266.0 %copy-start.39 = (f32[192]{0:T(256)}, f32[192]{0:T(256)S(1)}, u32[]{:S(2)}) copy-start(f32[192]{0:T(256)S(1)} %get-tuple-element.154) | copy-start | bytes 2308
  270.4 18.7 %collective-permute-start.10 = (bf16[128,1536]{1,0:T(8,128)(2,1)}, bf16[128,1536]{1,0:T(8,128)(2,1)}, u32[]{:S(2)}, u32[]{:S(2)}) collective-permute-start(bf16[128,1536]{1,0:T(8,128)(2,1)} %collective-permute-done.5), channel_id=1, source_target_pairs={{0,1},{1,0},{2,3},{3,2},{4,5},{5,4},{6,7},{7,6}} | collective-permute-start | bytes 1179656 | tf_op jit(solution)/shard_map/ppermute | solution.py:529
  283.5 251.1 %copy-start.40 = (f32[192]{0:T(256)}, f32[192]{0:T(256)S(1)}, u32[]{:S(2)}) copy-start(f32[192]{0:T(256)S(1)} %fusion.117) | copy-start | bytes 2308
  283.5 7.6 %collective-permute-start.7 = (bf16[1536,256]{1,0:T(8,128)(2,1)}, bf16[1536,256]{1,0:T(8,128)(2,1)S(1)}, u32[]{:S(2)}, u32[]{:S(2)}) collective-permute-start(bf16[1536,256]{1,0:T(8,128)(2,1)} %collective-permute-done.3), channel_id=1, source_target_pairs={{0,1},{1,0},{2,3},{3,2},{4,5},{5,4},{6,7},{7,6}} | collective-permute-start | bytes 2359304 | tf_op jit(solution)/shard_map/ppermute | solution.py:528
  283.7 4.4 copy-start.15
  287.7 213.1 %collective-permute-start.12 = (f32[504,1536]{1,0:T(8,128)}, f32[504,1536]{1,0:T(8,128)}, u32[]{:S(2)}, u32[]{:S(2)}) collective-permute-start(f32[504,1536]{1,0:T(8,128)} %get-tuple-element.101), channel_id=1, source_target_pairs={{0,4},{4,0},{1,5},{5,1},{2,6},{6,2},{3,7},{7,3}} | collective-permute-start | bytes 9289736 | tf_op jit(solution)/shard_map/ppermute | solution.py:466
  289.1 3.8 collective-permute-start.8
  291.2 4.4 copy-start.23
  291.2 178.2 %collective-permute-start.17 = (f32[504,1536]{1,0:T(8,128)S(1)}, f32[504,1536]{1,0:T(8,128)S(1)}, u32[]{:S(2)}, u32[]{:S(2)}) collective-permute-start(f32[504,1536]{1,0:T(8,128)S(1)} %copy-done.52), channel_id=1, source_target_pairs={{0,4},{4,0},{1,5},{5,1},{2,6},{6,2},{3,7},{7,3}} | collective-permute-start | bytes 9289736 | tf_op jit(solution)/shard_map/ppermute | solution.py:579
  295.6 42.4 %copy-start.14 = (f32[504,1536]{1,0:T(8,128)S(1)}, f32[504,1536]{1,0:T(8,128)}, u32[]{:S(2)}) copy-start(f32[504,1536]{1,0:T(8,128)} %get-tuple-element.106) | copy-start | bytes 9289732
  340.7 128.8 %copy-start.13 = (f32[504,1536]{1,0:T(8,128)S(1)}, f32[504,1536]{1,0:T(8,128)}, u32[]{:S(2)}) copy-start(f32[504,1536]{1,0:T(8,128)} %get-tuple-element.108) | copy-start | bytes 9289732
  343.3 202.8 %collective-permute-start.14 = (bf16[168,1536]{1,0:T(8,128)(2,1)}, bf16[168,1536]{1,0:T(8,128)(2,1)}, u32[]{:S(2)}, u32[]{:S(2)}) collective-permute-start(bf16[168,1536]{1,0:T(8,128)(2,1)} %convolution_convert_fusion.8), channel_id=1, source_target_pairs={{0,2},{1,3},{2,0},{3,1},{4,6},{5,7},{6,4},{7,5}} | collective-permute-start | bytes 1548296 | tf_op jit(solution)/shard_map/ppermute | solution.py:600
  344.6 165.9 %collective-permute-start.15 = (bf16[168,1536]{1,0:T(8,128)(2,1)}, bf16[168,1536]{1,0:T(8,128)(2,1)}, u32[]{:S(2)}, u32[]{:S(2)}) collective-permute-start(bf16[168,1536]{1,0:T(8,128)(2,1)} %convolution_convert_fusion.7), channel_id=1, source_target_pairs={{0,1},{1,0},{2,3},{3,2},{4,5},{5,4},{6,7},{7,6}} | collective-permute-start | bytes 1548296 | tf_op jit(solution)/shard_map/ppermute | solution.py:600
  469.4 15.4 %collective-permute-start.16 = (bf16[168,1536]{1,0:T(8,128)(2,1)S(1)}, bf16[168,1536]{1,0:T(8,128)(2,1)}, u32[]{:S(2)}, u32[]{:S(2)}) collective-permute-start(bf16[168,1536]{1,0:T(8,128)(2,1)S(1)} %convolution_convert_fusion.6), channel_id=1, source_target_pairs={{0,3},{1,2},{2,1},{3,0},{4,7},{5,6},{6,5},{7,4}} | collective-permute-start | bytes 1548296 | tf_op jit(solution)/shard_map/ppermute | solution.py:600
  474.1 7.3 %copy-start.54 = (pred[192,672]{1,0:T(32,128)(4,1)S(1)}, pred[192,672]{1,0:T(32,128)(4,1)}, u32[]{:S(2)}) copy-start(pred[192,672]{1,0:T(32,128)(4,1)} %convolution_compare_fusion) | copy-start | bytes 387076
  474.1 41.6 %collective-permute-start.18 = (bf16[168,1536]{1,0:T(8,128)(2,1)}, bf16[168,1536]{1,0:T(8,128)(2,1)}, u32[]{:S(2)}, u32[]{:S(2)}) collective-permute-start(bf16[168,1536]{1,0:T(8,128)(2,1)} %convolution_convert_fusion.5), channel_id=1, source_target_pairs={{0,2},{1,3},{2,0},{3,1},{4,6},{5,7},{6,4},{7,5}} | collective-permute-start | bytes 1548296 | tf_op jit(solution)/shard_map/ppermute | solution.py:600
  477.9 22.9 %all-to-all-start.1 = ((bf16[4,48,1536]{2,1,0:T(8,128)(2,1)}), bf16[4,48,1536]{2,1,0:T(8,128)(2,1)S(1)}, u32[]{:S(2)}, u32[]{:S(2)}) async-start(bf16[4,48,1536]{2,1,0:T(8,128)(2,1)} %bitcast.93), calls=%async_computation.1 | async-start | bytes 1179648 | tf_op jit(solution)/shard_map/all_to_all | solution.py:519
  484.9 28.4 %collective-permute-start.19 = (bf16[168,1536]{1,0:T(8,128)(2,1)}, bf16[168,1536]{1,0:T(8,128)(2,1)S(1)}, u32[]{:S(2)}, u32[]{:S(2)}) collective-permute-start(bf16[168,1536]{1,0:T(8,128)(2,1)} %convolution_convert_fusion.4), channel_id=1, source_target_pairs={{0,1},{1,0},{2,3},{3,2},{4,5},{5,4},{6,7},{7,6}} | collective-permute-start | bytes 1548296 | tf_op jit(solution)/shard_map/ppermute | solution.py:600
  500.8 57.1 %collective-permute-start.20 = (bf16[168,1536]{1,0:T(8,128)(2,1)}, bf16[168,1536]{1,0:T(8,128)(2,1)}, u32[]{:S(2)}, u32[]{:S(2)}) collective-permute-start(bf16[168,1536]{1,0:T(8,128)(2,1)} %convolution_convert_fusion.3), channel_id=1, source_target_pairs={{0,3},{1,2},{2,1},{3,0},{4,7},{5,6},{6,5},{7,4}} | collective-permute-start | bytes 1548296 | tf_op jit(solution)/shard_map/ppermute | solution.py:600
  505.9 26.1 %all-to-all-start.2 = ((bf16[4,128,1536]{2,1,0:T(8,128)(2,1)}), bf16[4,128,1536]{2,1,0:T(8,128)(2,1)}, u32[]{:S(2)}, u32[]{:S(2)}) async-start(bf16[4,128,1536]{2,1,0:T(8,128)(2,1)} %bitcast.12), calls=%async_computation.2 | async-start | bytes 3145728 | tf_op jit(solution)/shard_map/all_to_all | solution.py:519
  535.5 34.1 %collective-permute-start.22 = (f32[192,64]{0,1:T(8,128)S(1)}, f32[192,64]{0,1:T(8,128)S(1)}, u32[]{:S(2)}, u32[]{:S(2)}) collective-permute-start(f32[192,64]{0,1:T(8,128)S(1)} %get-tuple-element.120), channel_id=1, source_target_pairs={{0,4},{4,0},{1,5},{5,1},{2,6},{6,2},{3,7},{7,3}} | collective-permute-start | bytes 147464 | tf_op jit(solution)/shard_map/ppermute | solution.py:577
  552.4 5.5 copy-start.11
  552.4 5.5 copy-start.50
  557.9 5.9 %copy-start.57 = (f32[192,512]{1,0:T(8,128)S(1)}, f32[192,512]{1,0:T(8,128)}, u32[]{:S(2)}) copy-start(f32[192,512]{1,0:T(8,128)} %copy-done.55) | copy-start | bytes 1179652
  569.7 6.1 %collective-permute-start.24 = (f32[2,192,64]{1,2,0:T(8,128)S(1)}, f32[2,192,64]{1,2,0:T(8,128)S(1)}, u32[]{:S(2)}, u32[]{:S(2)}) collective-permute-start(f32[2,192,64]{1,2,0:T(8,128)S(1)} %maximum_select_fusion.1), channel_id=1, source_target_pairs={{0,1},{1,0},{2,3},{3,2},{4,5},{5,4},{6,7},{7,6}} | collective-permute-start | bytes 294920 | tf_op jit(solution)/shard_map/ppermute | solution.py:435
  569.7 5.9 %collective-permute-start.23 = (f32[2,192,64]{1,2,0:T(8,128)S(1)}, f32[2,192,64]{1,2,0:T(8,128)S(1)}, u32[]{:S(2)}, u32[]{:S(2)}) collective-permute-start(f32[2,192,64]{1,2,0:T(8,128)S(1)} %maximum_select_fusion.1), channel_id=1, source_target_pairs={{0,2},{1,3},{2,0},{3,1},{4,6},{5,7},{6,4},{7,5}} | collective-permute-start | bytes 294920 | tf_op jit(solution)/shard_map/ppermute | solution.py:434
  575.7 1.4 collective-permute-start.25
  (39 other events, 91.0 us)

commit v5 on v4

--- a/solution.py
+++ b/solution.py
@@ -276,6 +276,29 @@
     )(x_all, dy_all, ws_gate, ws_up, ws_down)
 
 
+def last_join_kernel(hits_ref, recv_ref, own_ref, sum_ref, out_ref):
+    rows = (recv_ref[...] + own_ref[...]).astype(BF16)
+    out_ref[...] = (sum_ref[...] + dot(hits_ref[...], rows)).astype(out_ref.dtype)
+
+
+def last_join(hits, recv, own, dx_sum, block=256):
+    tok, slots = hits.shape
+    model = recv.shape[1]
+    part = pl.BlockSpec((slots, block), lambda i: (0, i))
+    token = pl.BlockSpec((tok, block), lambda i: (0, i))
+    return pl.pallas_call(
+        last_join_kernel,
+        grid=(model // block,),
+        in_specs=[pl.BlockSpec((tok, slots), lambda i: (0, 0)), part, part, token],
+        out_specs=token,
+        out_shape=jax.ShapeDtypeStruct((tok, model), BF16),
+        cost_estimate=pl.CostEstimate(
+            flops=2 * tok * slots * model, bytes_accessed=8 * slots * model + 6 * tok * model, transcendentals=0),
+        compiler_params=pltpu.CompilerParams(dimension_semantics=('arbitrary',)),
+        name='last_join',
+    )(hits, recv, own, dx_sum)
+
+
 def split3(v):
     hi = lax.reduce_precision(v, 8, 7)
     rest = v - hi
@@ -602,8 +625,8 @@
                 dx_sum = dx_sum + dot(hits, back)
             dx_sum = lax.optimization_barrier(dx_sum)
         recv, own = bwd_parts[-1]
-        dx_sum = dx_sum + dot(hits_of(ep_i, 0, local_exp), (recv + own).astype(BF16))
-        return y_out, dx_sum.astype(BF16), d_router, d_w_gate, d_w_up, d_w_down, ds_gate, ds_up, ds_down
+        dx = last_join(hits_of(ep_i, 0, local_exp), recv, own, dx_sum)
+        return y_out, dx, d_router, d_w_gate, d_w_up, d_w_down, ds_gate, ds_up, ds_down
 
     tok_spec = P(('ep', 'tp'), None)
     in_specs = (tok_spec, tok_spec, P(None, None), P('ep', None, 'tp'), P('ep', None, 'tp'), P('ep', 'tp', None), P(None, 'tp'), P(None, 'tp'), P('tp', None), tok_spec)

time: 584 us -> 536 us (0.918)
  waiting for transfers between devices: 197 us -> 151 us
    ppermute x1, waiting for transfers between devices: 40.6 us -> 0.16 us  [device_step(): bwd_parts = [(lax.ppermute(bwd_out[0][0], 'tp', swap_tp), bwd_out[0][1])]]
    all_to_all x3, waiting for transfers between devices: 25.1 us -> 14.3 us  [send_home(): out = lax.all_to_all(out, 'ep', 0, 0)]
    unnamed x119 -> x101, local copies, waits for them, and re-layouts: 12.6 us -> 13 us
  transfers between devices with their start and end apart: 29 -> 29, of which waited for: 6 -> 7; matrix products, arithmetic and copies ran while one was open for 21% -> 21% of each run, Pallas kernels for 31% -> 35%
where the time goes in v5:
time: 536 us; the launch traced here: 534 us
  Pallas kernels  226 us (42%)
  waiting for transfers between devices  151 us (28%)
  matrix products  88.5 us (17%)
  starting transfers between devices  30.4 us (6%)
  local copies, waits for them, and re-layouts  29.6 us (6%)
  other arithmetic  7.2 us (1%)
    ppermute x2, waiting for transfers between devices, device_step(): bwd_parts.append((lax.ppermute(send, 'tp', swap_tp), own))  126 us
    pallas_call x1, Pallas kernels, expert_bwd(): pl.pallas_call(functools.partial(bwd_kernel, sizes, per_chunk), grid=(cou...  105 us
    dot_general x44, matrix products, dot(): return lax.dot_general(a, b, dims, preferred_element_type=F32)  84.4 us
    pallas_call x3, Pallas kernels, expert_fwd(): pl.pallas_call(functools.partial(fwd_kernel, half, padded), grid=(count,)...  49.5 us
    pallas_call x1, Pallas kernels, gather_rows(): pl.pallas_call(gather_kernel, in_specs=[any_spec] * 6, out_specs=[any_spe...  41 us
    pallas_call x1, Pallas kernels, shared_grad(): pl.pallas_call(functools.partial(shared_grad_kernel, 256), grid=(width //...  25.7 us
    all_to_all x3, waiting for transfers between devices, send_home(): out = lax.all_to_all(out, 'ep', 0, 0)  14.3 us
    unnamed x101, local copies, waits for them, and re-layouts  13 us
  transfers between devices with their start and end apart: 29, of which 7 were waited for; matrix products, arithmetic and copies ran while one was open for 21% of the time, Pallas kernels for 35%

profile of v5, /device:TPU:0, one launch (start us, length us, event | category | flops | bytes accessed | tf_op | source)
XLA Modules:
  0.0 534.2 jit_solution(6548373961094214026)
XLA Ops:
  0.7 41.0 %gather_rows.1 = (bf16[8,192,1536]{2,1,0:T(8,128)(2,1)}, s32[8,6,192]{2,1,0:T(8,128)}, bf16[2,192,1536]{2,1,0:T(8,128)(2,1)}, bf16[128,1536]{1,0:T(8,128)(2,1)}, bf16[1536,256]{1,0:T(8,128)(2,1)}) custom-call(bf16[192,1536]{1,0:T(8,128)(2,1)} %x_ref.1, s32[6,192]{1,0:T(8,128)} %bitcast.101, bf16[192,1536]{1,0:T(8,128)(2,1)} %dy_ref.1, ...), custom_call_target="tpu_custom_call" | custom-call | flops 60000002048 | bytes 9437184 | tf_op jit(solution)/shard_map/gather_rows/pallas_call | solution.py:407
  42.2 1.5 collective-permute-start.5
  46.6 8.8 %shard_map.169 = (f32[168,1536]{1,0:T(8,128)}, f32[168,1536]{1,0:T(8,128)S(1)}) custom-call(bf16[1536,1536]{1,0:T(8,128)(2,1)} %bitcast.84, s32[16,1,1536]{2,1,0:T(1,128)S(1)} %reshape.612.row_ref, bf16[16,1536,256]{2,1,0:T(8,128)(2,1)} %w1_ref.7, bf16[16,1536,256]{2,1,0:T(8,128)(2,1)} %w3_ref.7, bf16[16,256,1536]{2,1,0:T(8,128)(2,1)} %w2_ref.7), custom_call_target="tpu_custom_call" | custom-call | flops 2491416576 | bytes 11501568 | tf_op jit(solution)/shard_map/pallas_call | solution.py:166
  58.3 22.3 %shard_map.170 = (f32[672,1536]{1,0:T(8,128)S(1)}, f32[672,1536]{1,0:T(8,128)}) custom-call(bf16[1536,1536]{1,0:T(8,128)(2,1)} %bitcast.85, s32[16,1,1536]{2,1,0:T(1,128)S(1)} %reshape.612.row_ref, bf16[16,1536,256]{2,1,0:T(8,128)(2,1)} %w1_ref.7, bf16[16,1536,256]{2,1,0:T(8,128)(2,1)} %w3_ref.7, bf16[16,256,1536]{2,1,0:T(8,128)(2,1)} %w2_ref.7), custom_call_target="tpu_custom_call" | custom-call | flops 9965666304 | bytes 31850496 | tf_op jit(solution)/shard_map/pallas_call | solution.py:166
  80.6 1.9 copy-done.7
  82.6 18.3 %shard_map.171 = (f32[504,1536]{1,0:T(8,128)}, f32[504,1536]{1,0:T(8,128)}) custom-call(bf16[1536,1536]{1,0:T(8,128)(2,1)} %bitcast.86, s32[16,1,1536]{2,1,0:T(1,128)S(1)} %reshape.612.row_ref, bf16[16,1536,256]{2,1,0:T(8,128)(2,1)} %w1_ref.7, bf16[16,1536,256]{2,1,0:T(8,128)(2,1)} %w3_ref.7, bf16[16,256,1536]{2,1,0:T(8,128)(2,1)} %w2_ref.7), custom_call_target="tpu_custom_call" | custom-call | flops 7474249728 | bytes 25067520 | tf_op jit(solution)/shard_map/pallas_call | solution.py:166
  100.9 3.9 fusion.225
  105.0 2.6 broadcast_in_dim.97
  115.9 2.4 bitcast_dynamic-update-slice_fusion
  118.3 104.6 %expert_bwd.1 = (f32[16,1536,256]{2,1,0:T(8,128)}, f32[16,1536,256]{2,1,0:T(8,128)}, f32[16,256,1536]{2,1,0:T(8,128)}, f32[504,1536]{1,0:T(8,128)}, f32[504,1536...) custom-call(bf16[1536,1536]{1,0:T(8,128)(2,1)} %bitcast.88, ...), custom_call_target="tpu_custom_call" | custom-call | flops 52344913920 | bytes 143130624 | tf_op jit(solution)/shard_map/expert_bwd/pallas_call | solution.py:197
  224.8 25.7 %shared_grad.1 = (f32[1536,512]{1,0:T(8,128)}, f32[1536,512]{1,0:T(8,128)}, f32[512,1536]{1,0:T(8,128)}) custom-call(bf16[1536,1536]{1,0:T(8,128)(2,1)} %bitcast.89, bf16[1536,1536]{1,0:T(8,128)(2,1)} %bitcast.6.dy_ref, bf16[1536,512]{1,0:T(8,128)(2,1)S(1)} %copy-done.2, bf16[1536,512]{1,0:T(8,128)(2,1)S(1)} %copy-done.3, bf16[512,1536]{1,0:T(8,128)(2,1)S(1)} %copy-done.1), custom_call_target="tpu_custom_call" | custom-call | flops 14495514624 | bytes 23592960 | tf_op jit(solution)/shard_map/shared_grad/pallas_call | solution.py:264
  250.5 5.3 %convolution_convert_fusion = bf16[672,1536]{1,0:T(8,128)(2,1)} fusion(f32[672,1536]{1,0:T(8,128)} %collective-permute-done.6, f32[672,1536]{1,0:T(8,128)S(1)} %copy-done.38, s32[672]{0:T(1024)S(1)} %add_select_fusion.7), kind=kOutput, calls=%fused_computation.1 | convolution fusion | flops 1390814208 | bytes 10324608 | tf_op jit(solution)/shard_map/dot_general | solution.py:25
  258.3 2.0 fusion.221
  260.8 1.8 constant_dynamic-update-slice_fusion.3
  262.6 4.8 all-to-all-start
  269.0 1.8 fusion.22
  272.3 1.5 fusion.74
  275.3 1.7 convolution_add_fusion.2
  280.4 1.6 collective-permute-start.12
  283.8 1.8 copy-done.39
  287.3 1.6 collective-permute-start.13
  291.3 1.7 fusion.65
  293.6 2.3 add_convert_fusion.2
  297.2 1.6 collective-permute-start.15
  299.3 126.5 %collective-permute-done.18 = f32[504,1536]{1,0:T(8,128)S(1)} collective-permute-done((f32[504,1536]{1,0:T(8,128)S(1)}, f32[504,1536]{1,0:T(8,128)S(1)}, u32[]{:S(2)}, u32[]{:S(2)}) %collective-permute-start.18) | collective-permute-done | bytes 3096608 | tf_op jit(solution)/shard_map/ppermute | solution.py:602
  433.1 2.4 convolution_convert_fusion.2
  435.5 3.5 all-to-all-start.1
  439.0 2.4 reduce-precision_convert_fusion.1
  442.5 3.0 collective-permute-done.17
  446.7 1.6 fusion.28
  448.3 4.6 all-to-all-done.1
  452.9 5.0 convolution_convert_fusion.1
  458.0 4.6 all-to-all-start.2
  464.1 2.7 fusion.27
  466.7 1.6 fusion.30
  468.4 2.7 fusion.29
  473.4 9.7 %all-to-all-done.2 = bf16[4,128,1536]{2,1,0:T(8,128)(2,1)} async-done(((bf16[4,128,1536]{2,1,0:T(8,128)(2,1)}), bf16[4,128,1536]{2,1,0:T(8,128)(2,1)}, u32[]{:S(2)}, u32[]{:S(2)}) %all-to-all-start.2) | async-done | bytes 1572896 | tf_op jit(solution)/shard_map/all_to_all | solution.py:542
  483.0 2.3 reduce-precision_convert_fusion.5
  488.6 1.8 fusion.4
  490.3 3.4 fusion.1
  493.7 2.7 fusion.24
  496.5 4.6 fusion.8
  501.1 5.3 fusion.7
  506.4 6.7 %fusion.5 = bf16[192,1536]{1,0:T(8,128)(2,1)} fusion(f32[192,1536]{1,0:T(8,128)} %fusion.74, bf16[512,1536]{1,0:T(8,128)(2,1)} %copy-done.16, f32[576,1536]{1,0:T(8,128)} %fusion.8, f32[576,1536]{1,0:T(8,128)} %fusion.24, f32[576,1536]{1,0:T(8,128)} %fusion.7, f32[192,512]{1,0:T(8,128)} %fusion.21, f32[192,512]{1,0:T(8,128)S(1)} %copy-done.46), kind=kOutput, calls=%fused_computation.15 | convolution fusion | flops 306216960 | bytes 14745600 | tf_op jit(solution)/shard_map/dot_general | solution.py:25
  513.0 3.1 add_add_fusion.sum_ref
  516.1 5.7 %last_join.1 = bf16[192,1536]{1,0:T(8,128)(2,1)} custom-call(bf16[192,336]{1,0:T(8,128)(2,1)} %fusion.25.hits_ref, f32[336,1536]{1,0:T(8,128)} %collective-permute-done.13.recv_ref, f32[336,1536]{1,0:T(8,128)} %get-tuple-element.105.own_ref, f32[192,1536]{1,0:T(8,128)} %add_add_fusion.sum_ref), custom_call_target="tpu_custom_call" | custom-call | flops 198180864 | bytes 5898240 | tf_op jit(solution)/shard_map/last_join/pallas_call | solution.py:289
  522.3 5.5 %collective-permute-done.23 = f32[2,192,64]{1,2,0:T(8,128)S(1)} collective-permute-done((f32[2,192,64]{1,2,0:T(8,128)S(1)}, f32[2,192,64]{1,2,0:T(8,128)S(1)}, u32[]{:S(2)}, u32[]{:S(2)}) %collective-permute-start.23) | collective-permute-done | bytes 98336 | tf_op jit(solution)/shard_map/ppermute | solution.py:457
  530.0 3.4 fusion.47
  (224 shorter events, 55.4 us)
Async XLA Ops:
  0.6 100.3 %copy-start = (bf16[1536,64]{0,1:T(8,128)(2,1)S(1)}, bf16[1536,64]{0,1:T(8,128)(2,1)}, u32[]{:S(2)}) copy-start(bf16[1536,64]{0,1:T(8,128)(2,1)} %param.12) | copy-start | bytes 589828
  41.6 72.6 %collective-permute-start.1 = (bf16[2,192,1536]{2,1,0:T(8,128)(2,1)}, bf16[2,192,1536]{2,1,0:T(8,128)(2,1)S(1)}, u32[]{:S(2)}, u32[]{:S(2)}) collective-permute-start(bf16[2,192,1536]{2,1,0:T(8,128)(2,1)} %get-tuple-element.65), channel_id=1, source_target_pairs={{0,1},{1,0},{2,3},{3,2},{4,5},{5,4},{6,7},{7,6}} | collective-permute-start | bytes 3538952 | tf_op jit(solution)/shard_map/ppermute | solution.py:458
  41.7 67.8 %collective-permute-start = (bf16[2,192,1536]{2,1,0:T(8,128)(2,1)}, bf16[2,192,1536]{2,1,0:T(8,128)(2,1)S(1)}, u32[]{:S(2)}, u32[]{:S(2)}) collective-permute-start(bf16[2,192,1536]{2,1,0:T(8,128)(2,1)} %get-tuple-element.65), channel_id=1, source_target_pairs={{0,2},{1,3},{2,0},{3,1},{4,6},{5,7},{6,4},{7,5}} | collective-permute-start | bytes 3538952 | tf_op jit(solution)/shard_map/ppermute | solution.py:457
  42.2 180.7 %collective-permute-start.5 = (bf16[128,1536]{1,0:T(8,128)(2,1)}, bf16[128,1536]{1,0:T(8,128)(2,1)}, u32[]{:S(2)}, u32[]{:S(2)}) collective-permute-start(bf16[128,1536]{1,0:T(8,128)(2,1)} %get-tuple-element.93), channel_id=1, source_target_pairs={{0,2},{1,3},{2,0},{3,1},{4,6},{5,7},{6,4},{7,5}} | collective-permute-start | bytes 1179656 | tf_op jit(solution)/shard_map/ppermute | solution.py:518
  43.7 69.1 %collective-permute-start.3 = (bf16[1536,256]{1,0:T(8,128)(2,1)}, bf16[1536,256]{1,0:T(8,128)(2,1)}, u32[]{:S(2)}, u32[]{:S(2)}) collective-permute-start(bf16[1536,256]{1,0:T(8,128)(2,1)} %get-tuple-element.74), channel_id=1, source_target_pairs={{0,4},{4,0},{1,5},{5,1},{2,6},{6,2},{3,7},{7,3}} | collective-permute-start | bytes 2359304 | tf_op jit(solution)/shard_map/ppermute | solution.py:470
  56.4 375.3 %collective-permute-start.11 = (f32[168,1536]{1,0:T(8,128)}, f32[168,1536]{1,0:T(8,128)}, u32[]{:S(2)}, u32[]{:S(2)}) collective-permute-start(f32[168,1536]{1,0:T(8,128)} %get-tuple-element.98), channel_id=1, source_target_pairs={{0,4},{4,0},{1,5},{5,1},{2,6},{6,2},{3,7},{7,3}} | collective-permute-start | bytes 3096584 | tf_op jit(solution)/shard_map/ppermute | solution.py:489
  109.4 6.5 %collective-permute-start.2 = (bf16[2,192,1536]{2,1,0:T(8,128)(2,1)S(1)}, bf16[2,192,1536]{2,1,0:T(8,128)(2,1)}, u32[]{:S(2)}, u32[]{:S(2)}) collective-permute-start(bf16[2,192,1536]{2,1,0:T(8,128)(2,1)S(1)} %collective-permute-done), channel_id=1, source_target_pairs={{0,1},{1,0},{2,3},{3,2},{4,5},{5,4},{6,7},{7,6}} | collective-permute-start | bytes 3538952 | tf_op jit(solution)/shard_map/ppermute | solution.py:458
  112.8 137.7 %collective-permute-start.6 = (f32[672,1536]{1,0:T(8,128)}, f32[672,1536]{1,0:T(8,128)}, u32[]{:S(2)}, u32[]{:S(2)}) collective-permute-start(f32[672,1536]{1,0:T(8,128)} %copy-done.7), channel_id=1, source_target_pairs={{0,4},{4,0},{1,5},{5,1},{2,6},{6,2},{3,7},{7,3}} | collective-permute-start | bytes 12386312 | tf_op jit(solution)/shard_map/ppermute | solution.py:489
  114.2 108.7 %collective-permute-start.4 = (bf16[1536,256]{1,0:T(8,128)(2,1)}, bf16[1536,256]{1,0:T(8,128)(2,1)}, u32[]{:S(2)}, u32[]{:S(2)}) collective-permute-start(bf16[1536,256]{1,0:T(8,128)(2,1)} %collective-permute-done.3), channel_id=1, source_target_pairs={{0,2},{1,3},{2,0},{3,1},{4,6},{5,7},{6,4},{7,5}} | collective-permute-start | bytes 2359304 | tf_op jit(solution)/shard_map/ppermute | solution.py:517
  118.3 105.0 %copy-start.1 = (bf16[512,1536]{1,0:T(8,128)(2,1)S(1)}, bf16[512,1536]{1,0:T(8,128)(2,1)}, u32[]{:S(2)}) copy-start(bf16[512,1536]{1,0:T(8,128)(2,1)} %wd_ref.3) | copy-start | bytes 4718596
  118.3 105.0 %copy-start.2 = (bf16[1536,512]{1,0:T(8,128)(2,1)S(1)}, bf16[1536,512]{1,0:T(8,128)(2,1)}, u32[]{:S(2)}) copy-start(bf16[1536,512]{1,0:T(8,128)(2,1)} %wg_ref.3) | copy-start | bytes 4718596
  222.9 70.3 %collective-permute-start.14 = (f32[504,1536]{1,0:T(8,128)}, f32[504,1536]{1,0:T(8,128)}, u32[]{:S(2)}, u32[]{:S(2)}) collective-permute-start(f32[504,1536]{1,0:T(8,128)} %get-tuple-element.107), channel_id=1, source_target_pairs={{0,4},{4,0},{1,5},{5,1},{2,6},{6,2},{3,7},{7,3}} | collective-permute-start | bytes 9289736 | tf_op jit(solution)/shard_map/ppermute | solution.py:513
  224.8 25.7 %copy-start.38 = (f32[672,1536]{1,0:T(8,128)S(1)}, f32[672,1536]{1,0:T(8,128)}, u32[]{:S(2)}) copy-start(f32[672,1536]{1,0:T(8,128)} %get-tuple-element.89) | copy-start | bytes 12386308
  250.5 5.4 %copy-start.9 = (bf16[192,1536]{1,0:T(8,128)(2,1)S(1)}, bf16[192,1536]{1,0:T(8,128)(2,1)}, u32[]{:S(2)}) copy-start(bf16[192,1536]{1,0:T(8,128)(2,1)} %x_ref.1) | copy-start | bytes 1769476
  260.3 23.5 %collective-permute-start.7 = (bf16[1536,256]{1,0:T(8,128)(2,1)}, bf16[1536,256]{1,0:T(8,128)(2,1)}, u32[]{:S(2)}, u32[]{:S(2)}) collective-permute-start(bf16[1536,256]{1,0:T(8,128)(2,1)} %collective-permute-done.3), channel_id=1, source_target_pairs={{0,1},{1,0},{2,3},{3,2},{4,5},{5,4},{6,7},{7,6}} | collective-permute-start | bytes 2359304 | tf_op jit(solution)/shard_map/ppermute | solution.py:551
  260.6 19.8 %collective-permute-start.9 = (bf16[128,1536]{1,0:T(8,128)(2,1)}, bf16[128,1536]{1,0:T(8,128)(2,1)}, u32[]{:S(2)}, u32[]{:S(2)}) collective-permute-start(bf16[128,1536]{1,0:T(8,128)(2,1)} %get-tuple-element.93), channel_id=1, source_target_pairs={{0,1},{1,0},{2,3},{3,2},{4,5},{5,4},{6,7},{7,6}} | collective-permute-start | bytes 1179656 | tf_op jit(solution)/shard_map/ppermute | solution.py:552
  262.6 4.8 copy-start.33
  262.6 169.1 %all-to-all-start = ((bf16[4,168,1536]{2,1,0:T(8,128)(2,1)}), bf16[4,168,1536]{2,1,0:T(8,128)(2,1)}, u32[]{:S(2)}, u32[]{:S(2)}) async-start(bf16[4,168,1536]{2,1,0:T(8,128)(2,1)} %bitcast.93), calls=%async_computation | async-start | bytes 4128768 | tf_op jit(solution)/shard_map/all_to_all | solution.py:542
  270.8 12.2 %collective-permute-start.10 = (bf16[128,1536]{1,0:T(8,128)(2,1)}, bf16[128,1536]{1,0:T(8,128)(2,1)S(1)}, u32[]{:S(2)}, u32[]{:S(2)}) collective-permute-start(bf16[128,1536]{1,0:T(8,128)(2,1)} %collective-permute-done.5), channel_id=1, source_target_pairs={{0,1},{1,0},{2,3},{3,2},{4,5},{5,4},{6,7},{7,6}} | collective-permute-start | bytes 1179656 | tf_op jit(solution)/shard_map/ppermute | solution.py:552
  272.3 16.6 %copy-start.24 = (bf16[1536,128]{1,0:T(8,128)(2,1)}, bf16[1536,128]{1,0:T(8,128)(2,1)S(1)}, u32[]{:S(2)}) copy-start(bf16[1536,128]{1,0:T(8,128)(2,1)S(1)} %get-tuple-element.127) | copy-start | bytes 1179652
  278.3 160.7 %copy-start.42 = (pred[192,672]{1,0:T(32,128)(4,1)}, pred[192,672]{1,0:T(32,128)(4,1)S(1)}, u32[]{:S(2)}) copy-start(pred[192,672]{1,0:T(32,128)(4,1)S(1)} %convolution_compare_fusion) | copy-start | bytes 387076
  278.3 4.8 copy-start.17
  280.4 172.5 %collective-permute-start.12 = (f32[504,1536]{1,0:T(8,128)}, f32[504,1536]{1,0:T(8,128)}, u32[]{:S(2)}, u32[]{:S(2)}) collective-permute-start(f32[504,1536]{1,0:T(8,128)} %get-tuple-element.101), channel_id=1, source_target_pairs={{0,4},{4,0},{1,5},{5,1},{2,6},{6,2},{3,7},{7,3}} | collective-permute-start | bytes 9289736 | tf_op jit(solution)/shard_map/ppermute | solution.py:489
  283.1 4.2 collective-permute-start.8
  283.1 4.1 copy-start.16
  283.8 7.5 %copy-start.20 = (f32[192,512]{1,0:T(8,128)}, f32[192,512]{1,0:T(8,128)S(1)}, u32[]{:S(2)}) copy-start(f32[192,512]{1,0:T(8,128)S(1)} %fusion.23) | copy-start | bytes 1179652
  285.6 3.3 copy-start.22
  285.6 140.2 %collective-permute-start.18 = (f32[504,1536]{1,0:T(8,128)S(1)}, f32[504,1536]{1,0:T(8,128)S(1)}, u32[]{:S(2)}, u32[]{:S(2)}) collective-permute-start(f32[504,1536]{1,0:T(8,128)S(1)} %copy-done.39), channel_id=1, source_target_pairs={{0,4},{4,0},{1,5},{5,1},{2,6},{6,2},{3,7},{7,3}} | collective-permute-start | bytes 9289736 | tf_op jit(solution)/shard_map/ppermute | solution.py:602
  287.3 228.8 %collective-permute-start.13 = (f32[336,1536]{1,0:T(8,128)}, f32[336,1536]{1,0:T(8,128)}, u32[]{:S(2)}, u32[]{:S(2)}) collective-permute-start(f32[336,1536]{1,0:T(8,128)} %get-tuple-element.104), channel_id=1, source_target_pairs={{0,4},{4,0},{1,5},{5,1},{2,6},{6,2},{3,7},{7,3}} | collective-permute-start | bytes 6193160 | tf_op jit(solution)/shard_map/ppermute | solution.py:602
  295.9 129.9 %copy-start.13 = (f32[504,1536]{1,0:T(8,128)S(1)}, f32[504,1536]{1,0:T(8,128)}, u32[]{:S(2)}) copy-start(f32[504,1536]{1,0:T(8,128)} %get-tuple-element.110) | copy-start | bytes 9289732
  297.2 193.1 %collective-permute-start.15 = (bf16[168,1536]{1,0:T(8,128)(2,1)}, bf16[168,1536]{1,0:T(8,128)(2,1)}, u32[]{:S(2)}, u32[]{:S(2)}) collective-permute-start(bf16[168,1536]{1,0:T(8,128)(2,1)} %convolution_convert_fusion.8), channel_id=1, source_target_pairs={{0,2},{1,3},{2,0},{3,1},{4,6},{5,7},{6,4},{7,5}} | collective-permute-start | bytes 1548296 | tf_op jit(solution)/shard_map/ppermute | solution.py:623
  425.8 36.8 %collective-permute-start.16 = (bf16[168,1536]{1,0:T(8,128)(2,1)S(1)}, bf16[168,1536]{1,0:T(8,128)(2,1)}, u32[]{:S(2)}, u32[]{:S(2)}) collective-permute-start(bf16[168,1536]{1,0:T(8,128)(2,1)S(1)} %convolution_convert_fusion.7), channel_id=1, source_target_pairs={{0,1},{1,0},{2,3},{3,2},{4,5},{5,4},{6,7},{7,6}} | collective-permute-start | bytes 1548296 | tf_op jit(solution)/shard_map/ppermute | solution.py:623
  429.1 4.0 copy-start.6
  431.7 13.9 %collective-permute-start.17 = (bf16[168,1536]{1,0:T(8,128)(2,1)}, bf16[168,1536]{1,0:T(8,128)(2,1)}, u32[]{:S(2)}, u32[]{:S(2)}) collective-permute-start(bf16[168,1536]{1,0:T(8,128)(2,1)} %convolution_convert_fusion.6), channel_id=1, source_target_pairs={{0,3},{1,2},{2,1},{3,0},{4,7},{5,6},{6,5},{7,4}} | collective-permute-start | bytes 1548296 | tf_op jit(solution)/shard_map/ppermute | solution.py:623
  435.5 17.4 %all-to-all-start.1 = ((bf16[4,48,1536]{2,1,0:T(8,128)(2,1)}), bf16[4,48,1536]{2,1,0:T(8,128)(2,1)S(1)}, u32[]{:S(2)}, u32[]{:S(2)}) async-start(bf16[4,48,1536]{2,1,0:T(8,128)(2,1)} %bitcast.10), calls=%async_computation.1 | async-start | bytes 1179648 | tf_op jit(solution)/shard_map/all_to_all | solution.py:542
  445.6 22.8 %collective-permute-start.19 = (bf16[168,1536]{1,0:T(8,128)(2,1)}, bf16[168,1536]{1,0:T(8,128)(2,1)}, u32[]{:S(2)}, u32[]{:S(2)}) collective-permute-start(bf16[168,1536]{1,0:T(8,128)(2,1)} %convolution_convert_fusion.5), channel_id=1, source_target_pairs={{0,2},{1,3},{2,0},{3,1},{4,6},{5,7},{6,4},{7,5}} | collective-permute-start | bytes 1548296 | tf_op jit(solution)/shard_map/ppermute | solution.py:623
  452.9 13.8 %collective-permute-start.20 = (bf16[168,1536]{1,0:T(8,128)(2,1)}, bf16[168,1536]{1,0:T(8,128)(2,1)}, u32[]{:S(2)}, u32[]{:S(2)}) collective-permute-start(bf16[168,1536]{1,0:T(8,128)(2,1)} %convolution_convert_fusion.4), channel_id=1, source_target_pairs={{0,1},{1,0},{2,3},{3,2},{4,5},{5,4},{6,7},{7,6}} | collective-permute-start | bytes 1548296 | tf_op jit(solution)/shard_map/ppermute | solution.py:623
  458.0 25.1 %all-to-all-start.2 = ((bf16[4,128,1536]{2,1,0:T(8,128)(2,1)}), bf16[4,128,1536]{2,1,0:T(8,128)(2,1)}, u32[]{:S(2)}, u32[]{:S(2)}) async-start(bf16[4,128,1536]{2,1,0:T(8,128)(2,1)} %bitcast.12), calls=%async_computation.2 | async-start | bytes 3145728 | tf_op jit(solution)/shard_map/all_to_all | solution.py:542
  462.6 50.4 %collective-permute-start.21 = (bf16[168,1536]{1,0:T(8,128)(2,1)}, bf16[168,1536]{1,0:T(8,128)(2,1)}, u32[]{:S(2)}, u32[]{:S(2)}) collective-permute-start(bf16[168,1536]{1,0:T(8,128)(2,1)} %convolution_convert_fusion.3), channel_id=1, source_target_pairs={{0,3},{1,2},{2,1},{3,0},{4,7},{5,6},{6,5},{7,4}} | collective-permute-start | bytes 1548296 | tf_op jit(solution)/shard_map/ppermute | solution.py:623
  485.9 35.9 %collective-permute-start.22 = (f32[192,64]{0,1:T(8,128)S(1)}, f32[192,64]{0,1:T(8,128)S(1)}, u32[]{:S(2)}, u32[]{:S(2)}) collective-permute-start(f32[192,64]{0,1:T(8,128)S(1)} %get-tuple-element.120), channel_id=1, source_target_pairs={{0,4},{4,0},{1,5},{5,1},{2,6},{6,2},{3,7},{7,3}} | collective-permute-start | bytes 147464 | tf_op jit(solution)/shard_map/ppermute | solution.py:600
  490.3 3.4 copy-start.35
  496.5 4.6 copy-start.43
  501.1 5.3 copy-start.46
  506.3 6.7 %copy-start.11 = (f32[192,1536]{1,0:T(8,128)S(1)}, f32[192,1536]{1,0:T(8,128)}, u32[]{:S(2)}) copy-start(f32[192,1536]{1,0:T(8,128)} %fusion.29) | copy-start | bytes 3538948
  506.3 6.7 %copy-start.37 = (s32[168]{0:T(256)S(1)}, s32[168]{0:T(256)}, u32[]{:S(2)}) copy-start(s32[168]{0:T(256)} %broadcast_add_fusion.1) | copy-start | bytes 2020
  521.8 6.1 %collective-permute-start.24 = (f32[2,192,64]{1,2,0:T(8,128)S(1)}, f32[2,192,64]{1,2,0:T(8,128)S(1)}, u32[]{:S(2)}, u32[]{:S(2)}) collective-permute-start(f32[2,192,64]{1,2,0:T(8,128)S(1)} %maximum_select_fusion.1), channel_id=1, source_target_pairs={{0,1},{1,0},{2,3},{3,2},{4,5},{5,4},{6,7},{7,6}} | collective-permute-start | bytes 294920 | tf_op jit(solution)/shard_map/ppermute | solution.py:458
  521.9 5.9 %collective-permute-start.23 = (f32[2,192,64]{1,2,0:T(8,128)S(1)}, f32[2,192,64]{1,2,0:T(8,128)S(1)}, u32[]{:S(2)}, u32[]{:S(2)}) collective-permute-start(f32[2,192,64]{1,2,0:T(8,128)S(1)} %maximum_select_fusion.1), channel_id=1, source_target_pairs={{0,2},{1,3},{2,0},{3,1},{4,6},{5,7},{6,4},{7,5}} | collective-permute-start | bytes 294920 | tf_op jit(solution)/shard_map/ppermute | solution.py:457
  527.9 1.4 collective-permute-start.25
  (30 other events, 61.5 us)

commit v6 on v4

--- a/solution.py
+++ b/solution.py
@@ -139,9 +139,11 @@
     def copies(c):
         out = []
         for side in range(2):
-            k = 2 * c + side
-            src = far_ref.at[k] if c < chunks else near_ref.at[side]
-            out.append(pltpu.make_async_copy(src.at[pl.ds(0, outs[k].shape[0])], outs[k], sem.at[k]))
+            for near in range(2):
+                k = 2 * (c + near * chunks) + side
+                rows = outs[k].shape[0]
+                src = near_ref.at[side, pl.ds(c * rows, rows)] if near else far_ref.at[2 * c + side, pl.ds(0, rows)]
+                out.append(pltpu.make_async_copy(src, outs[k], sem.at[k]))
         return out
 
     for c in range(chunks):
@@ -152,9 +154,7 @@
 
     @pl.when(e == chunks * per_chunk - 1)
     def _():
-        for copy in copies(chunks):
-            copy.start()
-        for c in range(chunks + 1):
+        for c in range(chunks):
             for copy in copies(c):
                 copy.wait()
 
@@ -189,10 +189,10 @@
     tokens, model = x_all.shape
     count, _, width = w_gate.shape
     per_chunk = count // chunks
-    far_rows, near_rows = per_chunk * other, count * own
+    far_rows, near_rows = per_chunk * other, per_chunk * own
     far_pad = max(j * other // 8 * 8 + win_other for j in range(per_chunk))
     near_pad = max(j * own // 8 * 8 + win_own for j in range(count))
-    part_shapes = [jax.ShapeDtypeStruct((far_rows, model), F32)] * (2 * chunks) + [jax.ShapeDtypeStruct((near_rows, model), F32)] * 2
+    part_shapes = [jax.ShapeDtypeStruct((n, model), F32) for n in (far_rows, near_rows) for _ in range(2 * chunks)]
     rows = 2 * (win_other + win_own)
     outs = pl.pallas_call(
         functools.partial(bwd_kernel, sizes, per_chunk),
@@ -232,7 +232,7 @@
         name='expert_bwd',
     )(x_all, dy_all, row_ids, gates, w_gate, w_up, w_down)
     parts = outs[3:]
-    return outs[:3], [(parts[2 * c], parts[2 * c + 1]) for c in range(chunks + 1)]
+    return outs[:3], [(parts[2 * c], parts[2 * c + 1]) for c in range(2 * chunks)]
 
 
 def shared_grad_kernel(step, x_ref, dy_ref, wg_ref, wu_ref, wd_ref, dg_ref, du_ref, dd_ref, h_ref, da_ref, db_ref):
@@ -590,7 +590,7 @@
             return (dot(want, table) == (slot % cap).astype(F32)[None, :]).astype(BF16)
 
         swaps = (swap_x, swap_c, [(i, core_partner(d)) for i, d in swap_x])
-        for c, (recv, own) in enumerate(bwd_parts[:-1]):
+        for c, (recv, own) in enumerate(bwd_parts[:BWD_CHUNKS]):
             rows = (recv + own).astype(BF16)
             slot = jnp.arange(per_chunk * cap, dtype=jnp.int32)
             for k, pairs in enumerate(swaps):
@@ -601,8 +601,11 @@
                 hits = hits_of(ep_order[1 + k], c * per_chunk, per_chunk)
                 dx_sum = dx_sum + dot(hits, back)
             dx_sum = lax.optimization_barrier(dx_sum)
-        recv, own = bwd_parts[-1]
-        dx_sum = dx_sum + dot(hits_of(ep_i, 0, local_exp), (recv + own).astype(BF16))
+        for c, (recv, own) in enumerate(bwd_parts[BWD_CHUNKS:]):
+            hits = hits_of(ep_i, c * per_chunk, per_chunk)
+            dx_sum = dx_sum + dot(hits, (recv + own).astype(BF16))
+            if c + 1 < BWD_CHUNKS:
+                dx_sum = lax.optimization_barrier(dx_sum)
         return y_out, dx_sum.astype(BF16), d_router, d_w_gate, d_w_up, d_w_down, ds_gate, ds_up, ds_down
 
     tok_spec = P(('ep', 'tp'), None)

time: 584 us -> 581 us (level)
    unnamed x119 -> x103, local copies, waits for them, and re-layouts: 12.6 us -> 15.6 us
    dot_general x44 -> x45, matrix products: 89.4 us -> 91.7 us  [dot(): return lax.dot_general(a, b, dims, preferred_element_type=F32)]
    ppermute x2 -> x3, waiting for transfers between devices: 125 us -> 124 us  [device_step(): bwd_parts.append((lax.ppermute(send, 'tp', swap_tp), own))]
  transfers between devices with their start and end apart: 29 -> 30, of which waited for: 6 -> 6; matrix products, arithmetic and copies ran while one was open for 21% -> 21% of each run, Pallas kernels for 31% -> 31%
where the time goes in v6:
time: 581 us; the launch traced here: 579 us
  Pallas kernels  220 us (38%)
  waiting for transfers between devices  193 us (33%)
  matrix products  95.7 us (16%)
  local copies, waits for them, and re-layouts  33.1 us (6%)
  starting transfers between devices  28.5 us (5%)
  other arithmetic  7.21 us (1%)
    ppermute x3, waiting for transfers between devices, device_step(): bwd_parts.append((lax.ppermute(send, 'tp', swap_tp), own))  124 us
    pallas_call x1, Pallas kernels, expert_bwd(): pl.pallas_call(functools.partial(bwd_kernel, sizes, per_chunk), grid=(cou...  104 us
    dot_general x45, matrix products, dot(): return lax.dot_general(a, b, dims, preferred_element_type=F32)  91.7 us
    pallas_call x3, Pallas kernels, expert_fwd(): pl.pallas_call(functools.partial(fwd_kernel, half, padded), grid=(count,)...  49.5 us
    pallas_call x1, Pallas kernels, gather_rows(): pl.pallas_call(gather_kernel, in_specs=[any_spec] * 6, out_specs=[any_spe...  41 us
    ppermute x1, waiting for transfers between devices, device_step(): bwd_parts = [(lax.ppermute(bwd_out[0][0], 'tp', swap_tp), bwd_out[0][1])]  37.5 us
    pallas_call x1, Pallas kernels, shared_grad(): pl.pallas_call(functools.partial(shared_grad_kernel, 256), grid=(width //...  25.7 us
    all_to_all x3, waiting for transfers between devices, send_home(): out = lax.all_to_all(out, 'ep', 0, 0)  24.9 us
  transfers between devices with their start and end apart: 30, of which 6 were waited for; matrix products, arithmetic and copies ran while one was open for 21% of the time, Pallas kernels for 31%

profile of v6, /device:TPU:0, one launch (start us, length us, event | category | flops | bytes accessed | tf_op | source)
XLA Modules:
  0.0 579.2 jit_solution(117992680739159626)
XLA Ops:
  0.7 41.0 %gather_rows.1 = (bf16[8,192,1536]{2,1,0:T(8,128)(2,1)}, s32[8,6,192]{2,1,0:T(8,128)}, bf16[2,192,1536]{2,1,0:T(8,128)(2,1)}, bf16[128,1536]{1,0:T(8,128)(2,1)}, bf16[1536,256]{1,0:T(8,128)(2,1)}) custom-call(bf16[192,1536]{1,0:T(8,128)(2,1)} %x_ref.1, s32[6,192]{1,0:T(8,128)} %bitcast.103, bf16[192,1536]{1,0:T(8,128)(2,1)} %dy_ref.1, ...), custom_call_target="tpu_custom_call" | custom-call | flops 60000002048 | bytes 9437184 | tf_op jit(solution)/shard_map/gather_rows/pallas_call | solution.py:384
  42.2 1.5 collective-permute-start.5
  46.6 8.8 %shard_map.169 = (f32[168,1536]{1,0:T(8,128)}, f32[168,1536]{1,0:T(8,128)S(1)}) custom-call(bf16[1536,1536]{1,0:T(8,128)(2,1)} %bitcast.85, s32[16,1,1536]{2,1,0:T(1,128)S(1)} %reshape.597.row_ref, bf16[16,1536,256]{2,1,0:T(8,128)(2,1)} %w1_ref.7, bf16[16,1536,256]{2,1,0:T(8,128)(2,1)} %w3_ref.7, bf16[16,256,1536]{2,1,0:T(8,128)(2,1)} %w2_ref.7), custom_call_target="tpu_custom_call" | custom-call | flops 2491416576 | bytes 11501568 | tf_op jit(solution)/shard_map/pallas_call | solution.py:166
  57.9 22.4 %shard_map.170 = (f32[672,1536]{1,0:T(8,128)S(1)}, f32[672,1536]{1,0:T(8,128)}) custom-call(bf16[1536,1536]{1,0:T(8,128)(2,1)} %bitcast.86, s32[16,1,1536]{2,1,0:T(1,128)S(1)} %reshape.597.row_ref, bf16[16,1536,256]{2,1,0:T(8,128)(2,1)} %w1_ref.7, bf16[16,1536,256]{2,1,0:T(8,128)(2,1)} %w3_ref.7, bf16[16,256,1536]{2,1,0:T(8,128)(2,1)} %w2_ref.7), custom_call_target="tpu_custom_call" | custom-call | flops 9965666304 | bytes 31850496 | tf_op jit(solution)/shard_map/pallas_call | solution.py:166
  80.3 1.9 copy-done.7
  82.2 18.3 %shard_map.171 = (f32[504,1536]{1,0:T(8,128)}, f32[504,1536]{1,0:T(8,128)}) custom-call(bf16[1536,1536]{1,0:T(8,128)(2,1)} %bitcast.87, s32[16,1,1536]{2,1,0:T(1,128)S(1)} %reshape.597.row_ref, bf16[16,1536,256]{2,1,0:T(8,128)(2,1)} %w1_ref.7, bf16[16,1536,256]{2,1,0:T(8,128)(2,1)} %w3_ref.7, bf16[16,256,1536]{2,1,0:T(8,128)(2,1)} %w2_ref.7), custom_call_target="tpu_custom_call" | custom-call | flops 7474249728 | bytes 25067520 | tf_op jit(solution)/shard_map/pallas_call | solution.py:166
  100.5 3.9 fusion.222
  104.6 2.6 broadcast_in_dim.97
  114.9 2.4 bitcast_dynamic-update-slice_fusion
  117.3 104.0 %expert_bwd.1 = (f32[16,1536,256]{2,1,0:T(8,128)}, f32[16,1536,256]{2,1,0:T(8,128)}, f32[16,256,1536]{2,1,0:T(8,128)}, f32[504,1536]{1,0:T(8,128)}, f32[504,1536...) custom-call(bf16[1536,1536]{1,0:T(8,128)(2,1)} %bitcast.89, ...), custom_call_target="tpu_custom_call" | custom-call | flops 52344913920 | bytes 143130624 | tf_op jit(solution)/shard_map/expert_bwd/pallas_call | solution.py:197
  225.4 25.7 %shared_grad.1 = (f32[1536,512]{1,0:T(8,128)}, f32[1536,512]{1,0:T(8,128)}, f32[512,1536]{1,0:T(8,128)}) custom-call(bf16[1536,1536]{1,0:T(8,128)(2,1)} %bitcast.90, bf16[1536,1536]{1,0:T(8,128)(2,1)} %bitcast.6.dy_ref, bf16[1536,512]{1,0:T(8,128)(2,1)S(1)} %copy-done.2, bf16[1536,512]{1,0:T(8,128)(2,1)S(1)} %copy-done.3, bf16[512,1536]{1,0:T(8,128)(2,1)S(1)} %copy-done.1), custom_call_target="tpu_custom_call" | custom-call | flops 14495514624 | bytes 23592960 | tf_op jit(solution)/shard_map/shared_grad/pallas_call | solution.py:264
  251.1 5.3 convolution_convert_fusion
  258.9 1.8 constant_dynamic-update-slice_fusion.3
  260.7 4.7 all-to-all-start
  266.9 1.8 fusion.22
  268.7 1.8 constant_dynamic-update-slice_fusion.2
  270.7 1.6 fusion.75
  273.6 1.7 convolution_add_fusion.2
  275.9 1.8 fusion.31
  278.6 2.0 fusion.218
  280.6 2.0 fusion.219
  282.7 3.2 fusion.32
  290.5 1.7 copy-done.42
  296.7 1.7 fusion.66
  298.4 37.5 %collective-permute-done.13 = f32[504,1536]{1,0:T(8,128)} collective-permute-done((f32[504,1536]{1,0:T(8,128)}, f32[504,1536]{1,0:T(8,128)}, u32[]{:S(2)}, u32[]{:S(2)}) %collective-permute-start.13) | collective-permute-done | bytes 3096608 | tf_op jit(solution)/shard_map/ppermute | solution.py:490
  335.9 2.3 add_convert_fusion.2
  343.6 123.9 %collective-permute-done.17 = f32[504,1536]{1,0:T(8,128)S(1)} collective-permute-done((f32[504,1536]{1,0:T(8,128)S(1)}, f32[504,1536]{1,0:T(8,128)S(1)}, u32[]{:S(2)}, u32[]{:S(2)}) %collective-permute-start.17) | collective-permute-done | bytes 3096608 | tf_op jit(solution)/shard_map/ppermute | solution.py:579
  473.5 2.4 convolution_convert_fusion.2
  475.9 3.5 all-to-all-start.1
  479.4 2.6 reduce-precision_convert_fusion.1
  483.6 1.6 fusion.27
  485.2 13.9 %all-to-all-done.1 = bf16[4,48,1536]{2,1,0:T(8,128)(2,1)S(1)} async-done(((bf16[4,48,1536]{2,1,0:T(8,128)(2,1)}), bf16[4,48,1536]{2,1,0:T(8,128)(2,1)S(1)}, u32[]{:S(2)}, u32[]{:S(2)}) %all-to-all-start.1) | async-done | bytes 589856 | tf_op jit(solution)/shard_map/all_to_all | solution.py:519
  499.3 5.0 convolution_convert_fusion.1
  504.3 4.6 all-to-all-start.2
  508.9 2.7 fusion.26
  511.6 2.7 fusion.29
  514.3 2.7 fusion.28
  519.3 11.0 %all-to-all-done.2 = bf16[4,128,1536]{2,1,0:T(8,128)(2,1)} async-done(((bf16[4,128,1536]{2,1,0:T(8,128)(2,1)}), bf16[4,128,1536]{2,1,0:T(8,128)(2,1)}, u32[]{:S(2)}, u32[]{:S(2)}) %all-to-all-start.2) | async-done | bytes 1572896 | tf_op jit(solution)/shard_map/all_to_all | solution.py:519
  530.3 2.3 reduce-precision_convert_fusion.5
  533.8 4.7 fusion.8
  540.5 3.2 fusion.4
  543.7 3.5 fusion.1
  547.1 2.7 fusion.24
  549.9 5.2 fusion.7
  555.1 2.7 add_add_fusion
  561.1 5.7 fusion.5
  567.2 5.6 collective-permute-done.24
  575.0 3.4 fusion.48
  (231 shorter events, 58.6 us)
Async XLA Ops:
  0.6 99.9 %copy-start = (bf16[1536,64]{0,1:T(8,128)(2,1)S(1)}, bf16[1536,64]{0,1:T(8,128)(2,1)}, u32[]{:S(2)}) copy-start(bf16[1536,64]{0,1:T(8,128)(2,1)} %param.12) | copy-start | bytes 589828
  41.6 71.6 %collective-permute-start.1 = (bf16[2,192,1536]{2,1,0:T(8,128)(2,1)}, bf16[2,192,1536]{2,1,0:T(8,128)(2,1)S(1)}, u32[]{:S(2)}, u32[]{:S(2)}) collective-permute-start(bf16[2,192,1536]{2,1,0:T(8,128)(2,1)} %get-tuple-element.67), channel_id=1, source_target_pairs={{0,1},{1,0},{2,3},{3,2},{4,5},{5,4},{6,7},{7,6}} | collective-permute-start | bytes 3538952 | tf_op jit(solution)/shard_map/ppermute | solution.py:435
  41.7 67.4 %collective-permute-start = (bf16[2,192,1536]{2,1,0:T(8,128)(2,1)}, bf16[2,192,1536]{2,1,0:T(8,128)(2,1)S(1)}, u32[]{:S(2)}, u32[]{:S(2)}) collective-permute-start(bf16[2,192,1536]{2,1,0:T(8,128)(2,1)} %get-tuple-element.67), channel_id=1, source_target_pairs={{0,2},{1,3},{2,0},{3,1},{4,6},{5,7},{6,4},{7,5}} | collective-permute-start | bytes 3538952 | tf_op jit(solution)/shard_map/ppermute | solution.py:434
  42.2 179.1 %collective-permute-start.5 = (bf16[128,1536]{1,0:T(8,128)(2,1)}, bf16[128,1536]{1,0:T(8,128)(2,1)}, u32[]{:S(2)}, u32[]{:S(2)}) collective-permute-start(bf16[128,1536]{1,0:T(8,128)(2,1)} %get-tuple-element.95), channel_id=1, source_target_pairs={{0,2},{1,3},{2,0},{3,1},{4,6},{5,7},{6,4},{7,5}} | collective-permute-start | bytes 1179656 | tf_op jit(solution)/shard_map/ppermute | solution.py:495
  43.7 68.1 %collective-permute-start.3 = (bf16[1536,256]{1,0:T(8,128)(2,1)}, bf16[1536,256]{1,0:T(8,128)(2,1)}, u32[]{:S(2)}, u32[]{:S(2)}) collective-permute-start(bf16[1536,256]{1,0:T(8,128)(2,1)} %get-tuple-element.76), channel_id=1, source_target_pairs={{0,4},{4,0},{1,5},{5,1},{2,6},{6,2},{3,7},{7,3}} | collective-permute-start | bytes 2359304 | tf_op jit(solution)/shard_map/ppermute | solution.py:447
  56.5 415.7 %collective-permute-start.11 = (f32[168,1536]{1,0:T(8,128)}, f32[168,1536]{1,0:T(8,128)}, u32[]{:S(2)}, u32[]{:S(2)}) collective-permute-start(f32[168,1536]{1,0:T(8,128)} %get-tuple-element.100), channel_id=1, source_target_pairs={{0,4},{4,0},{1,5},{5,1},{2,6},{6,2},{3,7},{7,3}} | collective-permute-start | bytes 3096584 | tf_op jit(solution)/shard_map/ppermute | solution.py:466
  109.0 5.9 %collective-permute-start.2 = (bf16[2,192,1536]{2,1,0:T(8,128)(2,1)S(1)}, bf16[2,192,1536]{2,1,0:T(8,128)(2,1)}, u32[]{:S(2)}, u32[]{:S(2)}) collective-permute-start(bf16[2,192,1536]{2,1,0:T(8,128)(2,1)S(1)} %collective-permute-done), channel_id=1, source_target_pairs={{0,1},{1,0},{2,3},{3,2},{4,5},{5,4},{6,7},{7,6}} | collective-permute-start | bytes 3538952 | tf_op jit(solution)/shard_map/ppermute | solution.py:435
  111.8 139.3 %collective-permute-start.6 = (f32[672,1536]{1,0:T(8,128)}, f32[672,1536]{1,0:T(8,128)}, u32[]{:S(2)}, u32[]{:S(2)}) collective-permute-start(f32[672,1536]{1,0:T(8,128)} %copy-done.7), channel_id=1, source_target_pairs={{0,4},{4,0},{1,5},{5,1},{2,6},{6,2},{3,7},{7,3}} | collective-permute-start | bytes 12386312 | tf_op jit(solution)/shard_map/ppermute | solution.py:466
  113.2 108.1 %collective-permute-start.4 = (bf16[1536,256]{1,0:T(8,128)(2,1)}, bf16[1536,256]{1,0:T(8,128)(2,1)}, u32[]{:S(2)}, u32[]{:S(2)}) collective-permute-start(bf16[1536,256]{1,0:T(8,128)(2,1)} %collective-permute-done.3), channel_id=1, source_target_pairs={{0,2},{1,3},{2,0},{3,1},{4,6},{5,7},{6,4},{7,5}} | collective-permute-start | bytes 2359304 | tf_op jit(solution)/shard_map/ppermute | solution.py:494
  117.3 106.7 %copy-start.1 = (bf16[512,1536]{1,0:T(8,128)(2,1)S(1)}, bf16[512,1536]{1,0:T(8,128)(2,1)}, u32[]{:S(2)}) copy-start(bf16[512,1536]{1,0:T(8,128)(2,1)} %wd_ref.3) | copy-start | bytes 4718596
  117.3 106.7 %copy-start.2 = (bf16[1536,512]{1,0:T(8,128)(2,1)S(1)}, bf16[1536,512]{1,0:T(8,128)(2,1)}, u32[]{:S(2)}) copy-start(bf16[1536,512]{1,0:T(8,128)(2,1)} %wg_ref.3) | copy-start | bytes 4718596
  221.4 54.0 %collective-permute-start.21 = (f32[168,1536]{1,0:T(8,128)}, f32[168,1536]{1,0:T(8,128)}, u32[]{:S(2)}, u32[]{:S(2)}) collective-permute-start(f32[168,1536]{1,0:T(8,128)} %get-tuple-element.111), channel_id=1, source_target_pairs={{0,4},{4,0},{1,5},{5,1},{2,6},{6,2},{3,7},{7,3}} | collective-permute-start | bytes 3096584 | tf_op jit(solution)/shard_map/ppermute | solution.py:579
  221.9 60.7 %collective-permute-start.22 = (f32[168,1536]{1,0:T(8,128)}, f32[168,1536]{1,0:T(8,128)}, u32[]{:S(2)}, u32[]{:S(2)}) collective-permute-start(f32[168,1536]{1,0:T(8,128)} %get-tuple-element.113), channel_id=1, source_target_pairs={{0,4},{4,0},{1,5},{5,1},{2,6},{6,2},{3,7},{7,3}} | collective-permute-start | bytes 3096584 | tf_op jit(solution)/shard_map/ppermute | solution.py:579
  223.4 112.5 %collective-permute-start.13 = (f32[504,1536]{1,0:T(8,128)}, f32[504,1536]{1,0:T(8,128)}, u32[]{:S(2)}, u32[]{:S(2)}) collective-permute-start(f32[504,1536]{1,0:T(8,128)} %get-tuple-element.107), channel_id=1, source_target_pairs={{0,4},{4,0},{1,5},{5,1},{2,6},{6,2},{3,7},{7,3}} | collective-permute-start | bytes 9289736 | tf_op jit(solution)/shard_map/ppermute | solution.py:490
  225.4 25.7 %copy-start.41 = (f32[672,1536]{1,0:T(8,128)S(1)}, f32[672,1536]{1,0:T(8,128)}, u32[]{:S(2)}) copy-start(f32[672,1536]{1,0:T(8,128)} %get-tuple-element.91) | copy-start | bytes 12386308
  251.1 5.4 copy-start.9
  258.9 28.3 %collective-permute-start.9 = (bf16[128,1536]{1,0:T(8,128)(2,1)}, bf16[128,1536]{1,0:T(8,128)(2,1)}, u32[]{:S(2)}, u32[]{:S(2)}) collective-permute-start(bf16[128,1536]{1,0:T(8,128)(2,1)} %get-tuple-element.95), channel_id=1, source_target_pairs={{0,1},{1,0},{2,3},{3,2},{4,5},{5,4},{6,7},{7,6}} | collective-permute-start | bytes 1179656 | tf_op jit(solution)/shard_map/ppermute | solution.py:529
  260.7 4.8 copy-start.39
  260.7 211.5 %all-to-all-start = ((bf16[4,168,1536]{2,1,0:T(8,128)(2,1)}), bf16[4,168,1536]{2,1,0:T(8,128)(2,1)}, u32[]{:S(2)}, u32[]{:S(2)}) async-start(bf16[4,168,1536]{2,1,0:T(8,128)(2,1)} %bitcast.95), calls=%async_computation | async-start | bytes 4128768 | tf_op jit(solution)/shard_map/all_to_all | solution.py:519
  266.9 3.8 copy-start.12
  275.3 14.3 %collective-permute-start.10 = (bf16[128,1536]{1,0:T(8,128)(2,1)}, bf16[128,1536]{1,0:T(8,128)(2,1)S(1)}, u32[]{:S(2)}, u32[]{:S(2)}) collective-permute-start(bf16[128,1536]{1,0:T(8,128)(2,1)} %collective-permute-done.5), channel_id=1, source_target_pairs={{0,1},{1,0},{2,3},{3,2},{4,5},{5,4},{6,7},{7,6}} | collective-permute-start | bytes 1179656 | tf_op jit(solution)/shard_map/ppermute | solution.py:529
  282.7 4.2 copy-start.43
  282.7 6.0 %copy-start.15 = (bf16[512,1536]{1,0:T(8,128)(2,1)S(1)}, bf16[512,1536]{1,0:T(8,128)(2,1)}, u32[]{:S(2)}) copy-start(bf16[512,1536]{1,0:T(8,128)(2,1)} %constant_dynamic-update-slice_fusion.2) | copy-start | bytes 4718596
  282.7 7.9 %collective-permute-start.7 = (bf16[1536,256]{1,0:T(8,128)(2,1)}, bf16[1536,256]{1,0:T(8,128)(2,1)}, u32[]{:S(2)}, u32[]{:S(2)}) collective-permute-start(bf16[1536,256]{1,0:T(8,128)(2,1)} %collective-permute-done.3), channel_id=1, source_target_pairs={{0,1},{1,0},{2,3},{3,2},{4,5},{5,4},{6,7},{7,6}} | collective-permute-start | bytes 2359304 | tf_op jit(solution)/shard_map/ppermute | solution.py:528
  286.0 3.9 copy-start.18
  287.1 229.9 %copy-start.37 = (pred[192,192]{0,1:T(32,128)(4,1)}, pred[192,192]{0,1:T(32,128)(4,1)S(1)}, u32[]{:S(2)}) copy-start(pred[192,192]{0,1:T(32,128)(4,1)S(1)} %convolution_compare_fusion.2) | copy-start | bytes 110596
  287.2 211.9 %collective-permute-start.12 = (f32[504,1536]{1,0:T(8,128)}, f32[504,1536]{1,0:T(8,128)}, u32[]{:S(2)}, u32[]{:S(2)}) collective-permute-start(f32[504,1536]{1,0:T(8,128)} %get-tuple-element.103), channel_id=1, source_target_pairs={{0,4},{4,0},{1,5},{5,1},{2,6},{6,2},{3,7},{7,3}} | collective-permute-start | bytes 9289736 | tf_op jit(solution)/shard_map/ppermute | solution.py:466
  289.7 4.3 collective-permute-start.8
  289.9 4.8 copy-start.16
  290.5 6.1 %copy-start.23 = (f32[192,512]{1,0:T(8,128)}, f32[192,512]{1,0:T(8,128)S(1)}, u32[]{:S(2)}) copy-start(f32[192,512]{1,0:T(8,128)S(1)} %fusion.23) | copy-start | bytes 1179652
  292.3 175.2 %collective-permute-start.17 = (f32[504,1536]{1,0:T(8,128)S(1)}, f32[504,1536]{1,0:T(8,128)S(1)}, u32[]{:S(2)}, u32[]{:S(2)}) collective-permute-start(f32[504,1536]{1,0:T(8,128)S(1)} %copy-done.42), channel_id=1, source_target_pairs={{0,4},{4,0},{1,5},{5,1},{2,6},{6,2},{3,7},{7,3}} | collective-permute-start | bytes 9289736 | tf_op jit(solution)/shard_map/ppermute | solution.py:579
  296.7 39.2 %copy-start.14 = (f32[504,1536]{1,0:T(8,128)S(1)}, f32[504,1536]{1,0:T(8,128)}, u32[]{:S(2)}) copy-start(f32[504,1536]{1,0:T(8,128)} %get-tuple-element.108) | copy-start | bytes 9289732
  339.5 128.2 %copy-start.13 = (f32[504,1536]{1,0:T(8,128)S(1)}, f32[504,1536]{1,0:T(8,128)}, u32[]{:S(2)}) copy-start(f32[504,1536]{1,0:T(8,128)} %get-tuple-element.110) | copy-start | bytes 9289732
  342.1 201.6 %collective-permute-start.14 = (bf16[168,1536]{1,0:T(8,128)(2,1)}, bf16[168,1536]{1,0:T(8,128)(2,1)}, u32[]{:S(2)}, u32[]{:S(2)}) collective-permute-start(bf16[168,1536]{1,0:T(8,128)(2,1)} %convolution_convert_fusion.8), channel_id=1, source_target_pairs={{0,2},{1,3},{2,0},{3,1},{4,6},{5,7},{6,4},{7,5}} | collective-permute-start | bytes 1548296 | tf_op jit(solution)/shard_map/ppermute | solution.py:600
  343.6 165.3 %collective-permute-start.15 = (bf16[168,1536]{1,0:T(8,128)(2,1)}, bf16[168,1536]{1,0:T(8,128)(2,1)}, u32[]{:S(2)}, u32[]{:S(2)}) collective-permute-start(bf16[168,1536]{1,0:T(8,128)(2,1)} %convolution_convert_fusion.7), channel_id=1, source_target_pairs={{0,1},{1,0},{2,3},{3,2},{4,5},{5,4},{6,7},{7,6}} | collective-permute-start | bytes 1548296 | tf_op jit(solution)/shard_map/ppermute | solution.py:600
  467.5 15.7 %collective-permute-start.16 = (bf16[168,1536]{1,0:T(8,128)(2,1)}, bf16[168,1536]{1,0:T(8,128)(2,1)}, u32[]{:S(2)}, u32[]{:S(2)}) collective-permute-start(bf16[168,1536]{1,0:T(8,128)(2,1)} %convolution_convert_fusion.6), channel_id=1, source_target_pairs={{0,3},{1,2},{2,1},{3,0},{4,7},{5,6},{6,5},{7,4}} | collective-permute-start | bytes 1548296 | tf_op jit(solution)/shard_map/ppermute | solution.py:600
  469.6 3.9 copy-start.6
  472.2 7.2 %copy-start.44 = (pred[192,672]{1,0:T(32,128)(4,1)S(1)}, pred[192,672]{1,0:T(32,128)(4,1)}, u32[]{:S(2)}) copy-start(pred[192,672]{1,0:T(32,128)(4,1)} %convolution_compare_fusion) | copy-start | bytes 387076
  472.2 42.1 %collective-permute-start.18 = (bf16[168,1536]{1,0:T(8,128)(2,1)}, bf16[168,1536]{1,0:T(8,128)(2,1)}, u32[]{:S(2)}, u32[]{:S(2)}) collective-permute-start(bf16[168,1536]{1,0:T(8,128)(2,1)} %convolution_convert_fusion.5), channel_id=1, source_target_pairs={{0,2},{1,3},{2,0},{3,1},{4,6},{5,7},{6,4},{7,5}} | collective-permute-start | bytes 1548296 | tf_op jit(solution)/shard_map/ppermute | solution.py:600
  475.9 23.2 %all-to-all-start.1 = ((bf16[4,48,1536]{2,1,0:T(8,128)(2,1)}), bf16[4,48,1536]{2,1,0:T(8,128)(2,1)S(1)}, u32[]{:S(2)}, u32[]{:S(2)}) async-start(bf16[4,48,1536]{2,1,0:T(8,128)(2,1)} %bitcast.94), calls=%async_computation.1 | async-start | bytes 1179648 | tf_op jit(solution)/shard_map/all_to_all | solution.py:519
  483.1 28.5 %collective-permute-start.19 = (bf16[168,1536]{1,0:T(8,128)(2,1)}, bf16[168,1536]{1,0:T(8,128)(2,1)}, u32[]{:S(2)}, u32[]{:S(2)}) collective-permute-start(bf16[168,1536]{1,0:T(8,128)(2,1)} %convolution_convert_fusion.4), channel_id=1, source_target_pairs={{0,1},{1,0},{2,3},{3,2},{4,5},{5,4},{6,7},{7,6}} | collective-permute-start | bytes 1548296 | tf_op jit(solution)/shard_map/ppermute | solution.py:600
  499.1 56.0 %collective-permute-start.20 = (bf16[168,1536]{1,0:T(8,128)(2,1)}, bf16[168,1536]{1,0:T(8,128)(2,1)}, u32[]{:S(2)}, u32[]{:S(2)}) collective-permute-start(bf16[168,1536]{1,0:T(8,128)(2,1)} %convolution_convert_fusion.3), channel_id=1, source_target_pairs={{0,3},{1,2},{2,1},{3,0},{4,7},{5,6},{6,5},{7,4}} | collective-permute-start | bytes 1548296 | tf_op jit(solution)/shard_map/ppermute | solution.py:600
  504.3 26.0 %all-to-all-start.2 = ((bf16[4,128,1536]{2,1,0:T(8,128)(2,1)}), bf16[4,128,1536]{2,1,0:T(8,128)(2,1)}, u32[]{:S(2)}, u32[]{:S(2)}) async-start(bf16[4,128,1536]{2,1,0:T(8,128)(2,1)} %bitcast.12), calls=%async_computation.2 | async-start | bytes 3145728 | tf_op jit(solution)/shard_map/all_to_all | solution.py:519
  533.2 33.6 %collective-permute-start.23 = (f32[192,64]{0,1:T(8,128)S(1)}, f32[192,64]{0,1:T(8,128)S(1)}, u32[]{:S(2)}, u32[]{:S(2)}) collective-permute-start(f32[192,64]{0,1:T(8,128)S(1)} %get-tuple-element.124), channel_id=1, source_target_pairs={{0,4},{4,0},{1,5},{5,1},{2,6},{6,2},{3,7},{7,3}} | collective-permute-start | bytes 147464 | tf_op jit(solution)/shard_map/ppermute | solution.py:577
  549.9 5.2 copy-start.40
  566.8 6.1 %collective-permute-start.25 = (f32[2,192,64]{1,2,0:T(8,128)S(1)}, f32[2,192,64]{1,2,0:T(8,128)S(1)}, u32[]{:S(2)}, u32[]{:S(2)}) collective-permute-start(f32[2,192,64]{1,2,0:T(8,128)S(1)} %maximum_select_fusion.1), channel_id=1, source_target_pairs={{0,1},{1,0},{2,3},{3,2},{4,5},{5,4},{6,7},{7,6}} | collective-permute-start | bytes 294920 | tf_op jit(solution)/shard_map/ppermute | solution.py:435
  566.8 5.9 %collective-permute-start.24 = (f32[2,192,64]{1,2,0:T(8,128)S(1)}, f32[2,192,64]{1,2,0:T(8,128)S(1)}, u32[]{:S(2)}, u32[]{:S(2)}) collective-permute-start(f32[2,192,64]{1,2,0:T(8,128)S(1)} %maximum_select_fusion.1), channel_id=1, source_target_pairs={{0,2},{1,3},{2,0},{3,1},{4,6},{5,7},{6,4},{7,5}} | collective-permute-start | bytes 294920 | tf_op jit(solution)/shard_map/ppermute | solution.py:434
  572.9 1.4 collective-permute-start.26
  (32 other events, 60.2 us)

commit v7 on v6

--- a/solution.py
+++ b/solution.py
@@ -590,6 +590,12 @@
             return (dot(want, table) == (slot % cap).astype(F32)[None, :]).astype(BF16)
 
         swaps = (swap_x, swap_c, [(i, core_partner(d)) for i, d in swap_x])
+
+        def join_near(c, total):
+            recv, own = bwd_parts[BWD_CHUNKS + c]
+            hits = hits_of(ep_i, c * per_chunk, per_chunk)
+            return total + dot(hits, (recv + own).astype(BF16))
+
         for c, (recv, own) in enumerate(bwd_parts[:BWD_CHUNKS]):
             rows = (recv + own).astype(BF16)
             slot = jnp.arange(per_chunk * cap, dtype=jnp.int32)
@@ -600,12 +606,10 @@
                 back = lax.ppermute(back, 'ep', pairs)
                 hits = hits_of(ep_order[1 + k], c * per_chunk, per_chunk)
                 dx_sum = dx_sum + dot(hits, back)
+            if c + 1 < BWD_CHUNKS:
+                dx_sum = join_near(c, lax.optimization_barrier(dx_sum))
             dx_sum = lax.optimization_barrier(dx_sum)
-        for c, (recv, own) in enumerate(bwd_parts[BWD_CHUNKS:]):
-            hits = hits_of(ep_i, c * per_chunk, per_chunk)
-            dx_sum = dx_sum + dot(hits, (recv + own).astype(BF16))
-            if c + 1 < BWD_CHUNKS:
-                dx_sum = lax.optimization_barrier(dx_sum)
+        dx_sum = join_near(BWD_CHUNKS - 1, dx_sum)
         return y_out, dx_sum.astype(BF16), d_router, d_w_gate, d_w_up, d_w_down, ds_gate, ds_up, ds_down
 
     tok_spec = P(('ep', 'tp'), None)

time: 581 us -> 581 us (level)
    unnamed x103 -> x109, local copies, waits for them, and re-layouts: 15.6 us -> 13.5 us
where the time goes in v7:
time: 581 us; the launch traced here: 579 us
  Pallas kernels  220 us (38%)
  waiting for transfers between devices  195 us (34%)
  matrix products  93.6 us (16%)
  local copies, waits for them, and re-layouts  30.9 us (5%)
  starting transfers between devices  28.5 us (5%)
  other arithmetic  9.97 us (2%)
    ppermute x3, waiting for transfers between devices, device_step(): bwd_parts.append((lax.ppermute(send, 'tp', swap_tp), own))  124 us
    pallas_call x1, Pallas kernels, expert_bwd(): pl.pallas_call(functools.partial(bwd_kernel, sizes, per_chunk), grid=(cou...  104 us
    dot_general x45, matrix products, dot(): return lax.dot_general(a, b, dims, preferred_element_type=F32)  89.5 us
    pallas_call x3, Pallas kernels, expert_fwd(): pl.pallas_call(functools.partial(fwd_kernel, half, padded), grid=(count,)...  49.5 us
    pallas_call x1, Pallas kernels, gather_rows(): pl.pallas_call(gather_kernel, in_specs=[any_spec] * 6, out_specs=[any_spe...  41 us
    ppermute x1, waiting for transfers between devices, device_step(): bwd_parts = [(lax.ppermute(bwd_out[0][0], 'tp', swap_tp), bwd_out[0][1])]  37.5 us
    all_to_all x3, waiting for transfers between devices, send_home(): out = lax.all_to_all(out, 'ep', 0, 0)  26.4 us
    pallas_call x1, Pallas kernels, shared_grad(): pl.pallas_call(functools.partial(shared_grad_kernel, 256), grid=(width //...  25.7 us
  transfers between devices with their start and end apart: 30, of which 6 were waited for; matrix products, arithmetic and copies ran while one was open for 21% of the time, Pallas kernels for 31%

profile of v7, /device:TPU:0, one launch (start us, length us, event | category | flops | bytes accessed | tf_op | source)
XLA Modules:
  0.0 579.4 jit_solution(16722751123279261130)
XLA Ops:
  0.7 41.0 %gather_rows.1 = (bf16[8,192,1536]{2,1,0:T(8,128)(2,1)}, s32[8,6,192]{2,1,0:T(8,128)}, bf16[2,192,1536]{2,1,0:T(8,128)(2,1)}, bf16[128,1536]{1,0:T(8,128)(2,1)}, bf16[1536,256]{1,0:T(8,128)(2,1)}) custom-call(bf16[192,1536]{1,0:T(8,128)(2,1)} %x_ref.1, s32[6,192]{1,0:T(8,128)} %bitcast.103, bf16[192,1536]{1,0:T(8,128)(2,1)} %dy_ref.1, ...), custom_call_target="tpu_custom_call" | custom-call | flops 60000002048 | bytes 9437184 | tf_op jit(solution)/shard_map/gather_rows/pallas_call | solution.py:384
  46.6 8.8 %shard_map.169 = (f32[168,1536]{1,0:T(8,128)}, f32[168,1536]{1,0:T(8,128)S(1)}) custom-call(bf16[1536,1536]{1,0:T(8,128)(2,1)} %bitcast.85, s32[16,1,1536]{2,1,0:T(1,128)S(1)} %reshape.597.row_ref, bf16[16,1536,256]{2,1,0:T(8,128)(2,1)} %w1_ref.7, bf16[16,1536,256]{2,1,0:T(8,128)(2,1)} %w3_ref.7, bf16[16,256,1536]{2,1,0:T(8,128)(2,1)} %w2_ref.7), custom_call_target="tpu_custom_call" | custom-call | flops 2491416576 | bytes 11501568 | tf_op jit(solution)/shard_map/pallas_call | solution.py:166
  57.9 22.4 %shard_map.170 = (f32[672,1536]{1,0:T(8,128)S(1)}, f32[672,1536]{1,0:T(8,128)}) custom-call(bf16[1536,1536]{1,0:T(8,128)(2,1)} %bitcast.86, s32[16,1,1536]{2,1,0:T(1,128)S(1)} %reshape.597.row_ref, bf16[16,1536,256]{2,1,0:T(8,128)(2,1)} %w1_ref.7, bf16[16,1536,256]{2,1,0:T(8,128)(2,1)} %w3_ref.7, bf16[16,256,1536]{2,1,0:T(8,128)(2,1)} %w2_ref.7), custom_call_target="tpu_custom_call" | custom-call | flops 9965666304 | bytes 31850496 | tf_op jit(solution)/shard_map/pallas_call | solution.py:166
  80.2 2.0 copy-done.7
  82.2 18.3 %shard_map.171 = (f32[504,1536]{1,0:T(8,128)}, f32[504,1536]{1,0:T(8,128)}) custom-call(bf16[1536,1536]{1,0:T(8,128)(2,1)} %bitcast.87, s32[16,1,1536]{2,1,0:T(1,128)S(1)} %reshape.597.row_ref, bf16[16,1536,256]{2,1,0:T(8,128)(2,1)} %w1_ref.7, bf16[16,1536,256]{2,1,0:T(8,128)(2,1)} %w3_ref.7, bf16[16,256,1536]{2,1,0:T(8,128)(2,1)} %w2_ref.7), custom_call_target="tpu_custom_call" | custom-call | flops 7474249728 | bytes 25067520 | tf_op jit(solution)/shard_map/pallas_call | solution.py:166
  100.6 3.9 fusion.222
  104.6 2.6 broadcast_in_dim.97
  114.9 2.4 bitcast_dynamic-update-slice_fusion
  117.3 104.0 %expert_bwd.1 = (f32[16,1536,256]{2,1,0:T(8,128)}, f32[16,1536,256]{2,1,0:T(8,128)}, f32[16,256,1536]{2,1,0:T(8,128)}, f32[504,1536]{1,0:T(8,128)}, f32[504,1536...) custom-call(bf16[1536,1536]{1,0:T(8,128)(2,1)} %bitcast.89, ...), custom_call_target="tpu_custom_call" | custom-call | flops 52344913920 | bytes 143130624 | tf_op jit(solution)/shard_map/expert_bwd/pallas_call | solution.py:197
  225.4 25.7 %shared_grad.1 = (f32[1536,512]{1,0:T(8,128)}, f32[1536,512]{1,0:T(8,128)}, f32[512,1536]{1,0:T(8,128)}) custom-call(bf16[1536,1536]{1,0:T(8,128)(2,1)} %bitcast.90, bf16[1536,1536]{1,0:T(8,128)(2,1)} %bitcast.6.dy_ref, bf16[1536,512]{1,0:T(8,128)(2,1)S(1)} %copy-done.2, bf16[1536,512]{1,0:T(8,128)(2,1)S(1)} %copy-done.3, bf16[512,1536]{1,0:T(8,128)(2,1)S(1)} %copy-done.1), custom_call_target="tpu_custom_call" | custom-call | flops 14495514624 | bytes 23592960 | tf_op jit(solution)/shard_map/shared_grad/pallas_call | solution.py:264
  251.1 5.3 convolution_convert_fusion
  258.9 1.8 constant_dynamic-update-slice_fusion.3
  260.7 4.7 all-to-all-start
  266.9 1.8 fusion.22
  268.7 1.8 constant_dynamic-update-slice_fusion.2
  270.7 1.6 fusion.75
  273.6 1.7 convolution_add_fusion.2
  275.8 1.8 fusion.28
  278.6 2.0 fusion.218
  280.6 2.0 fusion.219
  282.7 3.2 fusion.32
  290.5 1.7 copy-done.44
  296.6 1.7 fusion.66
  298.3 37.5 %collective-permute-done.13 = f32[504,1536]{1,0:T(8,128)} collective-permute-done((f32[504,1536]{1,0:T(8,128)}, f32[504,1536]{1,0:T(8,128)}, u32[]{:S(2)}, u32[]{:S(2)}) %collective-permute-start.13) | collective-permute-done | bytes 3096608 | tf_op jit(solution)/shard_map/ppermute | solution.py:490
  335.9 2.3 add_convert_fusion.2
  343.5 124.0 %collective-permute-done.18 = f32[504,1536]{1,0:T(8,128)S(1)} collective-permute-done((f32[504,1536]{1,0:T(8,128)S(1)}, f32[504,1536]{1,0:T(8,128)S(1)}, u32[]{:S(2)}, u32[]{:S(2)}) %collective-permute-start.18) | collective-permute-done | bytes 3096608 | tf_op jit(solution)/shard_map/ppermute | solution.py:579
  473.5 2.4 convolution_convert_fusion.2
  475.9 3.5 all-to-all-start.1
  479.4 2.6 reduce-precision_convert_fusion.1
  483.6 2.7 fusion.27
  486.3 12.7 %all-to-all-done.1 = bf16[4,48,1536]{2,1,0:T(8,128)(2,1)S(1)} async-done(((bf16[4,48,1536]{2,1,0:T(8,128)(2,1)}), bf16[4,48,1536]{2,1,0:T(8,128)(2,1)S(1)}, u32[]{:S(2)}, u32[]{:S(2)}) %all-to-all-start.1) | async-done | bytes 589856 | tf_op jit(solution)/shard_map/all_to_all | solution.py:519
  499.2 5.0 convolution_convert_fusion.1
  504.2 4.6 all-to-all-start.2
  508.8 2.6 fusion.26
  511.5 1.7 fusion.30
  513.2 2.7 fusion.29
  516.5 13.7 %all-to-all-done.2 = bf16[4,128,1536]{2,1,0:T(8,128)(2,1)} async-done(((bf16[4,128,1536]{2,1,0:T(8,128)(2,1)}), bf16[4,128,1536]{2,1,0:T(8,128)(2,1)}, u32[]{:S(2)}, u32[]{:S(2)}) %all-to-all-start.2) | async-done | bytes 1572896 | tf_op jit(solution)/shard_map/all_to_all | solution.py:519
  530.2 2.2 reduce-precision_convert_fusion.5
  533.6 4.6 fusion.8
  540.1 3.2 fusion.4
  543.3 2.7 fusion.1
  546.0 2.8 fusion.24
  550.0 5.3 fusion.7
  555.3 3.1 add_add_fusion
  558.4 2.7 add_convert_fusion.6
  561.2 5.8 %fusion.5 = bf16[192,1536]{1,0:T(8,128)(2,1)} fusion(f32[192,1536]{1,0:T(8,128)S(1)} %copy-done.21, bf16[512,1536]{1,0:T(8,128)(2,1)S(1)} %copy-done.18, f32[576,1536]{1,0:T(8,128)} %fusion.8, f32[576,1536]{1,0:T(8,128)} %fusion.24, f32[576,1536]{1,0:T(8,128)} %fusion.7, f32[192,512]{1,0:T(8,128)} %fusion.21, f32[192,512]{1,0:T(8,128)S(1)} %copy-done.52), kind=kOutput, calls=%fused_computation.15 | convolution fusion | flops 306216960 | bytes 14745600 | tf_op jit(solution)/shard_map/dot_general | solution.py:25
  567.4 5.6 collective-permute-done.24
  575.2 3.4 fusion.48
  (237 shorter events, 56.3 us)
Async XLA Ops:
  0.6 99.9 %copy-start = (bf16[1536,64]{0,1:T(8,128)(2,1)S(1)}, bf16[1536,64]{0,1:T(8,128)(2,1)}, u32[]{:S(2)}) copy-start(bf16[1536,64]{0,1:T(8,128)(2,1)} %param.12) | copy-start | bytes 589828
  41.6 71.6 %collective-permute-start.1 = (bf16[2,192,1536]{2,1,0:T(8,128)(2,1)}, bf16[2,192,1536]{2,1,0:T(8,128)(2,1)S(1)}, u32[]{:S(2)}, u32[]{:S(2)}) collective-permute-start(bf16[2,192,1536]{2,1,0:T(8,128)(2,1)} %get-tuple-element.67), channel_id=1, source_target_pairs={{0,1},{1,0},{2,3},{3,2},{4,5},{5,4},{6,7},{7,6}} | collective-permute-start | bytes 3538952 | tf_op jit(solution)/shard_map/ppermute | solution.py:435
  41.7 67.4 %collective-permute-start = (bf16[2,192,1536]{2,1,0:T(8,128)(2,1)}, bf16[2,192,1536]{2,1,0:T(8,128)(2,1)S(1)}, u32[]{:S(2)}, u32[]{:S(2)}) collective-permute-start(bf16[2,192,1536]{2,1,0:T(8,128)(2,1)} %get-tuple-element.67), channel_id=1, source_target_pairs={{0,2},{1,3},{2,0},{3,1},{4,6},{5,7},{6,4},{7,5}} | collective-permute-start | bytes 3538952 | tf_op jit(solution)/shard_map/ppermute | solution.py:434
  42.2 179.1 %collective-permute-start.5 = (bf16[128,1536]{1,0:T(8,128)(2,1)}, bf16[128,1536]{1,0:T(8,128)(2,1)}, u32[]{:S(2)}, u32[]{:S(2)}) collective-permute-start(bf16[128,1536]{1,0:T(8,128)(2,1)} %get-tuple-element.95), channel_id=1, source_target_pairs={{0,2},{1,3},{2,0},{3,1},{4,6},{5,7},{6,4},{7,5}} | collective-permute-start | bytes 1179656 | tf_op jit(solution)/shard_map/ppermute | solution.py:495
  43.7 68.0 %collective-permute-start.3 = (bf16[1536,256]{1,0:T(8,128)(2,1)}, bf16[1536,256]{1,0:T(8,128)(2,1)}, u32[]{:S(2)}, u32[]{:S(2)}) collective-permute-start(bf16[1536,256]{1,0:T(8,128)(2,1)} %get-tuple-element.76), channel_id=1, source_target_pairs={{0,4},{4,0},{1,5},{5,1},{2,6},{6,2},{3,7},{7,3}} | collective-permute-start | bytes 2359304 | tf_op jit(solution)/shard_map/ppermute | solution.py:447
  56.5 415.7 %collective-permute-start.11 = (f32[168,1536]{1,0:T(8,128)}, f32[168,1536]{1,0:T(8,128)}, u32[]{:S(2)}, u32[]{:S(2)}) collective-permute-start(f32[168,1536]{1,0:T(8,128)} %get-tuple-element.100), channel_id=1, source_target_pairs={{0,4},{4,0},{1,5},{5,1},{2,6},{6,2},{3,7},{7,3}} | collective-permute-start | bytes 3096584 | tf_op jit(solution)/shard_map/ppermute | solution.py:466
  109.0 5.9 %collective-permute-start.2 = (bf16[2,192,1536]{2,1,0:T(8,128)(2,1)S(1)}, bf16[2,192,1536]{2,1,0:T(8,128)(2,1)}, u32[]{:S(2)}, u32[]{:S(2)}) collective-permute-start(bf16[2,192,1536]{2,1,0:T(8,128)(2,1)S(1)} %collective-permute-done), channel_id=1, source_target_pairs={{0,1},{1,0},{2,3},{3,2},{4,5},{5,4},{6,7},{7,6}} | collective-permute-start | bytes 3538952 | tf_op jit(solution)/shard_map/ppermute | solution.py:435
  111.8 139.3 %collective-permute-start.6 = (f32[672,1536]{1,0:T(8,128)}, f32[672,1536]{1,0:T(8,128)}, u32[]{:S(2)}, u32[]{:S(2)}) collective-permute-start(f32[672,1536]{1,0:T(8,128)} %copy-done.7), channel_id=1, source_target_pairs={{0,4},{4,0},{1,5},{5,1},{2,6},{6,2},{3,7},{7,3}} | collective-permute-start | bytes 12386312 | tf_op jit(solution)/shard_map/ppermute | solution.py:466
  113.2 108.1 %collective-permute-start.4 = (bf16[1536,256]{1,0:T(8,128)(2,1)}, bf16[1536,256]{1,0:T(8,128)(2,1)}, u32[]{:S(2)}, u32[]{:S(2)}) collective-permute-start(bf16[1536,256]{1,0:T(8,128)(2,1)} %collective-permute-done.3), channel_id=1, source_target_pairs={{0,2},{1,3},{2,0},{3,1},{4,6},{5,7},{6,4},{7,5}} | collective-permute-start | bytes 2359304 | tf_op jit(solution)/shard_map/ppermute | solution.py:494
  117.3 106.7 %copy-start.1 = (bf16[512,1536]{1,0:T(8,128)(2,1)S(1)}, bf16[512,1536]{1,0:T(8,128)(2,1)}, u32[]{:S(2)}) copy-start(bf16[512,1536]{1,0:T(8,128)(2,1)} %wd_ref.3) | copy-start | bytes 4718596
  117.3 106.7 %copy-start.2 = (bf16[1536,512]{1,0:T(8,128)(2,1)S(1)}, bf16[1536,512]{1,0:T(8,128)(2,1)}, u32[]{:S(2)}) copy-start(bf16[1536,512]{1,0:T(8,128)(2,1)} %wg_ref.3) | copy-start | bytes 4718596
  221.4 54.0 %collective-permute-start.17 = (f32[168,1536]{1,0:T(8,128)}, f32[168,1536]{1,0:T(8,128)}, u32[]{:S(2)}, u32[]{:S(2)}) collective-permute-start(f32[168,1536]{1,0:T(8,128)} %get-tuple-element.109), channel_id=1, source_target_pairs={{0,4},{4,0},{1,5},{5,1},{2,6},{6,2},{3,7},{7,3}} | collective-permute-start | bytes 3096584 | tf_op jit(solution)/shard_map/ppermute | solution.py:579
  221.9 60.7 %collective-permute-start.22 = (f32[168,1536]{1,0:T(8,128)}, f32[168,1536]{1,0:T(8,128)}, u32[]{:S(2)}, u32[]{:S(2)}) collective-permute-start(f32[168,1536]{1,0:T(8,128)} %get-tuple-element.113), channel_id=1, source_target_pairs={{0,4},{4,0},{1,5},{5,1},{2,6},{6,2},{3,7},{7,3}} | collective-permute-start | bytes 3096584 | tf_op jit(solution)/shard_map/ppermute | solution.py:579
  223.4 112.4 %collective-permute-start.13 = (f32[504,1536]{1,0:T(8,128)}, f32[504,1536]{1,0:T(8,128)}, u32[]{:S(2)}, u32[]{:S(2)}) collective-permute-start(f32[504,1536]{1,0:T(8,128)} %get-tuple-element.107), channel_id=1, source_target_pairs={{0,4},{4,0},{1,5},{5,1},{2,6},{6,2},{3,7},{7,3}} | collective-permute-start | bytes 9289736 | tf_op jit(solution)/shard_map/ppermute | solution.py:490
  225.4 25.7 %copy-start.43 = (f32[672,1536]{1,0:T(8,128)S(1)}, f32[672,1536]{1,0:T(8,128)}, u32[]{:S(2)}) copy-start(f32[672,1536]{1,0:T(8,128)} %get-tuple-element.91) | copy-start | bytes 12386308
  251.1 5.4 copy-start.9
  258.9 28.2 %collective-permute-start.9 = (bf16[128,1536]{1,0:T(8,128)(2,1)}, bf16[128,1536]{1,0:T(8,128)(2,1)}, u32[]{:S(2)}, u32[]{:S(2)}) collective-permute-start(bf16[128,1536]{1,0:T(8,128)(2,1)} %get-tuple-element.95), channel_id=1, source_target_pairs={{0,1},{1,0},{2,3},{3,2},{4,5},{5,4},{6,7},{7,6}} | collective-permute-start | bytes 1179656 | tf_op jit(solution)/shard_map/ppermute | solution.py:529
  260.6 4.8 copy-start.41
  260.7 211.5 %all-to-all-start = ((bf16[4,168,1536]{2,1,0:T(8,128)(2,1)}), bf16[4,168,1536]{2,1,0:T(8,128)(2,1)}, u32[]{:S(2)}, u32[]{:S(2)}) async-start(bf16[4,168,1536]{2,1,0:T(8,128)(2,1)} %bitcast.95), calls=%async_computation | async-start | bytes 4128768 | tf_op jit(solution)/shard_map/all_to_all | solution.py:519
  275.3 14.3 %collective-permute-start.10 = (bf16[128,1536]{1,0:T(8,128)(2,1)}, bf16[128,1536]{1,0:T(8,128)(2,1)S(1)}, u32[]{:S(2)}, u32[]{:S(2)}) collective-permute-start(bf16[128,1536]{1,0:T(8,128)(2,1)} %collective-permute-done.5), channel_id=1, source_target_pairs={{0,1},{1,0},{2,3},{3,2},{4,5},{5,4},{6,7},{7,6}} | collective-permute-start | bytes 1179656 | tf_op jit(solution)/shard_map/ppermute | solution.py:529
  282.6 6.0 %copy-start.16 = (bf16[512,1536]{1,0:T(8,128)(2,1)S(1)}, bf16[512,1536]{1,0:T(8,128)(2,1)}, u32[]{:S(2)}) copy-start(bf16[512,1536]{1,0:T(8,128)(2,1)} %constant_dynamic-update-slice_fusion.2) | copy-start | bytes 4718596
  282.6 7.9 %collective-permute-start.7 = (bf16[1536,256]{1,0:T(8,128)(2,1)}, bf16[1536,256]{1,0:T(8,128)(2,1)}, u32[]{:S(2)}, u32[]{:S(2)}) collective-permute-start(bf16[1536,256]{1,0:T(8,128)(2,1)} %collective-permute-done.3), channel_id=1, source_target_pairs={{0,1},{1,0},{2,3},{3,2},{4,5},{5,4},{6,7},{7,6}} | collective-permute-start | bytes 2359304 | tf_op jit(solution)/shard_map/ppermute | solution.py:528
  287.0 228.8 %copy-start.39 = (pred[192,192]{0,1:T(32,128)(4,1)}, pred[192,192]{0,1:T(32,128)(4,1)S(1)}, u32[]{:S(2)}) copy-start(pred[192,192]{0,1:T(32,128)(4,1)S(1)} %convolution_compare_fusion.2) | copy-start | bytes 110596
  287.1 211.9 %collective-permute-start.12 = (f32[504,1536]{1,0:T(8,128)}, f32[504,1536]{1,0:T(8,128)}, u32[]{:S(2)}, u32[]{:S(2)}) collective-permute-start(f32[504,1536]{1,0:T(8,128)} %get-tuple-element.103), channel_id=1, source_target_pairs={{0,4},{4,0},{1,5},{5,1},{2,6},{6,2},{3,7},{7,3}} | collective-permute-start | bytes 9289736 | tf_op jit(solution)/shard_map/ppermute | solution.py:466
  289.7 4.3 collective-permute-start.8
  289.8 4.7 copy-start.17
  290.5 6.1 %copy-start.26 = (f32[192,512]{1,0:T(8,128)}, f32[192,512]{1,0:T(8,128)S(1)}, u32[]{:S(2)}) copy-start(f32[192,512]{1,0:T(8,128)S(1)} %fusion.23) | copy-start | bytes 1179652
  292.2 175.3 %collective-permute-start.18 = (f32[504,1536]{1,0:T(8,128)S(1)}, f32[504,1536]{1,0:T(8,128)S(1)}, u32[]{:S(2)}, u32[]{:S(2)}) collective-permute-start(f32[504,1536]{1,0:T(8,128)S(1)} %copy-done.44), channel_id=1, source_target_pairs={{0,4},{4,0},{1,5},{5,1},{2,6},{6,2},{3,7},{7,3}} | collective-permute-start | bytes 9289736 | tf_op jit(solution)/shard_map/ppermute | solution.py:579
  296.6 39.2 %copy-start.15 = (f32[504,1536]{1,0:T(8,128)S(1)}, f32[504,1536]{1,0:T(8,128)}, u32[]{:S(2)}) copy-start(f32[504,1536]{1,0:T(8,128)} %get-tuple-element.108) | copy-start | bytes 9289732
  339.5 128.1 %copy-start.14 = (f32[504,1536]{1,0:T(8,128)S(1)}, f32[504,1536]{1,0:T(8,128)}, u32[]{:S(2)}) copy-start(f32[504,1536]{1,0:T(8,128)} %get-tuple-element.112) | copy-start | bytes 9289732
  342.1 201.2 %collective-permute-start.14 = (bf16[168,1536]{1,0:T(8,128)(2,1)}, bf16[168,1536]{1,0:T(8,128)(2,1)}, u32[]{:S(2)}, u32[]{:S(2)}) collective-permute-start(bf16[168,1536]{1,0:T(8,128)(2,1)} %convolution_convert_fusion.8), channel_id=1, source_target_pairs={{0,2},{1,3},{2,0},{3,1},{4,6},{5,7},{6,4},{7,5}} | collective-permute-start | bytes 1548296 | tf_op jit(solution)/shard_map/ppermute | solution.py:606
  343.5 165.3 %collective-permute-start.15 = (bf16[168,1536]{1,0:T(8,128)(2,1)}, bf16[168,1536]{1,0:T(8,128)(2,1)}, u32[]{:S(2)}, u32[]{:S(2)}) collective-permute-start(bf16[168,1536]{1,0:T(8,128)(2,1)} %convolution_convert_fusion.7), channel_id=1, source_target_pairs={{0,1},{1,0},{2,3},{3,2},{4,5},{5,4},{6,7},{7,6}} | collective-permute-start | bytes 1548296 | tf_op jit(solution)/shard_map/ppermute | solution.py:606
  467.5 15.6 %collective-permute-start.16 = (bf16[168,1536]{1,0:T(8,128)(2,1)}, bf16[168,1536]{1,0:T(8,128)(2,1)}, u32[]{:S(2)}, u32[]{:S(2)}) collective-permute-start(bf16[168,1536]{1,0:T(8,128)(2,1)} %convolution_convert_fusion.6), channel_id=1, source_target_pairs={{0,3},{1,2},{2,1},{3,0},{4,7},{5,6},{6,5},{7,4}} | collective-permute-start | bytes 1548296 | tf_op jit(solution)/shard_map/ppermute | solution.py:606
  472.2 7.3 %copy-start.48 = (pred[192,672]{1,0:T(32,128)(4,1)S(1)}, pred[192,672]{1,0:T(32,128)(4,1)}, u32[]{:S(2)}) copy-start(pred[192,672]{1,0:T(32,128)(4,1)} %convolution_compare_fusion) | copy-start | bytes 387076
  472.2 41.0 %collective-permute-start.19 = (bf16[168,1536]{1,0:T(8,128)(2,1)}, bf16[168,1536]{1,0:T(8,128)(2,1)}, u32[]{:S(2)}, u32[]{:S(2)}) collective-permute-start(bf16[168,1536]{1,0:T(8,128)(2,1)} %convolution_convert_fusion.5), channel_id=1, source_target_pairs={{0,2},{1,3},{2,0},{3,1},{4,6},{5,7},{6,4},{7,5}} | collective-permute-start | bytes 1548296 | tf_op jit(solution)/shard_map/ppermute | solution.py:606
  475.9 23.1 %all-to-all-start.1 = ((bf16[4,48,1536]{2,1,0:T(8,128)(2,1)}), bf16[4,48,1536]{2,1,0:T(8,128)(2,1)S(1)}, u32[]{:S(2)}, u32[]{:S(2)}) async-start(bf16[4,48,1536]{2,1,0:T(8,128)(2,1)} %bitcast.94), calls=%async_computation.1 | async-start | bytes 1179648 | tf_op jit(solution)/shard_map/all_to_all | solution.py:519
  483.1 28.3 %collective-permute-start.20 = (bf16[168,1536]{1,0:T(8,128)(2,1)S(1)}, bf16[168,1536]{1,0:T(8,128)(2,1)S(1)}, u32[]{:S(2)}, u32[]{:S(2)}) collective-permute-start(bf16[168,1536]{1,0:T(8,128)(2,1)S(1)} %copy-done.25), channel_id=1, source_target_pairs={{0,1},{1,0},{2,3},{3,2},{4,5},{5,4},{6,7},{7,6}} | collective-permute-start | bytes 1548296 | tf_op jit(solution)/shard_map/ppermute | solution.py:606
  499.0 56.3 %collective-permute-start.21 = (bf16[168,1536]{1,0:T(8,128)(2,1)}, bf16[168,1536]{1,0:T(8,128)(2,1)}, u32[]{:S(2)}, u32[]{:S(2)}) collective-permute-start(bf16[168,1536]{1,0:T(8,128)(2,1)} %convolution_convert_fusion.3), channel_id=1, source_target_pairs={{0,3},{1,2},{2,1},{3,0},{4,7},{5,6},{6,5},{7,4}} | collective-permute-start | bytes 1548296 | tf_op jit(solution)/shard_map/ppermute | solution.py:606
  504.2 26.0 %all-to-all-start.2 = ((bf16[4,128,1536]{2,1,0:T(8,128)(2,1)}), bf16[4,128,1536]{2,1,0:T(8,128)(2,1)}, u32[]{:S(2)}, u32[]{:S(2)}) async-start(bf16[4,128,1536]{2,1,0:T(8,128)(2,1)} %bitcast.12), calls=%async_computation.2 | async-start | bytes 3145728 | tf_op jit(solution)/shard_map/all_to_all | solution.py:519
  513.2 17.1 %copy-start.46 = (pred[192,512]{1,0:T(32,128)(4,1)S(1)}, pred[192,512]{1,0:T(32,128)(4,1)}, u32[]{:S(2)}) copy-start(pred[192,512]{1,0:T(32,128)(4,1)} %convolution_compare_fusion.1) | copy-start | bytes 294916
  532.9 34.0 %collective-permute-start.23 = (f32[192,64]{0,1:T(8,128)S(1)}, f32[192,64]{0,1:T(8,128)S(1)}, u32[]{:S(2)}, u32[]{:S(2)}) collective-permute-start(f32[192,64]{0,1:T(8,128)S(1)} %get-tuple-element.124), channel_id=1, source_target_pairs={{0,4},{4,0},{1,5},{5,1},{2,6},{6,2},{3,7},{7,3}} | collective-permute-start | bytes 147464 | tf_op jit(solution)/shard_map/ppermute | solution.py:577
  550.0 5.3 copy-start.11
  550.0 5.3 copy-start.12
  550.0 5.4 copy-start.42
  555.3 5.8 %copy-start.52 = (f32[192,512]{1,0:T(8,128)S(1)}, f32[192,512]{1,0:T(8,128)}, u32[]{:S(2)}) copy-start(f32[192,512]{1,0:T(8,128)} %copy-done.50) | copy-start | bytes 1179652
  567.0 6.1 %collective-permute-start.25 = (f32[2,192,64]{1,2,0:T(8,128)S(1)}, f32[2,192,64]{1,2,0:T(8,128)S(1)}, u32[]{:S(2)}, u32[]{:S(2)}) collective-permute-start(f32[2,192,64]{1,2,0:T(8,128)S(1)} %maximum_select_fusion.1), channel_id=1, source_target_pairs={{0,1},{1,0},{2,3},{3,2},{4,5},{5,4},{6,7},{7,6}} | collective-permute-start | bytes 294920 | tf_op jit(solution)/shard_map/ppermute | solution.py:435
  567.0 5.9 %collective-permute-start.24 = (f32[2,192,64]{1,2,0:T(8,128)S(1)}, f32[2,192,64]{1,2,0:T(8,128)S(1)}, u32[]{:S(2)}, u32[]{:S(2)}) collective-permute-start(f32[2,192,64]{1,2,0:T(8,128)S(1)} %maximum_select_fusion.1), channel_id=1, source_target_pairs={{0,2},{1,3},{2,0},{3,1},{4,6},{5,7},{6,4},{7,5}} | collective-permute-start | bytes 294920 | tf_op jit(solution)/shard_map/ppermute | solution.py:434
  573.1 1.4 collective-permute-start.26
  (35 other events, 73.6 us)
